TPU v7x, 256 devices: a whole 4x4x8 slice. The times are simulated.
256 devices in a mesh: cp: 32 (over x, y, core), tp: 8 (over z).
Axes of the slice: x: 4, y: 4, z: 8, core: 2. Of those that a mesh axis runs over, the one named last changes fastest.
Arguments:
- hidden: bfloat16 [16384, 4096], P('cp', 'tp'), may hold values from -9 to 9
- lengths: int32 [64], replicated, may hold values from 1 to 512, 16384 in all
- targets: int32 [64], replicated, may hold values from 0 to 128255
- norm_gain: float32 [4096], replicated, may hold values from 0.25 to 1.75
- lm_weight: bfloat16 [4096, 128256], P('cp', 'tp'), may hold values from -16 to 16, as said below
Outputs:
- target_logprob: float32 [64], replicated
Inputs may be any that keep to these rules, and one draw needn't show every extreme that they name: `lm_weight`: most entries are of order 3 / sqrt(4096). The lengths sum to 16384, and one prompt has exactly 512 positions.
All inputs are finite; a program needn't handle non-finite values.
Results may differ from a plain program's by a relative error of at most 0.00058.
Values may be sent and summed in bfloat16 or wider, within the bound.
No kernel may reach another device: no remote copies, remote signals or barrier semaphores. Data moves between devices by JAX's collectives and lax.ppermute only.
A program may use at most 64 MiB of HBM per device.

v0:
```python
import jax
import jax.numpy as jnp
from jax import lax
from jax.sharding import Mesh
from jax.sharding import PartitionSpec as P

CP = ("cp_0", "cp_1", "cp_2")


def sent_to_all(x, axis):
    copies = jnp.broadcast_to(x, (lax.axis_size(axis), *x.shape))
    return lax.all_to_all(copies, axis, split_axis=0, concat_axis=0, tiled=True)


def gathered_once(x, axis):
    leaves = jax.tree.leaves(x)
    sequence = sorted(range(len(leaves)), key=lambda k: -leaves[k].size)
    width = (1, *leaves[sequence[0]].shape)[-1]
    lines = [
        jnp.pad(leaves[k].reshape(-1), (0, -leaves[k].size % width)).reshape(-1, width)
        for k in sequence
    ]
    both, at, found = (sent_to_all(jnp.concatenate(lines), axis), 0, {})
    for k, line in zip(sequence, lines):
        piece = both[:, at : at + len(line)].reshape(len(both), -1)
        found[k] = piece[:, : leaves[k].size].reshape(-1, *leaves[k].shape)
        at += len(line)
    numbers = iter(range(len(leaves)))
    return jax.tree.map(lambda _: found[next(numbers)], x)


def joined_by_halves(pieces, combine):
    while len(jax.tree.leaves(pieces)[0]) > 1:
        pieces = jax.vmap(combine)(
            *(jax.tree.map(lambda part: part[side::2], pieces) for side in (0, 1))
        )
    return jax.tree.map(lambda part: part[0], pieces)


def combined_all(x, axis, combine):
    pieces = gathered_once(x, axis)
    return joined_by_halves(pieces, combine)


def split_up(x, dim, peers):
    before, after = (x.shape[:dim], x.shape[dim + 1 :])
    return jnp.moveaxis(x.reshape(*before, peers, -1, *after), dim, 0)


def sum_at_owner(x, axis, dim):
    tiles = split_up(x, dim, lax.axis_size(axis))
    arrived = lax.all_to_all(tiles, axis, split_axis=0, concat_axis=0, tiled=True)
    return arrived.astype(jnp.float32).sum(axis=0)


def padded_to(lines, peers):
    spare = -len(lines) % peers
    return jnp.pad(lines, [(0, spare)] + [(0, 0)] * (lines.ndim - 1))


def laid_out(tiles, dim):
    lengths = list(tiles.shape[1:])
    lengths[dim] *= tiles.shape[0]
    return jnp.moveaxis(tiles, 0, dim).reshape(lengths)


def gathered_copies(x, axis, dim):
    tiles = sent_to_all(x, axis)
    return laid_out(tiles, dim)


def nested_sum(x, axes):
    lines = x.reshape(-1, x.shape[-1])
    own = sum_at_owner(padded_to(lines, lax.axis_size(axes)), axes, 0)
    whole = gathered_copies(own.astype(jnp.bfloat16), axes, 0)
    return whole[: len(lines)].reshape(x.shape).astype(jnp.float32)


def sent_and_summed(x, axis, dim):
    peers = lax.axis_size(axis)
    tiles = lax.all_to_all(split_up(x, dim, peers), axis, 0, 0, tiled=True)
    return jnp.sum(tiles, axis=0)


def summed_rows(x, axes, dim):
    far, near = axes
    own = sent_and_summed(split_up(x, dim, lax.axis_size(far)), near, dim + 1)
    return jnp.sum(lax.all_to_all(own, far, 0, 0, tiled=True), axis=0)


def gather_axes(x, axes, dim):
    far, near = axes
    initial = sent_to_all(x, far)
    tiles = jnp.swapaxes(sent_to_all(initial, near), 0, 1)
    return laid_out(tiles.reshape(-1, *x.shape), dim)


def sum_by_parts(x, axes):
    lines = x.reshape(-1, x.shape[-1])
    own = summed_rows(padded_to(lines, lax.axis_size(axes[0]) * lax.axis_size(axes[1])), axes, 0)
    whole = gather_axes(own, axes, 0)
    return whole[: len(lines)].reshape(x.shape)


def combine_stats(first, second):
    top = jnp.maximum(first[0], second[0])
    total = first[1] * jnp.exp(first[0] - top) + second[1] * jnp.exp(second[0] - top)
    return (top, total, first[2] + second[2])


def local_stats(logits, target_local):
    top = jnp.max(logits, axis=1)
    total = jnp.sum(jnp.exp(logits - top[:, None]), axis=1)
    return (top, total, target_local)


def stats_group(logits, target_local):
    top, total, target_sum = combined_all(local_stats(logits, target_local), "tp", combine_stats)
    return target_sum - top - jnp.log(total)


def target_terms(logits, targets, first_column):
    columns = first_column + lax.iota(jnp.int32, logits.shape[1])
    matches = targets[:, None] == columns[None, :]
    return jnp.sum(jnp.where(matches, logits, 0.0), axis=1)


def local(hidden, lengths, targets, norm_gain, lm_weight):
    seq_index = lax.axis_index(CP)
    voc_index = lax.axis_index("tp")
    local_rows = hidden.shape[0]
    ends = jnp.cumsum(lengths) - 1
    offsets = ends - seq_index * local_rows
    selector = (offsets[:, None] == lax.iota(jnp.int32, local_rows)[None, :]).astype(jnp.bfloat16)
    picked = jnp.dot(selector, hidden, preferred_element_type=jnp.float32)
    rows_part = nested_sum(picked.astype(jnp.bfloat16), CP).astype(jnp.bfloat16)
    last_rows = gathered_copies(rows_part, "tp", 1).astype(jnp.float32)
    mean_sq = jnp.mean(last_rows * last_rows, axis=1, keepdims=True)
    normed = (last_rows * norm_gain[None, :] / jnp.sqrt(mean_sq + 1e-05)).astype(jnp.bfloat16)
    width_block = lm_weight.shape[0]
    block = lax.dynamic_slice_in_dim(normed, seq_index * width_block, width_block, 1)
    partial_logits = jnp.dot(block, lm_weight, preferred_element_type=jnp.float32)
    voc_shard = lm_weight.shape[1]
    logits = sum_by_parts(partial_logits, (("cp_0", "cp_1"), "cp_2"))
    target_local = target_terms(logits, targets, voc_index * voc_shard)
    return stats_group(logits, target_local)


def solution(mesh):
    split = Mesh(mesh.devices.reshape(4, 4, 2, mesh.shape["tp"]), ("cp_0", "cp_1", "cp_2", "tp"))
    return jax.shard_map(
        local,
        mesh=split,
        in_specs=(P(CP, "tp"), P(), P(), P(), P(CP, "tp")),
        out_specs=P(),
        check_vma=False,
    )
```

profile of v0, /device:TPU:1, one launch (start us, length us, event | category | flops | bytes accessed | tf_op | source)
XLA Modules:
  0.0 175.7 jit_solution(15994535645717592323)
XLA Ops:
  0.0 0.0 copy-start
  0.0 0.8 copy.28
  0.8 0.1 reduce-window.8
  0.9 0.1 subtract_reduce_fusion
  1.0 0.0 copy-done
  1.1 0.2 convolution_convert_fusion
  1.3 15.7 %all_to_all.40 = bf16[32,2,512]{2,1,0:T(2,128)(2,1)S(1)} all-to-all(bf16[32,2,512]{2,1,0:T(2,128)(2,1)S(1)} %reshape.95), channel_id=1, replica_groups=mesh['cp_0'=4,'cp_1'=4,'cp_2'=2,'tp'=8] {'cp_0','cp_1','cp_2'}, dimensions={0} | all-to-all | bytes 131072 | tf_op jit(solution)/shard_map/all_to_all | solution.py:52
  17.1 0.1 reduce_sum.57
  17.2 10.9 %all_to_all.41 = bf16[32,2,512]{2,1,0:T(2,128)(2,1)S(1)} all-to-all(bf16[32,2,512]{2,1,0:T(2,128)(2,1)S(1)} %broadcast_in_dim.26), channel_id=1, replica_groups=mesh['cp_0'=4,'cp_1'=4,'cp_2'=2,'tp'=8] {'cp_0','cp_1','cp_2'}, dimensions={0} | all-to-all | bytes 131072 | tf_op jit(solution)/shard_map/all_to_all | solution.py:12
  28.1 0.8 broadcast_in_dim.27
  28.9 8.2 %all-to-all-start.2 = ((bf16[8,64,512]{2,1,0:T(8,128)(2,1)}), bf16[8,64,512]{2,1,0:T(8,128)(2,1)S(1)}, u32[]{:S(2)}, u32[]{:S(2)}) async-start(bf16[8,64,512]{2,1,0:T(8,128)(2,1)} %broadcast_in_dim.27), calls=%async_computation.2 | async-start | bytes 1048576 | tf_op jit(solution)/shard_map/all_to_all | solution.py:12
  37.1 0.8 dynamic-slice
  37.9 17.2 %all-to-all-done.2 = bf16[8,64,512]{2,1,0:T(8,128)(2,1)S(1)} async-done(((bf16[8,64,512]{2,1,0:T(8,128)(2,1)}), bf16[8,64,512]{2,1,0:T(8,128)(2,1)S(1)}, u32[]{:S(2)}, u32[]{:S(2)}) %all-to-all-start.2) | async-done | bytes 524320 | tf_op jit(solution)/shard_map/all_to_all | solution.py:12
  55.1 0.0 copy-start.2
  55.1 0.1 convert_bitcast_fusion
  55.2 0.1 copy.42
  55.3 0.2 fusion.3
  55.5 1.7 copy-done.2
  57.3 3.5 %fusion.7 = f32[64,16032]{1,0:T(8,128)} fusion(bf16[128,16032]{0,1:T(8,128)(2,1)S(1)} %copy-done.2, f32[64,4096]{1,0:T(8,128)S(1)} %bitcast.30, s32[]{:T(128)S(6)} %select_n.8, f32[64]{0:T(128)S(1)} %add_sqrt_fusion, f32[128]{0:T(128)S(1)} %dynamic-slice), kind=kOutput, calls=%fused_computation.18 | convolution fusion | flops 262692864 | bytes 8242180 | tf_op jit(solution)/shard_map/dot_general | solution.py:142
  60.8 5.7 %reshape_reshape.4 = f32[16,2,2,16032]{3,2,1,0:T(2,128)} reshape(f32[64,16032]{1,0:T(8,128)} %fusion.7) | data formatting | bytes 8208384 | tf_op jit(solution)/shard_map/reshape;reshape | solution.py:47
  66.5 2.5 %copy.44 = f32[16,2,2,16032]{3,2,0,1:T(2,128)S(1)} copy(f32[16,2,2,16032]{3,2,1,0:T(2,128)} %reshape_reshape.4) | data formatting | bytes 8208384 | tf_op jit(solution)/shard_map/reshape;reshape | solution.py:47
  69.0 8.2 %all_to_all.42 = f32[2,16,2,16032]{3,2,1,0:T(2,128)} all-to-all(f32[2,16,2,16032]{3,2,1,0:T(2,128)S(1)} %bitcast.29), channel_id=1, replica_groups=mesh['cp_0'=4,'cp_1'=4,'cp_2'=2,'tp'=8] {'cp_2'}, dimensions={0} | all-to-all | bytes 8208384 | tf_op jit(solution)/shard_map/all_to_all | solution.py:81
  77.2 5.4 %reduce_sum.59 = f32[16,2,16032]{2,1,0:T(2,128)S(1)} reduce(f32[2,16,2,16032]{3,2,1,0:T(2,128)} %all_to_all.42, f32[]{:T(128)} %constant.41.clone.1), dimensions={0}, to_apply=%region_3.4 | reduce | flops 513024 | bytes 6156292 | tf_op jit(solution)/shard_map/reduce_sum | solution.py:82
  82.6 30.1 %all_to_all.43 = f32[16,2,16032]{2,1,0:T(2,128)} all-to-all(f32[16,2,16032]{2,1,0:T(2,128)S(1)} %reduce_sum.59), channel_id=1, replica_groups=mesh['cp_0'=4,'cp_1'=4,'cp_2'=2,'tp'=8] {'cp_0','cp_1'}, dimensions={0} | all-to-all | bytes 4104192 | tf_op jit(solution)/shard_map/all_to_all | solution.py:88
  112.6 0.0 copy-start.3
  112.6 2.2 %reduce_sum.60 = f32[2,16032]{1,0:T(2,128)S(1)} reduce(f32[16,2,16032]{2,1,0:T(2,128)} %all_to_all.43, f32[]{:T(128)} %constant.41.clone.1), dimensions={0}, to_apply=%region_4.5 | reduce | flops 480960 | bytes 2180356 | tf_op jit(solution)/shard_map/reduce_sum | solution.py:88
  114.9 1.9 %broadcast_in_dim.28 = f32[16,2,16032]{2,1,0:T(2,128)} broadcast(f32[2,16032]{1,0:T(2,128)S(1)} %reduce_sum.60), dimensions={1,2} | broadcast | bytes 2180352 | tf_op jit(solution)/shard_map/broadcast_in_dim | solution.py:11
  116.7 4.1 %all-to-all-start.5 = ((f32[16,2,16032]{2,1,0:T(2,128)}), f32[16,2,16032]{2,1,0:T(2,128)S(1)}, u32[]{:S(2)}, u32[]{:S(2)}) async-start(f32[16,2,16032]{2,1,0:T(2,128)} %broadcast_in_dim.28), calls=%async_computation.5 | async-start | bytes 4128768 | tf_op jit(solution)/shard_map/all_to_all | solution.py:12
  120.9 0.0 copy-done.3
  120.9 0.1 eq.32
  121.0 0.1 copy.35
  121.1 25.2 %all-to-all-done.5 = f32[16,2,16032]{2,1,0:T(2,128)S(1)} async-done(((f32[16,2,16032]{2,1,0:T(2,128)}), f32[16,2,16032]{2,1,0:T(2,128)S(1)}, u32[]{:S(2)}, u32[]{:S(2)}) %all-to-all-start.5) | async-done | bytes 2052128 | tf_op jit(solution)/shard_map/all_to_all | solution.py:12
  146.3 0.1 copy.32
  146.4 0.3 broadcast_in_dim.29
  146.7 11.6 %all_to_all.44 = f32[2,16,2,16032]{3,1,2,0:T(8,128)S(1)} all-to-all(f32[2,16,2,16032]{3,1,2,0:T(8,128)S(1)} %broadcast_in_dim.29), channel_id=1, replica_groups=mesh['cp_0'=4,'cp_1'=4,'cp_2'=2,'tp'=8] {'cp_2'}, dimensions={0} | all-to-all | bytes 8208384 | tf_op jit(solution)/shard_map/all_to_all | solution.py:12
  158.3 0.0 copy-start.1
  158.3 1.9 %copy-done.1 = f32[2,16,2,16032]{3,1,2,0:T(8,128)} copy-done((f32[2,16,2,16032]{3,1,2,0:T(8,128)}, f32[2,16,2,16032]{3,1,2,0:T(8,128)S(1)}, u32[]{:S(2)}) %copy-start.1) | copy-done | bytes 4104216
  160.2 0.3 bitcast_reduce_fusion
  160.6 0.1 copy.33
  160.7 3.4 %fusion.1 = (f32[16,2,2]{0,2,1:T(2,128)S(1)}, f32[16,2,2]{0,2,1:T(2,128)S(1)}) fusion(f32[2,16,2,16032]{3,1,2,0:T(8,128)} %copy-done.1, f32[16,2,2]{0,2,1:T(2,128)S(1)} %bitcast_reduce_fusion, s32[16032]{0:T(1024)S(1)} %iota_add_fusion, s32[16,2,2]{0,2,1:T(2,128)S(1)} %copy.35), kind=kLoop, calls=%fused_computation.4 | loop fusion | flops 5130112 | bytes 4169344 | tf_op jit(solution)/shard_map/reduce_sum | solution.py:113
  164.0 0.1 copy.34
  164.1 0.1 reshape.98
  164.2 0.1 copy.36
  164.3 0.1 reshape.99
  164.4 0.1 reshape.97
  164.6 0.1 reshape.105
  164.7 8.9 %all_to_all.45 = f32[8,1,192]{2,1,0:T(1,128)S(1)} all-to-all(f32[8,1,192]{2,1,0:T(1,128)S(1)} %reshape.105), channel_id=1, replica_groups=mesh['cp_0'=4,'cp_1'=4,'cp_2'=2,'tp'=8] {'tp'}, dimensions={0} | all-to-all | bytes 12288 | tf_op jit(solution)/shard_map/all_to_all | solution.py:12
  173.6 0.5 broadcast.44
  174.1 0.7 reduce.8
  174.8 0.1 reshape.106
  175.2 0.5 subtract_bitcast_fusion
  (24 shorter events, 0.5 us)
Async XLA Ops:
  0.0 1.1 copy-start
  28.9 26.1 %all-to-all-start.2 = ((bf16[8,64,512]{2,1,0:T(8,128)(2,1)}), bf16[8,64,512]{2,1,0:T(8,128)(2,1)S(1)}, u32[]{:S(2)}, u32[]{:S(2)}) async-start(bf16[8,64,512]{2,1,0:T(8,128)(2,1)} %broadcast_in_dim.27), calls=%async_computation.2 | async-start | bytes 1048576 | tf_op jit(solution)/shard_map/all_to_all | solution.py:12
  55.1 2.2 %copy-start.2 = (bf16[128,16032]{0,1:T(8,128)(2,1)S(1)}, bf16[128,16032]{0,1:T(8,128)(2,1)}, u32[]{:S(2)}) copy-start(bf16[128,16032]{0,1:T(8,128)(2,1)} %param.9) | copy-start | bytes 12312580
  112.6 8.2 %copy-start.3 = (s32[64]{0:T(128)S(1)}, s32[64]{0:T(128)}, u32[]{:S(2)}) copy-start(s32[64]{0:T(128)} %param.7) | copy-start | bytes 772
  116.7 29.6 %all-to-all-start.5 = ((f32[16,2,16032]{2,1,0:T(2,128)}), f32[16,2,16032]{2,1,0:T(2,128)S(1)}, u32[]{:S(2)}, u32[]{:S(2)}) async-start(f32[16,2,16032]{2,1,0:T(2,128)} %broadcast_in_dim.28), calls=%async_computation.5 | async-start | bytes 4128768 | tf_op jit(solution)/shard_map/all_to_all | solution.py:12
  158.3 1.9 %copy-start.1 = (f32[2,16,2,16032]{3,1,2,0:T(8,128)}, f32[2,16,2,16032]{3,1,2,0:T(8,128)S(1)}, u32[]{:S(2)}) copy-start(f32[2,16,2,16032]{3,1,2,0:T(8,128)S(1)} %all_to_all.44) | copy-start | bytes 12312580
where the time goes:
time: 176 us
  blocking collectives  85.4 us (49%)
  waiting for transfers between devices  42.4 us (24%)
  local copies, waits for them, and re-layouts  18.5 us (11%)
  other arithmetic  13.2 us (8%)
  starting transfers between devices  12.3 us (7%)
  matrix products  3.76 us (2%)
    all_to_all x2, waiting for transfers between devices, sent_to_all(): return lax.all_to_all(copies, axis, split_axis=0, concat_axis=0, tiled=True)  42.4 us
    all_to_all x3, blocking collectives, sent_to_all(): return lax.all_to_all(copies, axis, split_axis=0, concat_axis=0, tiled=True)  31.4 us
    all_to_all x1, blocking collectives, summed_rows(): return jnp.sum(lax.all_to_all(own, far, 0, 0, tiled=True), axis=0)  30.1 us
    all_to_all x1, blocking collectives, sum_at_owner(): lax.all_to_all(tiles, axis, split_axis=0, concat_axis=0, tiled=True)  15.7 us
    all_to_all x2, starting transfers between devices, sent_to_all(): return lax.all_to_all(copies, axis, split_axis=0, concat_axis=0, tiled=True)  12.3 us
    all_to_all x1, blocking collectives, sent_and_summed(): tiles = lax.all_to_all(split_up(x, dim, peers), axis, 0, 0, tiled=True)  8.23 us
    another operation x2, local copies, waits for them, and re-layouts, split_up(): return jnp.moveaxis(x.reshape(*before, peers, -1, *after), dim, 0)  8.17 us
    reduce_sum x1, other arithmetic, sent_and_summed(): return jnp.sum(tiles, axis=0)  5.37 us
  transfers between devices with their start and end apart: 2, of which 2 were waited for; matrix products, arithmetic and copies ran while one was open for 1% of the time, Pallas kernels for 0%

commit v1 on v0

v1 whole, which is shorter than its diff:
```python
import functools

import jax
import jax.numpy as jnp
from jax import lax
from jax.experimental import pallas as pl
from jax.experimental.pallas import tpu as pltpu
from jax.sharding import Mesh
from jax.sharding import PartitionSpec as P

CHIPS = ("x", "y")
CP = ("x", "y", "c")
ALL = ("x", "y", "c", "z")
SLOTS = 8
BLOCK = 512
NEG = -1e30

VMEM = pl.BlockSpec(memory_space=pltpu.VMEM)
SMEM = pl.BlockSpec(memory_space=pltpu.SMEM)
ANY = pl.BlockSpec(memory_space=pl.ANY)


def iota(shape, dim):
    return lax.broadcasted_iota(jnp.int32, shape, dim).astype(jnp.float32)


def total(x, axis):
    return jnp.sum(x, axis=axis, keepdims=True)


def place():
    return (lax.axis_index("x") * lax.axis_size("y") + lax.axis_index("y")) * lax.axis_size(
        "c"
    ) + lax.axis_index("c")


def as_column(row):
    n = row.shape[1]
    return total(jnp.where(iota((n, n), 0) == iota((n, n), 1), row, 0.0), 1)


def ends_of(lengths_ref):
    row = lengths_ref[...].astype(jnp.float32)
    n = row.shape[1]
    down, across = iota((n, n), 0), iota((n, n), 1)
    column = total(jnp.where(across <= down, row, 0.0), 1) - 1.0
    return total(jnp.where(down <= across, as_column(row), 0.0), 0) - 1.0, column


def pick_kernel(lengths_ref, first_ref, hidden_ref, out_ref, most_ref):
    n = lengths_ref.shape[1]
    rows = hidden_ref.shape[0]
    ends, _ = ends_of(lengths_ref)
    base = (place() * rows).astype(jnp.float32)
    owned = (ends >= base) & (ends < base + rows)
    before = total(jnp.where(ends < base, 1.0, 0.0), 1)
    slot = iota((1, n), 1) - before - first_ref[0, 0].astype(jnp.float32)
    wanted = owned & (slot == iota((SLOTS, n), 0))
    at = total(jnp.where(wanted, ends - base + 1.0, 0.0), 1) - 1.0
    selector = (at == iota((SLOTS, rows), 1)).astype(jnp.bfloat16)
    picked = jnp.dot(selector, hidden_ref[...], preferred_element_type=jnp.float32)
    picked = picked.astype(jnp.bfloat16)
    for peer in range(out_ref.shape[0]):
        out_ref[peer] = picked
    owners = iota((32, n), 0)
    counts = total(jnp.where(jnp.floor(ends / rows) == owners, 1.0, 0.0), 1)
    most_ref[0, 0] = jnp.max(counts).astype(jnp.int32)


def norm_kernel(rows_ref, gain_ref, out_ref):
    parts, _, width = rows_ref.shape
    squares = jnp.zeros((SLOTS, 1), jnp.float32)
    for part in range(parts):
        values = rows_ref[part].astype(jnp.float32)
        squares = squares + total(values * values, 1)
    scale = jnp.sqrt(squares / (parts * width) + 1e-05)
    chips, cores, _, block = out_ref.shape
    for chip in range(chips):
        part, at = divmod(chip * block, width)
        values = rows_ref[part, :, at : at + block].astype(jnp.float32)
        gain = gain_ref[:, chip * block : (chip + 1) * block]
        normed = (values * gain / scale).astype(jnp.bfloat16)
        for core in range(cores):
            out_ref[chip, core] = normed


def rows_in_order(lengths_ref, first_ref, found_ref):
    n = lengths_ref.shape[1]
    places = found_ref.shape[0]
    rows = 512
    ends_row, ends = ends_of(lengths_ref)
    owner = jnp.floor(ends / rows)
    before = total(jnp.where(ends_row < owner * rows, 1.0, 0.0), 1)
    slot = iota((n, 1), 0) - before - first_ref[0, 0].astype(jnp.float32)
    inside = (slot >= 0.0) & (slot < SLOTS)
    at = jnp.where(inside, owner * SLOTS + slot, -1.0)
    selector = (at == iota((n, places), 1)).astype(jnp.bfloat16)
    return jnp.dot(selector, found_ref[...], preferred_element_type=jnp.float32)


def order_kernel(lengths_ref, first_ref, found_ref, more_ref, out_ref):
    rows = rows_in_order(lengths_ref, first_ref, found_ref)
    out_ref[...] = more_ref[...] + rows.astype(jnp.bfloat16)


def split_kernel(weight_ref, keep_ref, send_ref, sems):
    core = lax.axis_index("c")
    half = keep_ref.shape[0]
    spare = weight_ref.shape[0] - half
    copies = [
        pltpu.make_async_copy(
            weight_ref.at[pl.ds(pl.multiple_of(which * spare, 16), half)], ref, sems.at[k]
        )
        for k, (which, ref) in enumerate(((1 - core, send_ref), (core, keep_ref)))
    ]
    for copy in copies:
        copy.start()
    for copy in copies:
        copy.wait()


def head_kernel(lengths_ref, first_ref, found_ref, more_ref, keep_ref, other_ref, out_ref):
    rows = rows_in_order(lengths_ref, first_ref, found_ref).astype(jnp.bfloat16) + more_ref[...]
    width = keep_ref.shape[1]
    low, high = rows[:, :width], rows[:, width:]
    first = lax.axis_index("c") == 0
    left = jnp.concatenate([jnp.where(first, low, high), jnp.where(first, high, low)], axis=1)
    for block in range(out_ref.shape[0]):
        span = slice(block * BLOCK, (block + 1) * BLOCK)
        weight = jnp.concatenate([keep_ref[span, :], other_ref[span, :]], axis=1)
        part = lax.dot_general(
            left, weight, (((1,), (1,)), ((), ())), preferred_element_type=jnp.float32
        )
        out_ref[block] = part.astype(out_ref.dtype)


def stats_kernel(spare, vocab, logits_ref, targets_ref, out_ref):
    logits = logits_ref[...]
    n, block = logits.shape
    core = lax.axis_index("c")
    chip = lax.axis_index("x") * lax.axis_size("y") + lax.axis_index("y")
    start = (core * spare + chip * block).astype(jnp.float32)
    column = iota((1, block), 1) + start
    half = vocab - spare
    valid = column >= (core * half).astype(jnp.float32)
    shift = (lax.axis_index("z") * vocab).astype(jnp.float32)
    wanted = as_column(targets_ref[...].astype(jnp.float32)) - shift
    found = total(jnp.where(valid & (column == wanted), logits, 0.0), 1)
    logits = jnp.where(valid, logits, NEG)
    top = jnp.max(logits, axis=1, keepdims=True)
    both = top + jnp.log(total(jnp.exp(logits - top), 1))
    down, across = iota((n, 2 * n), 0), iota((n, 2 * n), 1)
    line = jnp.where(across == down, both, 0.0) + jnp.where(across == down + n, found, 0.0)
    out_ref[...] = jnp.broadcast_to(total(line, 0)[None], out_ref.shape)


def join_kernel(found_ref, out_ref):
    n = out_ref.shape[1]
    lines = found_ref[:, 0, :]
    top = jnp.max(lines, axis=0, keepdims=True)
    both = top + jnp.log(total(jnp.exp(lines - top), 0))
    chosen = total(lines, 0)
    out_ref[...] = chosen[:, n:] - both[:, :n]


def shape(dims, dtype):
    return jax.ShapeDtypeStruct(dims, dtype)


def exchange(x, axes):
    return lax.all_to_all(x, axes, split_axis=0, concat_axis=0, tiled=True)


def gathered(lengths, first, hidden, gain):
    peers = lax.axis_size("z")
    chips, cores = lax.axis_size(CHIPS), lax.axis_size("c")
    rows, most = pl.pallas_call(
        pick_kernel,
        out_shape=(shape((peers, SLOTS, hidden.shape[1]), hidden.dtype), shape((1, 1), jnp.int32)),
        in_specs=[VMEM, SMEM, VMEM],
        out_specs=(VMEM, SMEM),
        name="pick",
    )(lengths, first, hidden)
    rows = exchange(rows, "z")
    width = gain.shape[1] // chips
    normed = pl.pallas_call(
        norm_kernel,
        out_shape=shape((chips, cores, SLOTS, width), jnp.bfloat16),
        in_specs=[VMEM, VMEM],
        out_specs=VMEM,
        name="norm",
    )(rows, gain)
    return exchange(normed.reshape(chips * cores * SLOTS, width), CP), most


def local(hidden, lengths, targets, norm_gain, lm_weight):
    n = lengths.shape[0]
    lengths, targets, gain = lengths[None], targets[None], norm_gain[None]
    weight = lm_weight.T
    vocab, depth = weight.shape
    chips = lax.axis_size(CHIPS)
    half = chips * BLOCK
    start = jnp.zeros((1, 1), jnp.int32)
    found, most = gathered(lengths, start, hidden, gain)

    def again(state):
        first, more = state
        found, _ = gathered(lengths, first, hidden, gain)
        more = pl.pallas_call(
            order_kernel,
            out_shape=shape(more.shape, more.dtype),
            in_specs=[VMEM, SMEM, VMEM, VMEM],
            out_specs=VMEM,
            name="order",
        )(lengths, first, found, more)
        return first + SLOTS, more

    _, more = lax.while_loop(
        lambda state: state[0][0, 0] < most[0, 0],
        again,
        (start + SLOTS, jnp.zeros((n, found.shape[1]), jnp.bfloat16)),
    )
    keep, send = pl.pallas_call(
        split_kernel,
        out_shape=(shape((half, depth), weight.dtype),) * 2,
        in_specs=[ANY],
        out_specs=(VMEM, VMEM),
        scratch_shapes=[pltpu.SemaphoreType.DMA((2,))],
        name="split",
    )(weight)
    other = lax.ppermute(send, "c", [(0, 1), (1, 0)])
    parts = pl.pallas_call(
        head_kernel,
        out_shape=shape((chips, n, BLOCK), jnp.float32),
        in_specs=[VMEM, SMEM, VMEM, VMEM, VMEM, VMEM],
        out_specs=VMEM,
        name="head",
    )(lengths, start, found, more, keep, other)
    logits = jnp.sum(exchange(parts.astype(jnp.float16), CHIPS).astype(jnp.float32), axis=0)
    line = pl.pallas_call(
        functools.partial(stats_kernel, vocab - half, vocab),
        out_shape=shape((lax.axis_size(ALL), 1, 2 * n), jnp.float32),
        in_specs=[VMEM, VMEM],
        out_specs=VMEM,
        name="stats",
    )(logits, targets)
    lines = exchange(line, ALL)
    out = pl.pallas_call(
        join_kernel,
        out_shape=shape((1, n), jnp.float32),
        in_specs=[VMEM],
        out_specs=VMEM,
        name="join",
    )(lines)
    return out[0]


def solution(mesh):
    split = Mesh(mesh.devices.reshape(4, 4, 2, mesh.shape["tp"]), ALL)
    return jax.shard_map(
        local,
        mesh=split,
        in_specs=(P(CP, "z"), P(), P(), P(), P(CP, "z")),
        out_specs=P(),
        check_vma=False,
    )
```

time: 176 us -> 94.7 us (0.54)
  waiting for transfers between devices: 42.4 us -> 7.14 us
  blocking collectives: 85.4 us -> 56.2 us
  local copies, waits for them, and re-layouts: 18.5 us -> 2.13 us
  Pallas kernels: 0 us -> 15.7 us
  other arithmetic: 13.2 us -> 2.63 us
  matrix products: 3.76 us -> 0 us
  starting transfers between devices: 12.3 us -> 9.78 us
    all_to_all x2 -> x1, waiting for transfers between devices: 42.4 us -> 7.14 us  [exchange(): return lax.all_to_all(x, axes, split_axis=0, concat_axis=0, tiled=True)]
    all_to_all x6 -> x3, blocking collectives: 85.4 us -> 56.2 us  [exchange(): return lax.all_to_all(x, axes, split_axis=0, concat_axis=0, tiled=True)]
    pallas_call x0 -> x6, Pallas kernels: none -> 15.7 us  [the longest x1 5.25 us: local(): pl.pallas_call(head_kernel, out_shape=shape((chips, n, BLOCK), jnp.float3...]
    reduce_sum x5 -> x1, other arithmetic: 11.2 us -> 0.79 us  [local(): jnp.sum(exchange(parts.astype(jnp.float16), CHIPS).astype(jnp.float32), a...]
    another operation x3 -> x0, local copies, waits for them, and re-layouts: 8.98 us -> none  [the longest x2 8.17 us: split_up(): return jnp.moveaxis(x.reshape(*before, peers, -1, *after), dim, 0)]
    all_to_all x2 -> x1, starting transfers between devices: 12.3 us -> 6.5 us  [exchange(): return lax.all_to_all(x, axes, split_axis=0, concat_axis=0, tiled=True)]
    dot_general x2 -> x0, matrix products: 3.76 us -> none  [the longest x1 3.53 us: local(): jnp.dot(block, lm_weight, preferred_element_type=jnp.float32)]
    ppermute x0 -> x1, starting transfers between devices: none -> 3.27 us  [local(): other = lax.ppermute(send, 'c', [(0, 1), (1, 0)])]
  transfers between devices with their start and end apart: 2 -> 2, of which waited for: 2 -> 1; matrix products, arithmetic and copies ran while one was open for 1% -> 0% of each run, Pallas kernels for 0% -> 3%
where the time goes in v1:
time: 94.7 us; the launch traced here: 94.3 us
  blocking collectives  56.2 us (59%)
  Pallas kernels  15.7 us (17%)
  starting transfers between devices  9.78 us (10%)
  waiting for transfers between devices  7.14 us (8%)
  other arithmetic  2.63 us (3%)
  local copies, waits for them, and re-layouts  2.13 us (2%)
    all_to_all x3, blocking collectives, exchange(): return lax.all_to_all(x, axes, split_axis=0, concat_axis=0, tiled=True)  56.2 us
    all_to_all x1, waiting for transfers between devices, exchange(): return lax.all_to_all(x, axes, split_axis=0, concat_axis=0, tiled=True)  7.14 us
    all_to_all x1, starting transfers between devices, exchange(): return lax.all_to_all(x, axes, split_axis=0, concat_axis=0, tiled=True)  6.5 us
    pallas_call x1, Pallas kernels, local(): pl.pallas_call(head_kernel, out_shape=shape((chips, n, BLOCK), jnp.float3...  5.25 us
    pallas_call x1, Pallas kernels, local(): pl.pallas_call(split_kernel, out_shape=(shape((half, depth), weight.dtype...  4.25 us
    ppermute x1, starting transfers between devices, local(): other = lax.ppermute(send, 'c', [(0, 1), (1, 0)])  3.27 us
    unnamed x12, local copies, waits for them, and re-layouts  2.12 us
  transfers between devices with their start and end apart: 2, of which 1 were waited for; matrix products, arithmetic and copies ran while one was open for 0% of the time, Pallas kernels for 3%

profile of v1, /device:TPU:1, one launch (start us, length us, event | category | flops | bytes accessed | tf_op | source)
XLA Modules:
  0.0 94.3 jit_solution(11703652849606643563)
XLA Ops:
  0.0 0.0 copy-start
  0.0 0.0 copy-start.6
  0.0 0.0 copy-start.3
  0.0 4.3 %split.1 = (bf16[8192,128]{1,0:T(8,128)(2,1)}, bf16[8192,128]{1,0:T(8,128)(2,1)}) custom-call(bf16[16032,128]{1,0:T(8,128)(2,1)} %bitcast.15), custom_call_target="tpu_custom_call" | custom-call | tf_op jit(solution)/shard_map/split/pallas_call | solution.py:223
  4.3 3.3 %collective-permute-start = (bf16[8192,128]{1,0:T(8,128)(2,1)}, bf16[8192,128]{1,0:T(8,128)(2,1)S(1)}, u32[]{:S(2)}, u32[]{:S(2)}) collective-permute-start(bf16[8192,128]{1,0:T(8,128)(2,1)} %get-tuple-element.47), channel_id=1, source_target_pairs={{0,8},{8,0},{1,9},{9,1},{2,10},{10,2},{3,11},{11,3},{4,12},{12,4},... | collective-permute-start | bytes 6291464 | tf_op jit(solution)/shard_map/ppermute | solution.py:231
  7.5 0.0 copy-done
  7.5 0.0 copy-done.6
  7.5 1.0 %pick.2 = (bf16[8,8,512]{2,1,0:T(8,128)(2,1)}, s32[1,1]{1,0:T(1,128)}) custom-call(s32[1,64]{1,0:T(1,128)S(1)} %bitcast.20, s32[1,1]{1,0:T(1,128)} %constant.0.clone.1.first_ref, bf16[512,512]{1,0:T(8,128)(2,1)S(1)} %copy-done), custom_call_target="tpu_custom_call" | custom-call | tf_op jit(solution)/shard_map/pick/pallas_call | solution.py:177
  8.6 6.5 %all-to-all-start.2 = ((bf16[8,8,512]{2,1,0:T(8,128)(2,1)}), bf16[8,8,512]{2,1,0:T(8,128)(2,1)S(1)}, u32[]{:S(2)}, u32[]{:S(2)}) async-start(bf16[8,8,512]{2,1,0:T(8,128)(2,1)} %get-tuple-element.43), calls=%async_computation.2 | async-start | bytes 131072 | tf_op jit(solution)/shard_map/all_to_all | solution.py:171
  15.1 7.1 %all-to-all-done.2.rows_ref = bf16[8,8,512]{2,1,0:T(8,128)(2,1)S(1)} async-done(((bf16[8,8,512]{2,1,0:T(8,128)(2,1)}), bf16[8,8,512]{2,1,0:T(8,128)(2,1)S(1)}, u32[]{:S(2)}, u32[]{:S(2)}) %all-to-all-start.2) | async-done | bytes 65568 | tf_op jit(solution)/shard_map/all_to_all | solution.py:171
  22.2 0.0 copy-start.5
  22.2 0.6 copy-done.5
  22.8 0.0 copy-done.3
  22.9 1.6 %norm.2 = bf16[16,2,8,256]{3,2,1,0:T(8,128)(2,1)} custom-call(bf16[8,8,512]{2,1,0:T(8,128)(2,1)} %copy-done.5, f32[1,4096]{1,0:T(1,128)S(1)} %bitcast.16), custom_call_target="tpu_custom_call" | custom-call | tf_op jit(solution)/shard_map/norm/pallas_call | solution.py:186
  24.5 0.0 copy-start.4
  24.5 0.7 while.10
  25.2 0.2 copy-done.4
  25.4 16.2 %all_to_all.40 = bf16[32,8,256]{2,1,0:T(8,128)(2,1)} all-to-all(bf16[32,8,256]{2,1,0:T(8,128)(2,1)S(1)} %bitcast.19), channel_id=1, replica_groups=mesh['x'=4,'y'=4,'c'=2,'z'=8] {'x','y','c'}, dimensions={0} | all-to-all | bytes 262144 | tf_op jit(solution)/shard_map/all_to_all | solution.py:171
  41.6 0.0 collective-permute-done.other_ref
  41.6 0.0 copy-start.2
  41.6 1.3 %copy-done.2 = bf16[8192,128]{1,0:T(8,128)(2,1)} copy-done((bf16[8192,128]{1,0:T(8,128)(2,1)}, bf16[8192,128]{1,0:T(8,128)(2,1)S(1)}, u32[]{:S(2)}) %copy-start.2) | copy-done | bytes 2097176
  42.9 5.3 %head.1 = f32[16,64,512]{2,1,0:T(8,128)} custom-call(s32[1,64]{1,0:T(1,128)S(1)} %get-tuple-element.119, s32[1,1]{1,0:T(1,128)} %constant.0.clone.1.first_ref, bf16[256,256]{1,0:T(8,128)(2,1)} %bitcast.18, bf16[64,256]{1,0:T(8,128)(2,1)S(1)} %get-tuple-element.45.more_ref, bf16[8192,128]{1,0:T(8,128)(2,1)} %get-tuple-element.46.keep_ref, ...), custom_call_target="tpu_custom_call" | custom-call | tf_op jit(solution)/shard_map/head/pallas_call | solution.py:232
  48.1 1.8 %convert_element_type.6 = f16[16,64,512]{2,1,0:T(8,128)(2,1)S(1)} convert(f32[16,64,512]{2,1,0:T(8,128)} %head.1) | non-fusion elementwise | flops 524288 | bytes 3145728 | tf_op jit(solution)/shard_map/convert_element_type | solution.py:239
  50.0 18.6 %all_to_all.41 = f16[16,64,512]{2,1,0:T(8,128)(2,1)S(1)} all-to-all(f16[16,64,512]{2,1,0:T(8,128)(2,1)S(1)} %convert_element_type.6), channel_id=1, replica_groups=mesh['x'=4,'y'=4,'c'=2,'z'=8] {'x','y'}, dimensions={0} | all-to-all | bytes 2097152 | tf_op jit(solution)/shard_map/all_to_all | solution.py:171
  68.6 0.8 convert_reduce_fusion.logits_ref
  69.4 1.8 %stats.1 = f32[256,1,128]{2,1,0:T(1,128)} custom-call(f32[64,512]{1,0:T(8,128)} %convert_reduce_fusion.logits_ref, s32[1,64]{1,0:T(1,128)} %bitcast.22), custom_call_target="tpu_custom_call" | custom-call | tf_op jit(solution)/shard_map/stats/pallas_call | solution.py:240
  71.2 21.4 %all_to_all.42.found_ref = f32[256,1,128]{2,1,0:T(1,128)} all-to-all(f32[256,1,128]{2,1,0:T(1,128)} %stats.1), channel_id=1, replica_groups=mesh['x'=4,'y'=4,'c'=2,'z'=8] {'x','y','c','z'}, dimensions={0} | all-to-all | bytes 262144 | tf_op jit(solution)/shard_map/all_to_all | solution.py:171
  92.6 1.7 %join.1 = f32[1,64]{1,0:T(1,128)} custom-call(f32[256,1,128]{2,1,0:T(1,128)} %all_to_all.42.found_ref), custom_call_target="tpu_custom_call" | custom-call | tf_op jit(solution)/shard_map/join/pallas_call | solution.py:248
  (1 shorter events, 0.0 us)
Async XLA Ops:
  0.0 7.5 %copy-start = (bf16[512,512]{1,0:T(8,128)(2,1)S(1)}, bf16[512,512]{1,0:T(8,128)(2,1)}, u32[]{:S(2)}) copy-start(bf16[512,512]{1,0:T(8,128)(2,1)} %hidden_ref.1) | copy-start | bytes 1572868
  0.0 7.5 %copy-start.6 = (s32[64]{0:T(128)S(1)}, s32[64]{0:T(128)}, u32[]{:S(2)}) copy-start(s32[64]{0:T(128)} %param.8) | copy-start | bytes 772
  0.0 22.8 %copy-start.3 = (f32[4096]{0:T(1024)S(1)}, f32[4096]{0:T(1024)}, u32[]{:S(2)}) copy-start(f32[4096]{0:T(1024)} %param.10) | copy-start | bytes 49156
  4.3 37.3 %collective-permute-start = (bf16[8192,128]{1,0:T(8,128)(2,1)}, bf16[8192,128]{1,0:T(8,128)(2,1)S(1)}, u32[]{:S(2)}, u32[]{:S(2)}) collective-permute-start(bf16[8192,128]{1,0:T(8,128)(2,1)} %get-tuple-element.47), channel_id=1, source_target_pairs={{0,8},{8,0},{1,9},{9,1},{2,10},{10,2},{3,11},{11,3},{4,12},{12,4},... | collective-permute-start | bytes 6291464 | tf_op jit(solution)/shard_map/ppermute | solution.py:231
  8.6 13.6 %all-to-all-start.2 = ((bf16[8,8,512]{2,1,0:T(8,128)(2,1)}), bf16[8,8,512]{2,1,0:T(8,128)(2,1)S(1)}, u32[]{:S(2)}, u32[]{:S(2)}) async-start(bf16[8,8,512]{2,1,0:T(8,128)(2,1)} %get-tuple-element.43), calls=%async_computation.2 | async-start | bytes 131072 | tf_op jit(solution)/shard_map/all_to_all | solution.py:171
  22.2 0.6 copy-start.5
  24.5 0.9 copy-start.4
  41.6 1.3 %copy-start.2 = (bf16[8192,128]{1,0:T(8,128)(2,1)}, bf16[8192,128]{1,0:T(8,128)(2,1)S(1)}, u32[]{:S(2)}) copy-start(bf16[8192,128]{1,0:T(8,128)(2,1)S(1)} %collective-permute-done.other_ref) | copy-start | bytes 6291460

commit v2 on v1

--- a/solution.py
+++ b/solution.py
@@ -8,6 +8,7 @@
 from jax.sharding import Mesh
 from jax.sharding import PartitionSpec as P
 
+
 CHIPS = ("x", "y")
 CP = ("x", "y", "c")
 ALL = ("x", "y", "c", "z")
@@ -18,6 +19,11 @@
 VMEM = pl.BlockSpec(memory_space=pltpu.VMEM)
 SMEM = pl.BlockSpec(memory_space=pltpu.SMEM)
 ANY = pl.BlockSpec(memory_space=pl.ANY)
+MIB = 1 << 20
+
+
+def limit(mib):
+    return pltpu.CompilerParams(vmem_limit_bytes=mib * MIB)
 
 
 def iota(shape, dim):
@@ -103,31 +109,27 @@
     out_ref[...] = more_ref[...] + rows.astype(jnp.bfloat16)
 
 
-def split_kernel(weight_ref, keep_ref, send_ref, sems):
-    core = lax.axis_index("c")
-    half = keep_ref.shape[0]
-    spare = weight_ref.shape[0] - half
-    copies = [
-        pltpu.make_async_copy(
-            weight_ref.at[pl.ds(pl.multiple_of(which * spare, 16), half)], ref, sems.at[k]
-        )
-        for k, (which, ref) in enumerate(((1 - core, send_ref), (core, keep_ref)))
-    ]
-    for copy in copies:
-        copy.start()
-    for copy in copies:
-        copy.wait()
-
-
-def head_kernel(lengths_ref, first_ref, found_ref, more_ref, keep_ref, other_ref, out_ref):
+def split_kernel(weight_ref, send_ref, sem):
+    half = send_ref.shape[0]
+    start = (1 - lax.axis_index("c")) * (weight_ref.shape[0] - half)
+    copy = pltpu.make_async_copy(
+        weight_ref.at[pl.ds(pl.multiple_of(start, 16), half)], send_ref, sem
+    )
+    copy.start()
+    copy.wait()
+
+
+def head_kernel(lengths_ref, first_ref, found_ref, more_ref, weight_ref, other_ref, out_ref):
     rows = rows_in_order(lengths_ref, first_ref, found_ref).astype(jnp.bfloat16) + more_ref[...]
-    width = keep_ref.shape[1]
+    width = other_ref.shape[1]
+    start = lax.axis_index("c") * (weight_ref.shape[0] - other_ref.shape[0])
     low, high = rows[:, :width], rows[:, width:]
     first = lax.axis_index("c") == 0
     left = jnp.concatenate([jnp.where(first, low, high), jnp.where(first, high, low)], axis=1)
     for block in range(out_ref.shape[0]):
-        span = slice(block * BLOCK, (block + 1) * BLOCK)
-        weight = jnp.concatenate([keep_ref[span, :], other_ref[span, :]], axis=1)
+        own = weight_ref[pl.ds(pl.multiple_of(start + block * BLOCK, 16), BLOCK), :]
+        other = other_ref[block * BLOCK : (block + 1) * BLOCK, :]
+        weight = jnp.concatenate([own, other], axis=1)
         part = lax.dot_general(
             left, weight, (((1,), (1,)), ((), ())), preferred_element_type=jnp.float32
         )
@@ -171,26 +173,33 @@
     return lax.all_to_all(x, axes, split_axis=0, concat_axis=0, tiled=True)
 
 
-def gathered(lengths, first, hidden, gain):
-    peers = lax.axis_size("z")
-    chips, cores = lax.axis_size(CHIPS), lax.axis_size("c")
-    rows, most = pl.pallas_call(
+def picked(lengths, first, hidden):
+    return pl.pallas_call(
         pick_kernel,
-        out_shape=(shape((peers, SLOTS, hidden.shape[1]), hidden.dtype), shape((1, 1), jnp.int32)),
+        out_shape=(
+            shape((lax.axis_size("z"), SLOTS, hidden.shape[1]), hidden.dtype),
+            shape((1, 1), jnp.int32),
+        ),
         in_specs=[VMEM, SMEM, VMEM],
         out_specs=(VMEM, SMEM),
+        compiler_params=limit(4),
         name="pick",
     )(lengths, first, hidden)
+
+
+def spread(rows, gain):
+    chips, cores = lax.axis_size(CHIPS), lax.axis_size("c")
+    width = gain.shape[1] // chips
     rows = exchange(rows, "z")
-    width = gain.shape[1] // chips
     normed = pl.pallas_call(
         norm_kernel,
         out_shape=shape((chips, cores, SLOTS, width), jnp.bfloat16),
         in_specs=[VMEM, VMEM],
         out_specs=VMEM,
+        compiler_params=limit(4),
         name="norm",
     )(rows, gain)
-    return exchange(normed.reshape(chips * cores * SLOTS, width), CP), most
+    return exchange(normed.reshape(chips * cores * SLOTS, width), CP)
 
 
 def local(hidden, lengths, targets, norm_gain, lm_weight):
@@ -201,16 +210,17 @@
     chips = lax.axis_size(CHIPS)
     half = chips * BLOCK
     start = jnp.zeros((1, 1), jnp.int32)
-    found, most = gathered(lengths, start, hidden, gain)
+    rows, most = picked(lengths, start, hidden)
 
     def again(state):
         first, more = state
-        found, _ = gathered(lengths, first, hidden, gain)
+        found = spread(picked(lengths, first, hidden)[0], gain)
         more = pl.pallas_call(
             order_kernel,
             out_shape=shape(more.shape, more.dtype),
             in_specs=[VMEM, SMEM, VMEM, VMEM],
             out_specs=VMEM,
+            compiler_params=limit(4),
             name="order",
         )(lengths, first, found, more)
         return first + SLOTS, more
@@ -218,30 +228,36 @@
     _, more = lax.while_loop(
         lambda state: state[0][0, 0] < most[0, 0],
         again,
-        (start + SLOTS, jnp.zeros((n, found.shape[1]), jnp.bfloat16)),
+        (start + SLOTS, jnp.zeros((n, gain.shape[1] // chips), jnp.bfloat16)),
     )
-    keep, send = pl.pallas_call(
+    rows, weight, more = lax.optimization_barrier((rows, weight, more))
+    found = spread(rows, gain)
+    send = pl.pallas_call(
         split_kernel,
-        out_shape=(shape((half, depth), weight.dtype),) * 2,
+        out_shape=pltpu.VMEM((half, depth), weight.dtype),
         in_specs=[ANY],
-        out_specs=(VMEM, VMEM),
-        scratch_shapes=[pltpu.SemaphoreType.DMA((2,))],
+        out_specs=VMEM,
+        scratch_shapes=[pltpu.SemaphoreType.DMA(())],
+        cost_estimate=pl.CostEstimate(flops=10**9, bytes_accessed=4 * MIB, transcendentals=0),
+        compiler_params=limit(8),
         name="split",
-    )(weight)
+    )(pltpu.with_memory_space_constraint(weight, pltpu.HBM))
     other = lax.ppermute(send, "c", [(0, 1), (1, 0)])
     parts = pl.pallas_call(
         head_kernel,
         out_shape=shape((chips, n, BLOCK), jnp.float32),
         in_specs=[VMEM, SMEM, VMEM, VMEM, VMEM, VMEM],
         out_specs=VMEM,
+        compiler_params=limit(16),
         name="head",
-    )(lengths, start, found, more, keep, other)
+    )(lengths, start, found, more, weight, other)
     logits = jnp.sum(exchange(parts.astype(jnp.float16), CHIPS).astype(jnp.float32), axis=0)
     line = pl.pallas_call(
         functools.partial(stats_kernel, vocab - half, vocab),
         out_shape=shape((lax.axis_size(ALL), 1, 2 * n), jnp.float32),
         in_specs=[VMEM, VMEM],
         out_specs=VMEM,
+        compiler_params=limit(4),
         name="stats",
     )(logits, targets)
     lines = exchange(line, ALL)
@@ -250,6 +266,7 @@
         out_shape=shape((1, n), jnp.float32),
         in_specs=[VMEM],
         out_specs=VMEM,
+        compiler_params=limit(4),
         name="join",
     )(lines)
     return out[0]

time: 94.7 us -> 79.1 us (0.84)
  blocking collectives: 56.2 us -> 67.9 us
  Pallas kernels: 15.7 us -> 6.52 us
  waiting for transfers between devices: 7.14 us -> 0.01 us
  starting transfers between devices: 9.78 us -> 3.29 us
  other arithmetic: 2.63 us -> 0.42 us
  local copies, waits for them, and re-layouts: 2.13 us -> 0.03 us
    all_to_all x3 -> x4, blocking collectives: 56.2 us -> 67.9 us  [exchange(): return lax.all_to_all(x, axes, split_axis=0, concat_axis=0, tiled=True)]
    all_to_all x1 -> x0, waiting for transfers between devices: 7.14 us -> none  [exchange(): return lax.all_to_all(x, axes, split_axis=0, concat_axis=0, tiled=True)]
    all_to_all x1 -> x0, starting transfers between devices: 6.5 us -> none  [exchange(): return lax.all_to_all(x, axes, split_axis=0, concat_axis=0, tiled=True)]
    pallas_call x1, Pallas kernels: 5.25 us -> 1.66 us  [local(): pl.pallas_call(head_kernel, out_shape=shape((chips, n, BLOCK), jnp.float3...]
    pallas_call x3, Pallas kernels: 6.88 us -> 3.76 us  [the longest x1 1.88 us: picked(): pl.pallas_call(pick_kernel, out_shape=(shape((lax.axis_size('z'), SLOTS,...]
    unnamed x12 -> x8, local copies, waits for them, and re-layouts: 2.12 us -> 0.03 us
    convert_element_type x1, other arithmetic: 1.84 us -> 0.27 us  [local(): parts.astype(jnp.float16)]
    pallas_call x1, Pallas kernels: 1.83 us -> 0.28 us  [local(): pl.pallas_call(functools.partial(stats_kernel, vocab - half, vocab), out_...]
  transfers between devices with their start and end apart: 2 -> 1, of which waited for: 1 -> 0; matrix products, arithmetic and copies ran while one was open for 0% -> 0% of each run, Pallas kernels for 3% -> 0%
where the time goes in v2:
time: 79.1 us; the launch traced here: 78.9 us
  blocking collectives  67.9 us (86%)
  Pallas kernels  6.52 us (8%)
  starting transfers between devices  3.29 us (4%)
    all_to_all x4, blocking collectives, exchange(): return lax.all_to_all(x, axes, split_axis=0, concat_axis=0, tiled=True)  67.9 us
    ppermute x1, starting transfers between devices, local(): other = lax.ppermute(send, 'c', [(0, 1), (1, 0)])  3.29 us
    pallas_call x1, Pallas kernels, picked(): pl.pallas_call(pick_kernel, out_shape=(shape((lax.axis_size('z'), SLOTS,...  1.88 us
    pallas_call x1, Pallas kernels, local(): pl.pallas_call(split_kernel, out_shape=pltpu.VMEM((half, depth), weight.d...  1.76 us
    pallas_call x1, Pallas kernels, local(): pl.pallas_call(head_kernel, out_shape=shape((chips, n, BLOCK), jnp.float3...  1.66 us
  transfers between devices with their start and end apart: 1, of which 0 were waited for; matrix products, arithmetic and copies ran while one was open for 0% of the time, Pallas kernels for 0%

profile of v2, /device:TPU:1, one launch (start us, length us, event | category | flops | bytes accessed | tf_op | source)
XLA Modules:
  0.0 78.9 jit_solution(10030503696091007963)
XLA Ops:
  0.0 1.9 %pick.2 = (bf16[8,8,512]{2,1,0:T(8,128)(2,1)S(1)}, s32[1,1]{1,0:T(1,128)}) custom-call(s32[1,64]{1,0:T(1,128)} %bitcast.20, s32[1,1]{1,0:T(1,128)} %constant.0.clone.1.first_ref, bf16[512,512]{1,0:T(8,128)(2,1)} %hidden_ref.1), custom_call_target="tpu_custom_call" | custom-call | tf_op jit(solution)/shard_map/pick/pallas_call | solution.py:177
  1.9 0.6 while.10
  2.5 0.0 copy-start.2
  2.5 0.0 copy-start
  2.6 0.0 copy-start.3
  2.6 1.8 %split.1 = bf16[8192,128]{1,0:T(8,128)(2,1)S(1)} custom-call(bf16[16032,128]{1,0:T(8,128)(2,1)} %bitcast.13), custom_call_target="tpu_custom_call" | custom-call | flops 1000000000 | bytes 4194304 | tf_op jit(solution)/shard_map/split/pallas_call | solution.py:235
  4.3 3.3 %collective-permute-start = (bf16[8192,128]{1,0:T(8,128)(2,1)S(1)}, bf16[8192,128]{1,0:T(8,128)(2,1)S(1)}, u32[]{:S(2)}, u32[]{:S(2)}) collective-permute-start(bf16[8192,128]{1,0:T(8,128)(2,1)S(1)} %split.1), channel_id=1, source_target_pairs={{0,8},{8,0},{1,9},{9,1},{2,10},{10,2},{3,11},{11,3},{4,12},{12,4},... | collective-permute-start | bytes 6291464 | tf_op jit(solution)/shard_map/ppermute | solution.py:245
  7.6 13.4 %all_to_all.40.rows_ref = bf16[8,8,512]{2,1,0:T(8,128)(2,1)S(1)} all-to-all(bf16[8,8,512]{2,1,0:T(8,128)(2,1)S(1)} %get-tuple-element.47), channel_id=1, replica_groups=mesh['x'=4,'y'=4,'c'=2,'z'=8] {'z'}, dimensions={0} | all-to-all | bytes 131072 | tf_op jit(solution)/shard_map/all_to_all | solution.py:173
  21.0 0.0 copy-done.2
  21.0 0.1 norm.2
  21.2 16.1 %all_to_all.41 = bf16[32,8,256]{2,1,0:T(8,128)(2,1)S(1)} all-to-all(bf16[32,8,256]{2,1,0:T(8,128)(2,1)S(1)} %bitcast.17), channel_id=1, replica_groups=mesh['x'=4,'y'=4,'c'=2,'z'=8] {'x','y','c'}, dimensions={0} | all-to-all | bytes 262144 | tf_op jit(solution)/shard_map/all_to_all | solution.py:173
  37.3 0.0 collective-permute-done.other_ref
  37.3 0.0 copy-done
  37.3 0.0 copy-done.3
  37.3 1.7 %head.1 = f32[16,64,512]{2,1,0:T(8,128)S(1)} custom-call(s32[1,64]{1,0:T(1,128)S(1)} %copy-done.3, s32[1,1]{1,0:T(1,128)} %constant.0.clone.1.first_ref, bf16[256,256]{1,0:T(8,128)(2,1)S(1)} %bitcast.16, bf16[64,256]{1,0:T(8,128)(2,1)S(1)} %get-tuple-element.48.more_ref, bf16[16032,128]{1,0:T(8,128)(2,1)S(1)} %bitcast.14, ...), custom_call_target="tpu_custom_call" | custom-call | tf_op jit(solution)/shard_map/head/pallas_call | solution.py:246
  38.9 0.3 convert_element_type.6
  39.2 0.0 copy-start.1
  39.2 18.6 %all_to_all.42 = f16[16,64,512]{2,1,0:T(8,128)(2,1)S(1)} all-to-all(f16[16,64,512]{2,1,0:T(8,128)(2,1)S(1)} %convert_element_type.6), channel_id=1, replica_groups=mesh['x'=4,'y'=4,'c'=2,'z'=8] {'x','y'}, dimensions={0} | all-to-all | bytes 2097152 | tf_op jit(solution)/shard_map/all_to_all | solution.py:173
  57.9 0.1 convert_reduce_fusion.logits_ref
  58.0 0.0 copy-done.1
  58.0 0.3 stats.1
  58.3 19.8 %all_to_all.43.found_ref = f32[256,1,128]{2,1,0:T(1,128)S(1)} all-to-all(f32[256,1,128]{2,1,0:T(1,128)S(1)} %stats.1), channel_id=1, replica_groups=mesh['x'=4,'y'=4,'c'=2,'z'=8] {'x','y','c','z'}, dimensions={0} | all-to-all | bytes 262144 | tf_op jit(solution)/shard_map/all_to_all | solution.py:173
  78.1 0.8 %join.1 = f32[1,64]{1,0:T(1,128)} custom-call(f32[256,1,128]{2,1,0:T(1,128)S(1)} %all_to_all.43.found_ref), custom_call_target="tpu_custom_call" | custom-call | tf_op jit(solution)/shard_map/join/pallas_call | solution.py:264
  (1 shorter events, 0.0 us)
Async XLA Ops:
  2.5 18.5 %copy-start.2 = (f32[1,4096]{1,0:T(1,128)S(1)}, f32[1,4096]{1,0:T(1,128)}, u32[]{:S(2)}) copy-start(f32[1,4096]{1,0:T(1,128)} %get-tuple-element.119) | copy-start | bytes 49156
  2.5 34.7 %copy-start = (bf16[128,16032]{0,1:T(8,128)(2,1)S(1)}, bf16[128,16032]{0,1:T(8,128)(2,1)}, u32[]{:S(2)}) copy-start(bf16[128,16032]{0,1:T(8,128)(2,1)} %param.11) | copy-start | bytes 12312580
  2.6 34.7 %copy-start.3 = (s32[1,64]{1,0:T(1,128)S(1)}, s32[1,64]{1,0:T(1,128)}, u32[]{:S(2)}) copy-start(s32[1,64]{1,0:T(1,128)} %get-tuple-element.120) | copy-start | bytes 772
  4.3 32.9 %collective-permute-start = (bf16[8192,128]{1,0:T(8,128)(2,1)S(1)}, bf16[8192,128]{1,0:T(8,128)(2,1)S(1)}, u32[]{:S(2)}, u32[]{:S(2)}) collective-permute-start(bf16[8192,128]{1,0:T(8,128)(2,1)S(1)} %split.1), channel_id=1, source_target_pairs={{0,8},{8,0},{1,9},{9,1},{2,10},{10,2},{3,11},{11,3},{4,12},{12,4},... | collective-permute-start | bytes 6291464 | tf_op jit(solution)/shard_map/ppermute | solution.py:245
  39.2 18.8 %copy-start.1 = (s32[64]{0:T(128)S(1)}, s32[64]{0:T(128)}, u32[]{:S(2)}) copy-start(s32[64]{0:T(128)} %param.9) | copy-start | bytes 772

commit v3 on v2

--- a/solution.py
+++ b/solution.py
@@ -18,7 +18,7 @@
 
 VMEM = pl.BlockSpec(memory_space=pltpu.VMEM)
 SMEM = pl.BlockSpec(memory_space=pltpu.SMEM)
-ANY = pl.BlockSpec(memory_space=pl.ANY)
+HBM = pl.BlockSpec(memory_space=pltpu.HBM)
 MIB = 1 << 20
 
 
@@ -64,13 +64,31 @@
     wanted = owned & (slot == iota((SLOTS, n), 0))
     at = total(jnp.where(wanted, ends - base + 1.0, 0.0), 1) - 1.0
     selector = (at == iota((SLOTS, rows), 1)).astype(jnp.bfloat16)
+    owners = iota((32, n), 0)
+    counts = total(jnp.where(jnp.floor(ends / rows) == owners, 1.0, 0.0), 1)
+    most_ref[0, 0] = jnp.max(counts).astype(jnp.int32)
     picked = jnp.dot(selector, hidden_ref[...], preferred_element_type=jnp.float32)
     picked = picked.astype(jnp.bfloat16)
     for peer in range(out_ref.shape[0]):
         out_ref[peer] = picked
-    owners = iota((32, n), 0)
-    counts = total(jnp.where(jnp.floor(ends / rows) == owners, 1.0, 0.0), 1)
-    most_ref[0, 0] = jnp.max(counts).astype(jnp.int32)
+
+
+def half_of(weight_ref, half, core):
+    start = core * (weight_ref.shape[0] - half)
+    return weight_ref.at[pl.ds(pl.multiple_of(start, 16), half)]
+
+
+def begin_kernel(
+    lengths_ref, first_ref, hidden_ref, weight_ref, out_ref, most_ref, send_ref, held, sems
+):
+    source = half_of(weight_ref, send_ref.shape[0], 1 - lax.axis_index("c"))
+    rows = pltpu.make_async_copy(hidden_ref, held, sems.at[0])
+    swap = pltpu.make_async_copy(source, send_ref, sems.at[1])
+    rows.start()
+    swap.start()
+    rows.wait()
+    pick_kernel(lengths_ref, first_ref, held, out_ref, most_ref)
+    swap.wait()
 
 
 def norm_kernel(rows_ref, gain_ref, out_ref):
@@ -109,27 +127,23 @@
     out_ref[...] = more_ref[...] + rows.astype(jnp.bfloat16)
 
 
-def split_kernel(weight_ref, send_ref, sem):
-    half = send_ref.shape[0]
-    start = (1 - lax.axis_index("c")) * (weight_ref.shape[0] - half)
+def keep_kernel(weight_ref, keep_ref, sem):
     copy = pltpu.make_async_copy(
-        weight_ref.at[pl.ds(pl.multiple_of(start, 16), half)], send_ref, sem
+        half_of(weight_ref, keep_ref.shape[0], lax.axis_index("c")), keep_ref, sem
     )
     copy.start()
     copy.wait()
 
 
-def head_kernel(lengths_ref, first_ref, found_ref, more_ref, weight_ref, other_ref, out_ref):
+def head_kernel(lengths_ref, first_ref, found_ref, more_ref, keep_ref, other_ref, out_ref):
     rows = rows_in_order(lengths_ref, first_ref, found_ref).astype(jnp.bfloat16) + more_ref[...]
-    width = other_ref.shape[1]
-    start = lax.axis_index("c") * (weight_ref.shape[0] - other_ref.shape[0])
+    width = keep_ref.shape[1]
     low, high = rows[:, :width], rows[:, width:]
     first = lax.axis_index("c") == 0
     left = jnp.concatenate([jnp.where(first, low, high), jnp.where(first, high, low)], axis=1)
     for block in range(out_ref.shape[0]):
-        own = weight_ref[pl.ds(pl.multiple_of(start + block * BLOCK, 16), BLOCK), :]
-        other = other_ref[block * BLOCK : (block + 1) * BLOCK, :]
-        weight = jnp.concatenate([own, other], axis=1)
+        span = slice(block * BLOCK, (block + 1) * BLOCK)
+        weight = jnp.concatenate([keep_ref[span, :], other_ref[span, :]], axis=1)
         part = lax.dot_general(
             left, weight, (((1,), (1,)), ((), ())), preferred_element_type=jnp.float32
         )
@@ -153,12 +167,12 @@
     both = top + jnp.log(total(jnp.exp(logits - top), 1))
     down, across = iota((n, 2 * n), 0), iota((n, 2 * n), 1)
     line = jnp.where(across == down, both, 0.0) + jnp.where(across == down + n, found, 0.0)
-    out_ref[...] = jnp.broadcast_to(total(line, 0)[None], out_ref.shape)
+    out_ref[...] = jnp.broadcast_to(total(line, 0), out_ref.shape)
 
 
 def join_kernel(found_ref, out_ref):
     n = out_ref.shape[1]
-    lines = found_ref[:, 0, :]
+    lines = found_ref[...]
     top = jnp.max(lines, axis=0, keepdims=True)
     both = top + jnp.log(total(jnp.exp(lines - top), 0))
     chosen = total(lines, 0)
@@ -167,6 +181,10 @@
 
 def shape(dims, dtype):
     return jax.ShapeDtypeStruct(dims, dtype)
+
+
+def in_hbm(x):
+    return pltpu.with_memory_space_constraint(x, pltpu.HBM)
 
 
 def exchange(x, axes):
@@ -210,7 +228,20 @@
     chips = lax.axis_size(CHIPS)
     half = chips * BLOCK
     start = jnp.zeros((1, 1), jnp.int32)
-    rows, most = picked(lengths, start, hidden)
+    rows, most, send = pl.pallas_call(
+        begin_kernel,
+        out_shape=(
+            pltpu.VMEM((lax.axis_size("z"), SLOTS, hidden.shape[1]), hidden.dtype),
+            shape((1, 1), jnp.int32),
+            pltpu.VMEM((half, depth), weight.dtype),
+        ),
+        in_specs=[VMEM, SMEM, HBM, HBM],
+        out_specs=(VMEM, SMEM, VMEM),
+        scratch_shapes=[pltpu.VMEM(hidden.shape, hidden.dtype), pltpu.SemaphoreType.DMA((2,))],
+        compiler_params=limit(8),
+        name="begin",
+    )(lengths, start, in_hbm(hidden), in_hbm(weight))
+    other = lax.ppermute(send, "c", [(0, 1), (1, 0)])
 
     def again(state):
         first, more = state
@@ -232,17 +263,15 @@
     )
     rows, weight, more = lax.optimization_barrier((rows, weight, more))
     found = spread(rows, gain)
-    send = pl.pallas_call(
-        split_kernel,
+    keep = pl.pallas_call(
+        keep_kernel,
         out_shape=pltpu.VMEM((half, depth), weight.dtype),
-        in_specs=[ANY],
+        in_specs=[HBM],
         out_specs=VMEM,
         scratch_shapes=[pltpu.SemaphoreType.DMA(())],
-        cost_estimate=pl.CostEstimate(flops=10**9, bytes_accessed=4 * MIB, transcendentals=0),
         compiler_params=limit(8),
-        name="split",
-    )(pltpu.with_memory_space_constraint(weight, pltpu.HBM))
-    other = lax.ppermute(send, "c", [(0, 1), (1, 0)])
+        name="half",
+    )(in_hbm(weight))
     parts = pl.pallas_call(
         head_kernel,
         out_shape=shape((chips, n, BLOCK), jnp.float32),
@@ -250,11 +279,11 @@
         out_specs=VMEM,
         compiler_params=limit(16),
         name="head",
-    )(lengths, start, found, more, weight, other)
+    )(lengths, start, found, more, keep, other)
     logits = jnp.sum(exchange(parts.astype(jnp.float16), CHIPS).astype(jnp.float32), axis=0)
     line = pl.pallas_call(
         functools.partial(stats_kernel, vocab - half, vocab),
-        out_shape=shape((lax.axis_size(ALL), 1, 2 * n), jnp.float32),
+        out_shape=shape((lax.axis_size(ALL), 2 * n), jnp.float32),
         in_specs=[VMEM, VMEM],
         out_specs=VMEM,
         compiler_params=limit(4),

time: 79.1 us -> 81.7 us (1.033)
  blocking collectives: 67.9 us -> 51.8 us
  starting transfers between devices: 3.29 us -> 11.9 us
  waiting for transfers between devices: 0.01 us -> 6.06 us
  Pallas kernels: 6.52 us -> 10.4 us
    all_to_all x4 -> x3, blocking collectives: 67.9 us -> 51.8 us  [exchange(): return lax.all_to_all(x, axes, split_axis=0, concat_axis=0, tiled=True)]
    all_to_all x0 -> x1, starting transfers between devices: none -> 8.64 us  [exchange(): return lax.all_to_all(x, axes, split_axis=0, concat_axis=0, tiled=True)]
    all_to_all x0 -> x1, waiting for transfers between devices: none -> 6.06 us  [exchange(): return lax.all_to_all(x, axes, split_axis=0, concat_axis=0, tiled=True)]
    pallas_call x2, Pallas kernels: 3.64 us -> 5.47 us  [the longest x1 3.85 us: local(): pl.pallas_call(begin_kernel, out_shape=(pltpu.VMEM((lax.axis_size('z'), S...]
    pallas_call x1, Pallas kernels: 1.66 us -> 3.24 us  [local(): pl.pallas_call(head_kernel, out_shape=shape((chips, n, BLOCK), jnp.float3...]
  transfers between devices with their start and end apart: 1 -> 2, of which waited for: 0 -> 1; matrix products, arithmetic and copies ran while one was open for 0% -> 0% of each run, Pallas kernels for 0% -> 3%
where the time goes in v3:
time: 81.7 us; the launch traced here: 81.4 us
  blocking collectives  51.8 us (63%)
  starting transfers between devices  11.9 us (15%)
  Pallas kernels  10.4 us (13%)
  waiting for transfers between devices  6.06 us (7%)
    all_to_all x3, blocking collectives, exchange(): return lax.all_to_all(x, axes, split_axis=0, concat_axis=0, tiled=True)  51.8 us
    all_to_all x1, starting transfers between devices, exchange(): return lax.all_to_all(x, axes, split_axis=0, concat_axis=0, tiled=True)  8.64 us
    all_to_all x1, waiting for transfers between devices, exchange(): return lax.all_to_all(x, axes, split_axis=0, concat_axis=0, tiled=True)  6.06 us
    pallas_call x1, Pallas kernels, local(): pl.pallas_call(begin_kernel, out_shape=(pltpu.VMEM((lax.axis_size('z'), S...  3.85 us
    ppermute x1, starting transfers between devices, local(): other = lax.ppermute(send, 'c', [(0, 1), (1, 0)])  3.29 us
    pallas_call x1, Pallas kernels, local(): pl.pallas_call(head_kernel, out_shape=shape((chips, n, BLOCK), jnp.float3...  3.24 us
  transfers between devices with their start and end apart: 2, of which 1 were waited for; matrix products, arithmetic and copies ran while one was open for 0% of the time, Pallas kernels for 3%

profile of v3, /device:TPU:1, one launch (start us, length us, event | category | flops | bytes accessed | tf_op | source)
XLA Modules:
  0.0 81.4 jit_solution(8830315773702700752)
XLA Ops:
  0.0 0.0 copy-start.1
  0.0 0.0 copy-start.2
  0.0 0.0 copy-start.3
  0.0 3.9 %begin.1 = (bf16[8,8,512]{2,1,0:T(8,128)(2,1)S(1)}, s32[1,1]{1,0:T(1,128)}, bf16[8192,128]{1,0:T(8,128)(2,1)}) custom-call(s32[1,64]{1,0:T(1,128)} %bitcast.25, s32[1,1]{1,0:T(1,128)} %constant.0.clone.1.first_ref, bf16[512,512]{1,0:T(8,128)(2,1)} %hidden_ref.1, bf16[16032,128]{1,0:T(8,128)(2,1)} %bitcast.22), custom_call_target="tpu_custom_call" | custom-call | tf_op jit(solution)/shard_map/begin/pallas_call | solution.py:231
  3.9 3.3 %collective-permute-start = (bf16[8192,128]{1,0:T(8,128)(2,1)}, bf16[8192,128]{1,0:T(8,128)(2,1)}, u32[]{:S(2)}, u32[]{:S(2)}) collective-permute-start(bf16[8192,128]{1,0:T(8,128)(2,1)} %get-tuple-element.51), channel_id=1, source_target_pairs={{0,8},{8,0},{1,9},{9,1},{2,10},{10,2},{3,11},{11,3},{4,12},{12,4},... | collective-permute-start | bytes 6291464 | tf_op jit(solution)/shard_map/ppermute | solution.py:244
  7.2 0.0 copy-done.1
  7.2 0.0 copy-done.2
  7.2 0.0 copy-done.3
  7.2 0.6 while.10
  7.8 13.4 %all_to_all.46.rows_ref = bf16[8,8,512]{2,1,0:T(8,128)(2,1)S(1)} all-to-all(bf16[8,8,512]{2,1,0:T(8,128)(2,1)S(1)} %get-tuple-element.48), channel_id=1, replica_groups=mesh['x'=4,'y'=4,'c'=2,'z'=8] {'z'}, dimensions={0} | all-to-all | bytes 131072 | tf_op jit(solution)/shard_map/all_to_all | solution.py:191
  21.2 0.8 norm.2
  22.0 8.6 %all-to-all-start.3 = ((bf16[32,8,256]{2,1,0:T(8,128)(2,1)}), bf16[32,8,256]{2,1,0:T(8,128)(2,1)S(1)}, u32[]{:S(2)}, u32[]{:S(2)}) async-start(bf16[32,8,256]{2,1,0:T(8,128)(2,1)} %bitcast.6), calls=%async_computation.3 | async-start | bytes 262144 | tf_op jit(solution)/shard_map/all_to_all | solution.py:191
  30.6 1.6 %half.1.keep_ref = bf16[8192,128]{1,0:T(8,128)(2,1)S(1)} custom-call(bf16[16032,128]{1,0:T(8,128)(2,1)} %bitcast.23), custom_call_target="tpu_custom_call" | custom-call | tf_op jit(solution)/shard_map/half/pallas_call | solution.py:266
  32.3 6.1 %all-to-all-done.3 = bf16[32,8,256]{2,1,0:T(8,128)(2,1)S(1)} async-done(((bf16[32,8,256]{2,1,0:T(8,128)(2,1)}), bf16[32,8,256]{2,1,0:T(8,128)(2,1)S(1)}, u32[]{:S(2)}, u32[]{:S(2)}) %all-to-all-start.3) | async-done | bytes 131104 | tf_op jit(solution)/shard_map/all_to_all | solution.py:191
  38.3 0.0 collective-permute-done.other_ref
  38.3 3.2 %head.1 = f32[16,64,512]{2,1,0:T(8,128)S(1)} custom-call(s32[1,64]{1,0:T(1,128)S(1)} %get-tuple-element.121, s32[1,1]{1,0:T(1,128)} %constant.0.clone.1.first_ref, bf16[256,256]{1,0:T(8,128)(2,1)S(1)} %bitcast.18, bf16[64,256]{1,0:T(8,128)(2,1)S(1)} %get-tuple-element.49.more_ref, bf16[8192,128]{1,0:T(8,128)(2,1)S(1)} %half.1.keep_ref, ...), custom_call_target="tpu_custom_call" | custom-call | tf_op jit(solution)/shard_map/head/pallas_call | solution.py:275
  41.6 0.3 convert_element_type.6
  41.8 0.0 copy-start
  41.9 18.6 %all_to_all.47 = f16[16,64,512]{2,1,0:T(8,128)(2,1)S(1)} all-to-all(f16[16,64,512]{2,1,0:T(8,128)(2,1)S(1)} %convert_element_type.6), channel_id=1, replica_groups=mesh['x'=4,'y'=4,'c'=2,'z'=8] {'x','y'}, dimensions={0} | all-to-all | bytes 2097152 | tf_op jit(solution)/shard_map/all_to_all | solution.py:191
  60.5 0.1 convert_reduce_fusion.logits_ref
  60.6 0.0 copy-done
  60.6 0.2 stats.1
  60.9 19.8 %all_to_all.48 = f32[256,1,128]{2,1,0:T(1,128)S(1)} all-to-all(f32[256,1,128]{2,1,0:T(1,128)S(1)} %bitcast.19), channel_id=1, replica_groups=mesh['x'=4,'y'=4,'c'=2,'z'=8] {'x','y','c','z'}, dimensions={0} | all-to-all | bytes 262144 | tf_op jit(solution)/shard_map/all_to_all | solution.py:191
  80.6 0.7 join.1
  (1 shorter events, 0.0 us)
Async XLA Ops:
  0.0 7.2 %copy-start.1 = (bf16[512,512]{1,0:T(8,128)(2,1)S(1)}, bf16[512,512]{1,0:T(8,128)(2,1)}, u32[]{:S(2)}) copy-start(bf16[512,512]{1,0:T(8,128)(2,1)} %hidden_ref.1) | copy-start | bytes 1572868
  0.0 7.2 %copy-start.2 = (f32[4096]{0:T(1024)S(1)}, f32[4096]{0:T(1024)}, u32[]{:S(2)}) copy-start(f32[4096]{0:T(1024)} %param.10) | copy-start | bytes 49156
  0.0 7.2 %copy-start.3 = (s32[64]{0:T(128)S(1)}, s32[64]{0:T(128)}, u32[]{:S(2)}) copy-start(s32[64]{0:T(128)} %param.8) | copy-start | bytes 772
  3.9 34.5 %collective-permute-start = (bf16[8192,128]{1,0:T(8,128)(2,1)}, bf16[8192,128]{1,0:T(8,128)(2,1)}, u32[]{:S(2)}, u32[]{:S(2)}) collective-permute-start(bf16[8192,128]{1,0:T(8,128)(2,1)} %get-tuple-element.51), channel_id=1, source_target_pairs={{0,8},{8,0},{1,9},{9,1},{2,10},{10,2},{3,11},{11,3},{4,12},{12,4},... | collective-permute-start | bytes 6291464 | tf_op jit(solution)/shard_map/ppermute | solution.py:244
  22.0 16.3 %all-to-all-start.3 = ((bf16[32,8,256]{2,1,0:T(8,128)(2,1)}), bf16[32,8,256]{2,1,0:T(8,128)(2,1)S(1)}, u32[]{:S(2)}, u32[]{:S(2)}) async-start(bf16[32,8,256]{2,1,0:T(8,128)(2,1)} %bitcast.6), calls=%async_computation.3 | async-start | bytes 262144 | tf_op jit(solution)/shard_map/all_to_all | solution.py:191
  41.8 18.8 %copy-start = (s32[64]{0:T(128)S(1)}, s32[64]{0:T(128)}, u32[]{:S(2)}) copy-start(s32[64]{0:T(128)} %param.9) | copy-start | bytes 772

commit v4 on v2

--- a/solution.py
+++ b/solution.py
@@ -14,11 +14,12 @@
 ALL = ("x", "y", "c", "z")
 SLOTS = 8
 BLOCK = 512
+PIECES = 8
 NEG = -1e30
 
 VMEM = pl.BlockSpec(memory_space=pltpu.VMEM)
 SMEM = pl.BlockSpec(memory_space=pltpu.SMEM)
-ANY = pl.BlockSpec(memory_space=pl.ANY)
+HBM = pl.BlockSpec(memory_space=pltpu.HBM)
 MIB = 1 << 20
 
 
@@ -53,24 +54,28 @@
     return total(jnp.where(down <= across, as_column(row), 0.0), 0) - 1.0, column
 
 
-def pick_kernel(lengths_ref, first_ref, hidden_ref, out_ref, most_ref):
-    n = lengths_ref.shape[1]
-    rows = hidden_ref.shape[0]
+def pick_kernel(lengths_ref, *refs):
+    *first_ref, hidden_ref, out_ref, most_ref, held, sem = refs
+    rows = pltpu.make_async_copy(hidden_ref, held, sem)
+    rows.start()
+    n, rows_here = lengths_ref.shape[1], held.shape[0]
     ends, _ = ends_of(lengths_ref)
-    base = (place() * rows).astype(jnp.float32)
-    owned = (ends >= base) & (ends < base + rows)
+    base = (place() * rows_here).astype(jnp.float32)
+    owned = (ends >= base) & (ends < base + rows_here)
     before = total(jnp.where(ends < base, 1.0, 0.0), 1)
-    slot = iota((1, n), 1) - before - first_ref[0, 0].astype(jnp.float32)
+    slot = iota((1, n), 1) - before
+    if first_ref:
+        slot = slot - first_ref[0][0, 0].astype(jnp.float32)
     wanted = owned & (slot == iota((SLOTS, n), 0))
     at = total(jnp.where(wanted, ends - base + 1.0, 0.0), 1) - 1.0
-    selector = (at == iota((SLOTS, rows), 1)).astype(jnp.bfloat16)
-    picked = jnp.dot(selector, hidden_ref[...], preferred_element_type=jnp.float32)
+    selector = (at == iota((SLOTS, rows_here), 1)).astype(jnp.bfloat16)
+    counts = total(jnp.where(jnp.floor(ends / rows_here) == iota((32, n), 0), 1.0, 0.0), 1)
+    most_ref[0, 0] = jnp.max(counts).astype(jnp.int32)
+    rows.wait()
+    picked = jnp.dot(selector, held[...], preferred_element_type=jnp.float32)
     picked = picked.astype(jnp.bfloat16)
     for peer in range(out_ref.shape[0]):
         out_ref[peer] = picked
-    owners = iota((32, n), 0)
-    counts = total(jnp.where(jnp.floor(ends / rows) == owners, 1.0, 0.0), 1)
-    most_ref[0, 0] = jnp.max(counts).astype(jnp.int32)
 
 
 def norm_kernel(rows_ref, gain_ref, out_ref):
@@ -90,14 +95,14 @@
             out_ref[chip, core] = normed
 
 
-def rows_in_order(lengths_ref, first_ref, found_ref):
+def rows_in_order(lengths_ref, found_ref, first=0.0):
     n = lengths_ref.shape[1]
     places = found_ref.shape[0]
     rows = 512
     ends_row, ends = ends_of(lengths_ref)
     owner = jnp.floor(ends / rows)
     before = total(jnp.where(ends_row < owner * rows, 1.0, 0.0), 1)
-    slot = iota((n, 1), 0) - before - first_ref[0, 0].astype(jnp.float32)
+    slot = iota((n, 1), 0) - before - first
     inside = (slot >= 0.0) & (slot < SLOTS)
     at = jnp.where(inside, owner * SLOTS + slot, -1.0)
     selector = (at == iota((n, places), 1)).astype(jnp.bfloat16)
@@ -105,31 +110,43 @@
 
 
 def order_kernel(lengths_ref, first_ref, found_ref, more_ref, out_ref):
-    rows = rows_in_order(lengths_ref, first_ref, found_ref)
+    first = first_ref[0, 0].astype(jnp.float32)
+    rows = rows_in_order(lengths_ref, found_ref, first)
     out_ref[...] = more_ref[...] + rows.astype(jnp.bfloat16)
 
 
-def split_kernel(weight_ref, send_ref, sem):
-    half = send_ref.shape[0]
-    start = (1 - lax.axis_index("c")) * (weight_ref.shape[0] - half)
+def half_kernel(weight_ref, keep_ref, sem):
+    half = keep_ref.shape[0]
+    start = lax.axis_index("c") * (weight_ref.shape[0] - half)
     copy = pltpu.make_async_copy(
-        weight_ref.at[pl.ds(pl.multiple_of(start, 16), half)], send_ref, sem
+        weight_ref.at[pl.ds(pl.multiple_of(start, 16), half)], keep_ref, sem
     )
     copy.start()
     copy.wait()
 
 
-def head_kernel(lengths_ref, first_ref, found_ref, more_ref, weight_ref, other_ref, out_ref):
-    rows = rows_in_order(lengths_ref, first_ref, found_ref).astype(jnp.bfloat16) + more_ref[...]
-    width = other_ref.shape[1]
-    start = lax.axis_index("c") * (weight_ref.shape[0] - other_ref.shape[0])
+def head_kernel(lengths_ref, found_ref, more_ref, keep_ref, other_ref, out_ref, held, sems):
+    half, width = keep_ref.shape
+    first = lax.axis_index("c") == 0
+    start = lax.axis_index("c") * (other_ref.shape[0] - half)
+    piece = half // PIECES
+    copies = []
+    for k in range(PIECES):
+        rows = pl.ds(pl.multiple_of(start + k * piece, 16), piece)
+        copy = pltpu.make_async_copy(other_ref.at[rows], held.at[k], sems.at[k])
+        copy.start()
+        copies.append(copy)
+    rows = rows_in_order(lengths_ref, found_ref).astype(jnp.bfloat16) + more_ref[...]
     low, high = rows[:, :width], rows[:, width:]
-    first = lax.axis_index("c") == 0
     left = jnp.concatenate([jnp.where(first, low, high), jnp.where(first, high, low)], axis=1)
     for block in range(out_ref.shape[0]):
-        own = weight_ref[pl.ds(pl.multiple_of(start + block * BLOCK, 16), BLOCK), :]
-        other = other_ref[block * BLOCK : (block + 1) * BLOCK, :]
-        weight = jnp.concatenate([own, other], axis=1)
+        at = block * BLOCK
+        k, inside = divmod(at, piece)
+        if inside == 0:
+            copies[k].wait()
+        weight = jnp.concatenate(
+            [keep_ref[at : at + BLOCK, :], held[k, inside : inside + BLOCK, :]], axis=1
+        )
         part = lax.dot_general(
             left, weight, (((1,), (1,)), ((), ())), preferred_element_type=jnp.float32
         )
@@ -153,12 +170,12 @@
     both = top + jnp.log(total(jnp.exp(logits - top), 1))
     down, across = iota((n, 2 * n), 0), iota((n, 2 * n), 1)
     line = jnp.where(across == down, both, 0.0) + jnp.where(across == down + n, found, 0.0)
-    out_ref[...] = jnp.broadcast_to(total(line, 0)[None], out_ref.shape)
+    out_ref[...] = jnp.broadcast_to(total(line, 0), out_ref.shape)
 
 
 def join_kernel(found_ref, out_ref):
     n = out_ref.shape[1]
-    lines = found_ref[:, 0, :]
+    lines = found_ref[...]
     top = jnp.max(lines, axis=0, keepdims=True)
     both = top + jnp.log(total(jnp.exp(lines - top), 0))
     chosen = total(lines, 0)
@@ -169,8 +186,24 @@
     return jax.ShapeDtypeStruct(dims, dtype)
 
 
+def in_hbm(x):
+    return pltpu.with_memory_space_constraint(x, pltpu.HBM)
+
+
 def exchange(x, axes):
     return lax.all_to_all(x, axes, split_axis=0, concat_axis=0, tiled=True)
+
+
+def own_half(weight, half):
+    return pl.pallas_call(
+        half_kernel,
+        out_shape=shape((half, weight.shape[1]), weight.dtype),
+        in_specs=[HBM],
+        out_specs=VMEM,
+        scratch_shapes=[pltpu.SemaphoreType.DMA(())],
+        compiler_params=limit(8),
+        name="half",
+    )(in_hbm(weight))
 
 
 def picked(lengths, first, hidden):
@@ -180,11 +213,12 @@
             shape((lax.axis_size("z"), SLOTS, hidden.shape[1]), hidden.dtype),
             shape((1, 1), jnp.int32),
         ),
-        in_specs=[VMEM, SMEM, VMEM],
+        in_specs=[VMEM] + [SMEM] * len(first) + [HBM],
         out_specs=(VMEM, SMEM),
+        scratch_shapes=[pltpu.VMEM(hidden.shape, hidden.dtype), pltpu.SemaphoreType.DMA(())],
         compiler_params=limit(4),
         name="pick",
-    )(lengths, first, hidden)
+    )(lengths, *first, in_hbm(hidden))
 
 
 def spread(rows, gain):
@@ -210,11 +244,11 @@
     chips = lax.axis_size(CHIPS)
     half = chips * BLOCK
     start = jnp.zeros((1, 1), jnp.int32)
-    rows, most = picked(lengths, start, hidden)
+    rows, most = picked(lengths, (), hidden)
 
     def again(state):
         first, more = state
-        found = spread(picked(lengths, first, hidden)[0], gain)
+        found = spread(picked(lengths, (first,), hidden)[0], gain)
         more = pl.pallas_call(
             order_kernel,
             out_shape=shape(more.shape, more.dtype),
@@ -232,29 +266,24 @@
     )
     rows, weight, more = lax.optimization_barrier((rows, weight, more))
     found = spread(rows, gain)
-    send = pl.pallas_call(
-        split_kernel,
-        out_shape=pltpu.VMEM((half, depth), weight.dtype),
-        in_specs=[ANY],
-        out_specs=VMEM,
-        scratch_shapes=[pltpu.SemaphoreType.DMA(())],
-        cost_estimate=pl.CostEstimate(flops=10**9, bytes_accessed=4 * MIB, transcendentals=0),
-        compiler_params=limit(8),
-        name="split",
-    )(pltpu.with_memory_space_constraint(weight, pltpu.HBM))
-    other = lax.ppermute(send, "c", [(0, 1), (1, 0)])
+    other = lax.ppermute(weight, "c", [(0, 1), (1, 0)])
+    keep = own_half(weight, half)
     parts = pl.pallas_call(
         head_kernel,
         out_shape=shape((chips, n, BLOCK), jnp.float32),
-        in_specs=[VMEM, SMEM, VMEM, VMEM, VMEM, VMEM],
-        out_specs=VMEM,
+        in_specs=[VMEM] * 4 + [HBM],
+        out_specs=VMEM,
+        scratch_shapes=[
+            pltpu.VMEM((PIECES, half // PIECES, depth), weight.dtype),
+            pltpu.SemaphoreType.DMA((PIECES,)),
+        ],
         compiler_params=limit(16),
         name="head",
-    )(lengths, start, found, more, weight, other)
+    )(lengths, found, more, keep, in_hbm(other))
     logits = jnp.sum(exchange(parts.astype(jnp.float16), CHIPS).astype(jnp.float32), axis=0)
     line = pl.pallas_call(
         functools.partial(stats_kernel, vocab - half, vocab),
-        out_shape=shape((lax.axis_size(ALL), 1, 2 * n), jnp.float32),
+        out_shape=shape((lax.axis_size(ALL), 2 * n), jnp.float32),
         in_specs=[VMEM, VMEM],
         out_specs=VMEM,
         compiler_params=limit(4),

time: 79.1 us -> 81 us (1.024)
  blocking collectives: 67.9 us -> 51.8 us
  starting transfers between devices: 3.29 us -> 11.9 us
  waiting for transfers between devices: 0.01 us -> 6.05 us
  Pallas kernels: 6.52 us -> 9.69 us
    all_to_all x4 -> x3, blocking collectives: 67.9 us -> 51.8 us  [exchange(): return lax.all_to_all(x, axes, split_axis=0, concat_axis=0, tiled=True)]
    all_to_all x0 -> x1, starting transfers between devices: none -> 8.63 us  [exchange(): return lax.all_to_all(x, axes, split_axis=0, concat_axis=0, tiled=True)]
    all_to_all x0 -> x1, waiting for transfers between devices: none -> 6.04 us  [exchange(): return lax.all_to_all(x, axes, split_axis=0, concat_axis=0, tiled=True)]
    pallas_call x1, Pallas kernels: 1.66 us -> 3.42 us  [local(): pl.pallas_call(head_kernel, out_shape=shape((chips, n, BLOCK), jnp.float3...]
    pallas_call x1, Pallas kernels: 0.12 us -> 1.48 us  [spread(): pl.pallas_call(norm_kernel, out_shape=shape((chips, cores, SLOTS, width),...]
  transfers between devices with their start and end apart: 1 -> 2, of which waited for: 0 -> 1; matrix products, arithmetic and copies ran while one was open for 0% -> 0% of each run, Pallas kernels for 0% -> 4%
where the time goes in v4:
time: 81 us; the launch traced here: 80.6 us
  blocking collectives  51.8 us (64%)
  starting transfers between devices  11.9 us (15%)
  Pallas kernels  9.69 us (12%)
  waiting for transfers between devices  6.05 us (7%)
    all_to_all x3, blocking collectives, exchange(): return lax.all_to_all(x, axes, split_axis=0, concat_axis=0, tiled=True)  51.8 us
    all_to_all x1, starting transfers between devices, exchange(): return lax.all_to_all(x, axes, split_axis=0, concat_axis=0, tiled=True)  8.63 us
    all_to_all x1, waiting for transfers between devices, exchange(): return lax.all_to_all(x, axes, split_axis=0, concat_axis=0, tiled=True)  6.04 us
    pallas_call x1, Pallas kernels, local(): pl.pallas_call(head_kernel, out_shape=shape((chips, n, BLOCK), jnp.float3...  3.42 us
    ppermute x1, starting transfers between devices, local(): other = lax.ppermute(weight, 'c', [(0, 1), (1, 0)])  3.29 us
    pallas_call x1, Pallas kernels, picked(): pl.pallas_call(pick_kernel, out_shape=(shape((lax.axis_size('z'), SLOTS,...  2.24 us
  transfers between devices with their start and end apart: 2, of which 1 were waited for; matrix products, arithmetic and copies ran while one was open for 0% of the time, Pallas kernels for 4%

profile of v4, /device:TPU:1, one launch (start us, length us, event | category | flops | bytes accessed | tf_op | source)
XLA Modules:
  0.0 80.6 jit_solution(10943706531940377757)
XLA Ops:
  0.0 2.2 %pick.2 = (bf16[8,8,512]{2,1,0:T(8,128)(2,1)S(1)}, s32[1,1]{1,0:T(1,128)}) custom-call(s32[1,64]{1,0:T(1,128)} %bitcast.25, bf16[512,512]{1,0:T(8,128)(2,1)} %refs_0_.1), custom_call_target="tpu_custom_call" | custom-call | tf_op jit(solution)/shard_map/pick/pallas_call | solution.py:210
  2.3 0.6 while.10
  2.9 3.3 %collective-permute-start = (bf16[16032,128]{1,0:T(8,128)(2,1)}, bf16[16032,128]{1,0:T(8,128)(2,1)}, u32[]{:S(2)}, u32[]{:S(2)}) collective-permute-start(bf16[16032,128]{1,0:T(8,128)(2,1)} %bitcast.22), channel_id=1, source_target_pairs={{0,8},{8,0},{1,9},{9,1},{2,10},{10,2},{3,11},{11,3},{4,12},{12,4},... | collective-permute-start | bytes 12312584 | tf_op jit(solution)/shard_map/ppermute | solution.py:269
  6.2 13.4 %all_to_all.46.rows_ref = bf16[8,8,512]{2,1,0:T(8,128)(2,1)S(1)} all-to-all(bf16[8,8,512]{2,1,0:T(8,128)(2,1)S(1)} %get-tuple-element.47), channel_id=1, replica_groups=mesh['x'=4,'y'=4,'c'=2,'z'=8] {'z'}, dimensions={0} | all-to-all | bytes 131072 | tf_op jit(solution)/shard_map/all_to_all | solution.py:194
  19.6 1.5 %norm.2 = bf16[16,2,8,256]{3,2,1,0:T(8,128)(2,1)} custom-call(bf16[8,8,512]{2,1,0:T(8,128)(2,1)S(1)} %all_to_all.46.rows_ref, f32[1,4096]{1,0:T(1,128)} %get-tuple-element.119), custom_call_target="tpu_custom_call" | custom-call | tf_op jit(solution)/shard_map/norm/pallas_call | solution.py:228
  21.1 8.6 %all-to-all-start.3 = ((bf16[32,8,256]{2,1,0:T(8,128)(2,1)}), bf16[32,8,256]{2,1,0:T(8,128)(2,1)S(1)}, u32[]{:S(2)}, u32[]{:S(2)}) async-start(bf16[32,8,256]{2,1,0:T(8,128)(2,1)} %bitcast.6), calls=%async_computation.3 | async-start | bytes 262144 | tf_op jit(solution)/shard_map/all_to_all | solution.py:194
  29.7 0.0 copy-start.1
  29.7 1.6 %half.1.keep_ref = bf16[8192,128]{1,0:T(8,128)(2,1)S(1)} custom-call(bf16[16032,128]{1,0:T(8,128)(2,1)} %bitcast.23), custom_call_target="tpu_custom_call" | custom-call | tf_op jit(solution)/shard_map/half/pallas_call | solution.py:198
  31.3 6.0 %all-to-all-done.3 = bf16[32,8,256]{2,1,0:T(8,128)(2,1)S(1)} async-done(((bf16[32,8,256]{2,1,0:T(8,128)(2,1)}), bf16[32,8,256]{2,1,0:T(8,128)(2,1)S(1)}, u32[]{:S(2)}, u32[]{:S(2)}) %all-to-all-start.3) | async-done | bytes 131104 | tf_op jit(solution)/shard_map/all_to_all | solution.py:194
  37.4 0.0 collective-permute-done.other_ref
  37.4 0.0 copy-done.1
  37.4 3.4 %head.1 = f32[16,64,512]{2,1,0:T(8,128)S(1)} custom-call(s32[1,64]{1,0:T(1,128)S(1)} %copy-done.1, bf16[256,256]{1,0:T(8,128)(2,1)S(1)} %bitcast.18, bf16[64,256]{1,0:T(8,128)(2,1)S(1)} %get-tuple-element.48.more_ref, bf16[8192,128]{1,0:T(8,128)(2,1)S(1)} %half.1.keep_ref, bf16[16032,128]{1,0:T(8,128)(2,1)} %collective-permute-done.other_ref), custom_call_target="tpu_custom_call" | custom-call | tf_op jit(solution)/shard_map/head/pallas_call | solution.py:271
  40.8 0.3 convert_element_type.6
  41.1 0.0 copy-start
  41.1 18.6 %all_to_all.47 = f16[16,64,512]{2,1,0:T(8,128)(2,1)S(1)} all-to-all(f16[16,64,512]{2,1,0:T(8,128)(2,1)S(1)} %convert_element_type.6), channel_id=1, replica_groups=mesh['x'=4,'y'=4,'c'=2,'z'=8] {'x','y'}, dimensions={0} | all-to-all | bytes 2097152 | tf_op jit(solution)/shard_map/all_to_all | solution.py:194
  59.7 0.1 convert_reduce_fusion.logits_ref
  59.9 0.0 copy-done
  59.9 0.2 stats.1
  60.1 19.8 %all_to_all.48 = f32[256,1,128]{2,1,0:T(1,128)S(1)} all-to-all(f32[256,1,128]{2,1,0:T(1,128)S(1)} %bitcast.19), channel_id=1, replica_groups=mesh['x'=4,'y'=4,'c'=2,'z'=8] {'x','y','c','z'}, dimensions={0} | all-to-all | bytes 262144 | tf_op jit(solution)/shard_map/all_to_all | solution.py:194
  79.9 0.7 join.1
  (1 shorter events, 0.0 us)
Async XLA Ops:
  2.9 34.5 %collective-permute-start = (bf16[16032,128]{1,0:T(8,128)(2,1)}, bf16[16032,128]{1,0:T(8,128)(2,1)}, u32[]{:S(2)}, u32[]{:S(2)}) collective-permute-start(bf16[16032,128]{1,0:T(8,128)(2,1)} %bitcast.22), channel_id=1, source_target_pairs={{0,8},{8,0},{1,9},{9,1},{2,10},{10,2},{3,11},{11,3},{4,12},{12,4},... | collective-permute-start | bytes 12312584 | tf_op jit(solution)/shard_map/ppermute | solution.py:269
  21.1 16.3 %all-to-all-start.3 = ((bf16[32,8,256]{2,1,0:T(8,128)(2,1)}), bf16[32,8,256]{2,1,0:T(8,128)(2,1)S(1)}, u32[]{:S(2)}, u32[]{:S(2)}) async-start(bf16[32,8,256]{2,1,0:T(8,128)(2,1)} %bitcast.6), calls=%async_computation.3 | async-start | bytes 262144 | tf_op jit(solution)/shard_map/all_to_all | solution.py:194
  29.7 7.7 %copy-start.1 = (s32[1,64]{1,0:T(1,128)S(1)}, s32[1,64]{1,0:T(1,128)}, u32[]{:S(2)}) copy-start(s32[1,64]{1,0:T(1,128)} %get-tuple-element.120) | copy-start | bytes 772
  41.1 18.8 %copy-start = (s32[64]{0:T(128)S(1)}, s32[64]{0:T(128)}, u32[]{:S(2)}) copy-start(s32[64]{0:T(128)} %param.9) | copy-start | bytes 772

commit v5 on v4

--- a/solution.py
+++ b/solution.py
@@ -8,18 +8,17 @@
 from jax.sharding import Mesh
 from jax.sharding import PartitionSpec as P
 
-
 CHIPS = ("x", "y")
 CP = ("x", "y", "c")
 ALL = ("x", "y", "c", "z")
 SLOTS = 8
 BLOCK = 512
-PIECES = 8
+PIECES = 4
 NEG = -1e30
 
 VMEM = pl.BlockSpec(memory_space=pltpu.VMEM)
+HBM = pl.BlockSpec(memory_space=pltpu.HBM)
 SMEM = pl.BlockSpec(memory_space=pltpu.SMEM)
-HBM = pl.BlockSpec(memory_space=pltpu.HBM)
 MIB = 1 << 20
 
 
@@ -55,10 +54,8 @@
 
 
 def pick_kernel(lengths_ref, *refs):
-    *first_ref, hidden_ref, out_ref, most_ref, held, sem = refs
-    rows = pltpu.make_async_copy(hidden_ref, held, sem)
-    rows.start()
-    n, rows_here = lengths_ref.shape[1], held.shape[0]
+    *first_ref, hidden_ref, out_ref, most_ref = refs
+    n, rows_here = lengths_ref.shape[1], hidden_ref.shape[0]
     ends, _ = ends_of(lengths_ref)
     base = (place() * rows_here).astype(jnp.float32)
     owned = (ends >= base) & (ends < base + rows_here)
@@ -71,8 +68,7 @@
     selector = (at == iota((SLOTS, rows_here), 1)).astype(jnp.bfloat16)
     counts = total(jnp.where(jnp.floor(ends / rows_here) == iota((32, n), 0), 1.0, 0.0), 1)
     most_ref[0, 0] = jnp.max(counts).astype(jnp.int32)
-    rows.wait()
-    picked = jnp.dot(selector, held[...], preferred_element_type=jnp.float32)
+    picked = jnp.dot(selector, hidden_ref[...], preferred_element_type=jnp.float32)
     picked = picked.astype(jnp.bfloat16)
     for peer in range(out_ref.shape[0]):
         out_ref[peer] = picked
@@ -109,48 +105,44 @@
     return jnp.dot(selector, found_ref[...], preferred_element_type=jnp.float32)
 
 
-def order_kernel(lengths_ref, first_ref, found_ref, more_ref, out_ref):
+def order_kernel(lengths_ref, first_ref, found_ref, more_ref, next_ref, out_ref):
+    next_ref[0, 0] = first_ref[0, 0] + SLOTS
     first = first_ref[0, 0].astype(jnp.float32)
     rows = rows_in_order(lengths_ref, found_ref, first)
     out_ref[...] = more_ref[...] + rows.astype(jnp.bfloat16)
 
 
-def half_kernel(weight_ref, keep_ref, sem):
-    half = keep_ref.shape[0]
-    start = lax.axis_index("c") * (weight_ref.shape[0] - half)
-    copy = pltpu.make_async_copy(
-        weight_ref.at[pl.ds(pl.multiple_of(start, 16), half)], keep_ref, sem
-    )
-    copy.start()
-    copy.wait()
-
-
-def head_kernel(lengths_ref, found_ref, more_ref, keep_ref, other_ref, out_ref, held, sems):
-    half, width = keep_ref.shape
+def head_kernel(lengths_ref, found_ref, more_ref, weight_ref, other_ref, out_ref, own, sems):
+    width = weight_ref.shape[1]
+    blocks = out_ref.shape[0]
+    pieces, piece, _ = own.shape
+    start = lax.axis_index("c") * (weight_ref.shape[0] - blocks * BLOCK)
     first = lax.axis_index("c") == 0
-    start = lax.axis_index("c") * (other_ref.shape[0] - half)
-    piece = half // PIECES
-    copies = []
-    for k in range(PIECES):
-        rows = pl.ds(pl.multiple_of(start + k * piece, 16), piece)
-        copy = pltpu.make_async_copy(other_ref.at[rows], held.at[k], sems.at[k])
+
+    def span(at, count):
+        return pl.ds(pl.multiple_of(start + at, 16), count)
+
+    def product(left, right):
+        return lax.dot_general(
+            left, right, (((1,), (1,)), ((), ())), preferred_element_type=jnp.float32
+        )
+
+    copies = [
+        pltpu.make_async_copy(weight_ref.at[span(k * piece, piece)], own.at[k], sems.at[k])
+        for k in range(pieces)
+    ]
+    for copy in copies:
         copy.start()
-        copies.append(copy)
     rows = rows_in_order(lengths_ref, found_ref).astype(jnp.bfloat16) + more_ref[...]
     low, high = rows[:, :width], rows[:, width:]
-    left = jnp.concatenate([jnp.where(first, low, high), jnp.where(first, high, low)], axis=1)
-    for block in range(out_ref.shape[0]):
-        at = block * BLOCK
-        k, inside = divmod(at, piece)
-        if inside == 0:
+    here, there = jnp.where(first, low, high), jnp.where(first, high, low)
+    for block in range(blocks):
+        out_ref[block] = product(there, other_ref[span(block * BLOCK, BLOCK), :])
+    for block in range(blocks):
+        k, at = divmod(block * BLOCK, piece)
+        if at == 0:
             copies[k].wait()
-        weight = jnp.concatenate(
-            [keep_ref[at : at + BLOCK, :], held[k, inside : inside + BLOCK, :]], axis=1
-        )
-        part = lax.dot_general(
-            left, weight, (((1,), (1,)), ((), ())), preferred_element_type=jnp.float32
-        )
-        out_ref[block] = part.astype(out_ref.dtype)
+        out_ref[block] += product(here, own[k, at : at + BLOCK, :])
 
 
 def stats_kernel(spare, vocab, logits_ref, targets_ref, out_ref):
@@ -194,18 +186,6 @@
     return lax.all_to_all(x, axes, split_axis=0, concat_axis=0, tiled=True)
 
 
-def own_half(weight, half):
-    return pl.pallas_call(
-        half_kernel,
-        out_shape=shape((half, weight.shape[1]), weight.dtype),
-        in_specs=[HBM],
-        out_specs=VMEM,
-        scratch_shapes=[pltpu.SemaphoreType.DMA(())],
-        compiler_params=limit(8),
-        name="half",
-    )(in_hbm(weight))
-
-
 def picked(lengths, first, hidden):
     return pl.pallas_call(
         pick_kernel,
@@ -213,18 +193,17 @@
             shape((lax.axis_size("z"), SLOTS, hidden.shape[1]), hidden.dtype),
             shape((1, 1), jnp.int32),
         ),
-        in_specs=[VMEM] + [SMEM] * len(first) + [HBM],
+        in_specs=[VMEM] + [SMEM] * len(first) + [VMEM],
         out_specs=(VMEM, SMEM),
-        scratch_shapes=[pltpu.VMEM(hidden.shape, hidden.dtype), pltpu.SemaphoreType.DMA(())],
         compiler_params=limit(4),
         name="pick",
-    )(lengths, *first, in_hbm(hidden))
-
-
-def spread(rows, gain):
+    )(lengths, *first, hidden)
+
+
+def spread(rows, gain, after=()):
     chips, cores = lax.axis_size(CHIPS), lax.axis_size("c")
     width = gain.shape[1] // chips
-    rows = exchange(rows, "z")
+    rows, after = lax.optimization_barrier((exchange(rows, "z"), after))
     normed = pl.pallas_call(
         norm_kernel,
         out_shape=shape((chips, cores, SLOTS, width), jnp.bfloat16),
@@ -233,7 +212,7 @@
         compiler_params=limit(4),
         name="norm",
     )(rows, gain)
-    return exchange(normed.reshape(chips * cores * SLOTS, width), CP)
+    return exchange(normed.reshape(chips * cores * SLOTS, width), CP), after
 
 
 def local(hidden, lengths, targets, norm_gain, lm_weight):
@@ -245,33 +224,32 @@
     half = chips * BLOCK
     start = jnp.zeros((1, 1), jnp.int32)
     rows, most = picked(lengths, (), hidden)
+    other = lax.ppermute(weight, "c", [(0, 1), (1, 0)])
 
     def again(state):
         first, more = state
-        found = spread(picked(lengths, (first,), hidden)[0], gain)
-        more = pl.pallas_call(
+        found = spread(picked(lengths, (first,), hidden)[0], gain)[0]
+        return pl.pallas_call(
             order_kernel,
-            out_shape=shape(more.shape, more.dtype),
+            out_shape=(shape(first.shape, first.dtype), shape(more.shape, more.dtype)),
             in_specs=[VMEM, SMEM, VMEM, VMEM],
-            out_specs=VMEM,
+            out_specs=(SMEM, VMEM),
+            input_output_aliases={1: 0, 3: 1},
             compiler_params=limit(4),
             name="order",
         )(lengths, first, found, more)
-        return first + SLOTS, more
 
     _, more = lax.while_loop(
         lambda state: state[0][0, 0] < most[0, 0],
         again,
         (start + SLOTS, jnp.zeros((n, gain.shape[1] // chips), jnp.bfloat16)),
     )
-    rows, weight, more = lax.optimization_barrier((rows, weight, more))
-    found = spread(rows, gain)
-    other = lax.ppermute(weight, "c", [(0, 1), (1, 0)])
-    keep = own_half(weight, half)
+    rows, more = lax.optimization_barrier((rows, more))
+    found, other = spread(rows, gain, other)
     parts = pl.pallas_call(
         head_kernel,
         out_shape=shape((chips, n, BLOCK), jnp.float32),
-        in_specs=[VMEM] * 4 + [HBM],
+        in_specs=[VMEM] * 3 + [HBM, VMEM],
         out_specs=VMEM,
         scratch_shapes=[
             pltpu.VMEM((PIECES, half // PIECES, depth), weight.dtype),
@@ -279,7 +257,7 @@
         ],
         compiler_params=limit(16),
         name="head",
-    )(lengths, found, more, keep, in_hbm(other))
+    )(lengths, found, more, in_hbm(weight), other)
     logits = jnp.sum(exchange(parts.astype(jnp.float16), CHIPS).astype(jnp.float32), axis=0)
     line = pl.pallas_call(
         functools.partial(stats_kernel, vocab - half, vocab),

time: 81 us -> 79.9 us (0.986)
  blocking collectives: 51.8 us -> 67.9 us
  starting transfers between devices: 11.9 us -> 3.2 us
  waiting for transfers between devices: 6.05 us -> 0.01 us
  Pallas kernels: 9.69 us -> 7.36 us
    all_to_all x3 -> x4, blocking collectives: 51.8 us -> 67.9 us  [exchange(): return lax.all_to_all(x, axes, split_axis=0, concat_axis=0, tiled=True)]
    all_to_all x1 -> x0, starting transfers between devices: 8.63 us -> none  [exchange(): return lax.all_to_all(x, axes, split_axis=0, concat_axis=0, tiled=True)]
    all_to_all x1 -> x0, waiting for transfers between devices: 6.04 us -> none  [exchange(): return lax.all_to_all(x, axes, split_axis=0, concat_axis=0, tiled=True)]
    pallas_call x1 -> x0, Pallas kernels: 1.61 us -> none  [own_half(): pl.pallas_call(half_kernel, out_shape=shape((half, weight.shape[1]), weig...]
  transfers between devices with their start and end apart: 2 -> 1, of which waited for: 1 -> 0; matrix products, arithmetic and copies ran while one was open for 0% -> 0% of each run, Pallas kernels for 4% -> 2%
where the time goes in v5:
time: 79.9 us; the launch traced here: 79.6 us
  blocking collectives  67.9 us (85%)
  Pallas kernels  7.36 us (9%)
  starting transfers between devices  3.2 us (4%)
    all_to_all x4, blocking collectives, exchange(): return lax.all_to_all(x, axes, split_axis=0, concat_axis=0, tiled=True)  67.9 us
    pallas_call x1, Pallas kernels, local(): pl.pallas_call(head_kernel, out_shape=shape((chips, n, BLOCK), jnp.float3...  3.71 us
    ppermute x1, starting transfers between devices, local(): other = lax.ppermute(weight, 'c', [(0, 1), (1, 0)])  3.2 us
    pallas_call x1, Pallas kernels, picked(): pl.pallas_call(pick_kernel, out_shape=(shape((lax.axis_size('z'), SLOTS,...  1.87 us
  transfers between devices with their start and end apart: 1, of which 0 were waited for; matrix products, arithmetic and copies ran while one was open for 0% of the time, Pallas kernels for 2%

profile of v5, /device:TPU:1, one launch (start us, length us, event | category | flops | bytes accessed | tf_op | source)
XLA Modules:
  0.0 79.6 jit_solution(4744783214388870065)
XLA Ops:
  0.0 3.2 %collective-permute-start = (bf16[16032,128]{1,0:T(8,128)(2,1)}, bf16[16032,128]{1,0:T(8,128)(2,1)S(1)}, u32[]{:S(2)}, u32[]{:S(2)}) collective-permute-start(bf16[16032,128]{1,0:T(8,128)(2,1)} %bitcast.21), channel_id=1, source_target_pairs={{0,8},{8,0},{1,9},{9,1},{2,10},{10,2},{3,11},{11,3},{4,12},{12,4},... | collective-permute-start | bytes 12312584 | tf_op jit(solution)/shard_map/ppermute | solution.py:227
  3.2 1.9 %pick.3 = (bf16[8,8,512]{2,1,0:T(8,128)(2,1)S(1)}, s32[1,1]{1,0:T(1,128)}) custom-call(s32[1,64]{1,0:T(1,128)} %bitcast.24, bf16[512,512]{1,0:T(8,128)(2,1)} %refs_0_.1), custom_call_target="tpu_custom_call" | custom-call | tf_op jit(solution)/shard_map/pick/pallas_call | solution.py:190
  5.1 0.6 while.9
  5.7 13.4 %all_to_all.45.rows_ref = bf16[8,8,512]{2,1,0:T(8,128)(2,1)S(1)} all-to-all(bf16[8,8,512]{2,1,0:T(8,128)(2,1)S(1)} %get-tuple-element.50), channel_id=1, replica_groups=mesh['x'=4,'y'=4,'c'=2,'z'=8] {'z'}, dimensions={0} | all-to-all | bytes 131072 | tf_op jit(solution)/shard_map/all_to_all | solution.py:186
  19.1 0.0 collective-permute-done.other_ref
  19.1 0.8 %norm.3 = bf16[16,2,8,256]{3,2,1,0:T(8,128)(2,1)S(1)} custom-call(bf16[8,8,512]{2,1,0:T(8,128)(2,1)S(1)} %all_to_all.45.rows_ref, f32[1,4096]{1,0:T(1,128)} %get-tuple-element.92), custom_call_target="tpu_custom_call" | custom-call | tf_op jit(solution)/shard_map/norm/pallas_call | solution.py:207
  20.0 16.1 %all_to_all.46 = bf16[32,8,256]{2,1,0:T(8,128)(2,1)S(1)} all-to-all(bf16[32,8,256]{2,1,0:T(8,128)(2,1)S(1)} %bitcast.17), channel_id=1, replica_groups=mesh['x'=4,'y'=4,'c'=2,'z'=8] {'x','y','c'}, dimensions={0} | all-to-all | bytes 262144 | tf_op jit(solution)/shard_map/all_to_all | solution.py:186
  36.1 3.7 %head.1 = f32[16,64,512]{2,1,0:T(8,128)S(1)} custom-call(s32[1,64]{1,0:T(1,128)} %get-tuple-element.93, bf16[256,256]{1,0:T(8,128)(2,1)S(1)} %bitcast.16, bf16[64,256]{1,0:T(8,128)(2,1)S(1)} %get-tuple-element.52.more_ref, bf16[16032,128]{1,0:T(8,128)(2,1)} %bitcast.22, bf16[16032,128]{1,0:T(8,128)(2,1)S(1)} %collective-permute-done.other_ref), custom_call_target="tpu_custom_call" | custom-call | tf_op jit(solution)/shard_map/head/pallas_call | solution.py:249
  39.8 0.0 copy-start
  39.8 0.3 convert_element_type.6
  40.1 18.6 %all_to_all.47 = f16[16,64,512]{2,1,0:T(8,128)(2,1)S(1)} all-to-all(f16[16,64,512]{2,1,0:T(8,128)(2,1)S(1)} %convert_element_type.6), channel_id=1, replica_groups=mesh['x'=4,'y'=4,'c'=2,'z'=8] {'x','y'}, dimensions={0} | all-to-all | bytes 2097152 | tf_op jit(solution)/shard_map/all_to_all | solution.py:186
  58.7 0.1 convert_reduce_fusion.logits_ref
  58.9 0.0 copy-done
  58.9 0.2 stats.1
  59.1 19.8 %all_to_all.48 = f32[256,1,128]{2,1,0:T(1,128)S(1)} all-to-all(f32[256,1,128]{2,1,0:T(1,128)S(1)} %bitcast.18), channel_id=1, replica_groups=mesh['x'=4,'y'=4,'c'=2,'z'=8] {'x','y','c','z'}, dimensions={0} | all-to-all | bytes 262144 | tf_op jit(solution)/shard_map/all_to_all | solution.py:186
  78.9 0.7 join.1
  (1 shorter events, 0.0 us)
Async XLA Ops:
  0.0 19.1 %collective-permute-start = (bf16[16032,128]{1,0:T(8,128)(2,1)}, bf16[16032,128]{1,0:T(8,128)(2,1)S(1)}, u32[]{:S(2)}, u32[]{:S(2)}) collective-permute-start(bf16[16032,128]{1,0:T(8,128)(2,1)} %bitcast.21), channel_id=1, source_target_pairs={{0,8},{8,0},{1,9},{9,1},{2,10},{10,2},{3,11},{11,3},{4,12},{12,4},... | collective-permute-start | bytes 12312584 | tf_op jit(solution)/shard_map/ppermute | solution.py:227
  39.8 19.1 %copy-start = (s32[64]{0:T(128)S(1)}, s32[64]{0:T(128)}, u32[]{:S(2)}) copy-start(s32[64]{0:T(128)} %param.9) | copy-start | bytes 772

commit v6 on v5

--- a/solution.py
+++ b/solution.py
@@ -13,11 +13,9 @@
 ALL = ("x", "y", "c", "z")
 SLOTS = 8
 BLOCK = 512
-PIECES = 4
 NEG = -1e30
 
 VMEM = pl.BlockSpec(memory_space=pltpu.VMEM)
-HBM = pl.BlockSpec(memory_space=pltpu.HBM)
 SMEM = pl.BlockSpec(memory_space=pltpu.SMEM)
 MIB = 1 << 20
 
@@ -112,37 +110,21 @@
     out_ref[...] = more_ref[...] + rows.astype(jnp.bfloat16)
 
 
-def head_kernel(lengths_ref, found_ref, more_ref, weight_ref, other_ref, out_ref, own, sems):
+def head_kernel(lengths_ref, found_ref, more_ref, weight_ref, other_ref, out_ref):
     width = weight_ref.shape[1]
     blocks = out_ref.shape[0]
-    pieces, piece, _ = own.shape
     start = lax.axis_index("c") * (weight_ref.shape[0] - blocks * BLOCK)
     first = lax.axis_index("c") == 0
-
-    def span(at, count):
-        return pl.ds(pl.multiple_of(start + at, 16), count)
-
-    def product(left, right):
-        return lax.dot_general(
-            left, right, (((1,), (1,)), ((), ())), preferred_element_type=jnp.float32
-        )
-
-    copies = [
-        pltpu.make_async_copy(weight_ref.at[span(k * piece, piece)], own.at[k], sems.at[k])
-        for k in range(pieces)
-    ]
-    for copy in copies:
-        copy.start()
     rows = rows_in_order(lengths_ref, found_ref).astype(jnp.bfloat16) + more_ref[...]
     low, high = rows[:, :width], rows[:, width:]
-    here, there = jnp.where(first, low, high), jnp.where(first, high, low)
+    left = jnp.concatenate([jnp.where(first, low, high), jnp.where(first, high, low)], axis=1)
     for block in range(blocks):
-        out_ref[block] = product(there, other_ref[span(block * BLOCK, BLOCK), :])
-    for block in range(blocks):
-        k, at = divmod(block * BLOCK, piece)
-        if at == 0:
-            copies[k].wait()
-        out_ref[block] += product(here, own[k, at : at + BLOCK, :])
+        span = pl.ds(pl.multiple_of(start + block * BLOCK, 16), BLOCK)
+        weight = jnp.concatenate([weight_ref[span, :], other_ref[span, :]], axis=1)
+        part = lax.dot_general(
+            left, weight, (((1,), (1,)), ((), ())), preferred_element_type=jnp.float32
+        )
+        out_ref[block] = part.astype(out_ref.dtype)
 
 
 def stats_kernel(spare, vocab, logits_ref, targets_ref, out_ref):
@@ -178,10 +160,6 @@
     return jax.ShapeDtypeStruct(dims, dtype)
 
 
-def in_hbm(x):
-    return pltpu.with_memory_space_constraint(x, pltpu.HBM)
-
-
 def exchange(x, axes):
     return lax.all_to_all(x, axes, split_axis=0, concat_axis=0, tiled=True)
 
@@ -244,20 +222,17 @@
         again,
         (start + SLOTS, jnp.zeros((n, gain.shape[1] // chips), jnp.bfloat16)),
     )
-    rows, more = lax.optimization_barrier((rows, more))
-    found, other = spread(rows, gain, other)
+    rows, more, weight = lax.optimization_barrier((rows, more, weight))
+    own = lax.ppermute(weight, "c", [(0, 0), (1, 1)])
+    found, (own, other) = spread(rows, gain, (own, other))
     parts = pl.pallas_call(
         head_kernel,
         out_shape=shape((chips, n, BLOCK), jnp.float32),
-        in_specs=[VMEM] * 3 + [HBM, VMEM],
-        out_specs=VMEM,
-        scratch_shapes=[
-            pltpu.VMEM((PIECES, half // PIECES, depth), weight.dtype),
-            pltpu.SemaphoreType.DMA((PIECES,)),
-        ],
+        in_specs=[VMEM] * 5,
+        out_specs=VMEM,
         compiler_params=limit(16),
         name="head",
-    )(lengths, found, more, in_hbm(weight), other)
+    )(lengths, found, more, own, other)
     logits = jnp.sum(exchange(parts.astype(jnp.float16), CHIPS).astype(jnp.float32), axis=0)
     line = pl.pallas_call(
         functools.partial(stats_kernel, vocab - half, vocab),

time: 79.9 us -> 80.7 us (1.010)
  starting transfers between devices: 3.2 us -> 5.37 us
  Pallas kernels: 7.36 us -> 5.95 us
    ppermute x0 -> x1, starting transfers between devices: none -> 2.17 us  [local(): own = lax.ppermute(weight, 'c', [(0, 0), (1, 1)])]
    pallas_call x1, Pallas kernels: 3.71 us -> 2.3 us  [local(): pl.pallas_call(head_kernel, out_shape=shape((chips, n, BLOCK), jnp.float3...]
  transfers between devices with their start and end apart: 1 -> 2, of which waited for: 0 -> 0; matrix products, arithmetic and copies ran while one was open for 0% -> 0% of each run, Pallas kernels for 2% -> 0%
where the time goes in v6:
time: 80.7 us; the launch traced here: 80.3 us
  blocking collectives  67.9 us (84%)
  Pallas kernels  5.95 us (7%)
  starting transfers between devices  5.37 us (7%)
    all_to_all x4, blocking collectives, exchange(): return lax.all_to_all(x, axes, split_axis=0, concat_axis=0, tiled=True)  67.9 us
    ppermute x1, starting transfers between devices, local(): other = lax.ppermute(weight, 'c', [(0, 1), (1, 0)])  3.2 us
    pallas_call x1, Pallas kernels, local(): pl.pallas_call(head_kernel, out_shape=shape((chips, n, BLOCK), jnp.float3...  2.3 us
    ppermute x1, starting transfers between devices, local(): own = lax.ppermute(weight, 'c', [(0, 0), (1, 1)])  2.17 us
    pallas_call x1, Pallas kernels, picked(): pl.pallas_call(pick_kernel, out_shape=(shape((lax.axis_size('z'), SLOTS,...  1.87 us
  transfers between devices with their start and end apart: 2, of which 0 were waited for; matrix products, arithmetic and copies ran while one was open for 0% of the time, Pallas kernels for 0%

profile of v6, /device:TPU:1, one launch (start us, length us, event | category | flops | bytes accessed | tf_op | source)
XLA Modules:
  0.0 80.3 jit_solution(15878235020795989937)
XLA Ops:
  0.0 1.9 %pick.3 = (bf16[8,8,512]{2,1,0:T(8,128)(2,1)S(1)}, s32[1,1]{1,0:T(1,128)}) custom-call(s32[1,64]{1,0:T(1,128)} %bitcast.22, bf16[512,512]{1,0:T(8,128)(2,1)} %refs_0_.1), custom_call_target="tpu_custom_call" | custom-call | tf_op jit(solution)/shard_map/pick/pallas_call | solution.py:168
  1.9 0.6 while.9
  2.5 2.2 %collective-permute-start = (bf16[16032,128]{1,0:T(8,128)(2,1)}, bf16[16032,128]{1,0:T(8,128)(2,1)S(1)}, u32[]{:S(2)}, u32[]{:S(2)}) collective-permute-start(bf16[16032,128]{1,0:T(8,128)(2,1)} %bitcast.24), channel_id=1, source_target_pairs={{0,0},{8,8},{1,1},{9,9},{2,2},{10,10},{3,3},{11,11},{4,4},{12,12},... | collective-permute-start | bytes 12312584 | tf_op jit(solution)/shard_map/ppermute | solution.py:226
  4.7 3.2 %collective-permute-start.1 = (bf16[16032,128]{1,0:T(8,128)(2,1)}, bf16[16032,128]{1,0:T(8,128)(2,1)S(1)}, u32[]{:S(2)}, u32[]{:S(2)}) collective-permute-start(bf16[16032,128]{1,0:T(8,128)(2,1)} %bitcast.25), channel_id=1, source_target_pairs={{0,8},{8,0},{1,9},{9,1},{2,10},{10,2},{3,11},{11,3},{4,12},{12,4},... | collective-permute-start | bytes 12312584 | tf_op jit(solution)/shard_map/ppermute | solution.py:205
  7.9 13.4 %all_to_all.45.rows_ref = bf16[8,8,512]{2,1,0:T(8,128)(2,1)S(1)} all-to-all(bf16[8,8,512]{2,1,0:T(8,128)(2,1)S(1)} %get-tuple-element.52), channel_id=1, replica_groups=mesh['x'=4,'y'=4,'c'=2,'z'=8] {'z'}, dimensions={0} | all-to-all | bytes 131072 | tf_op jit(solution)/shard_map/all_to_all | solution.py:164
  21.3 0.0 collective-permute-done.weight_ref
  21.3 0.0 collective-permute-done.1.other_ref
  21.3 0.8 %norm.3 = bf16[16,2,8,256]{3,2,1,0:T(8,128)(2,1)S(1)} custom-call(bf16[8,8,512]{2,1,0:T(8,128)(2,1)S(1)} %all_to_all.45.rows_ref, f32[1,4096]{1,0:T(1,128)} %get-tuple-element.96), custom_call_target="tpu_custom_call" | custom-call | tf_op jit(solution)/shard_map/norm/pallas_call | solution.py:185
  22.1 16.1 %all_to_all.46 = bf16[32,8,256]{2,1,0:T(8,128)(2,1)S(1)} all-to-all(bf16[32,8,256]{2,1,0:T(8,128)(2,1)S(1)} %bitcast.17), channel_id=1, replica_groups=mesh['x'=4,'y'=4,'c'=2,'z'=8] {'x','y','c'}, dimensions={0} | all-to-all | bytes 262144 | tf_op jit(solution)/shard_map/all_to_all | solution.py:164
  38.3 2.3 %head.1 = f32[16,64,512]{2,1,0:T(8,128)S(1)} custom-call(s32[1,64]{1,0:T(1,128)} %get-tuple-element.97, bf16[256,256]{1,0:T(8,128)(2,1)S(1)} %bitcast.16, bf16[64,256]{1,0:T(8,128)(2,1)S(1)} %get-tuple-element.55.more_ref, bf16[16032,128]{1,0:T(8,128)(2,1)S(1)} %collective-permute-done.weight_ref, bf16[16032,128]{1,0:T(8,128)(2,1)S(1)} %collective-permute-done.1.other_ref), custom_call_target="tpu_custom_call" | custom-call | tf_op jit(solution)/shard_map/head/pallas_call | solution.py:228
  40.6 0.0 copy-start
  40.6 0.3 convert_element_type.6
  40.8 18.6 %all_to_all.47 = f16[16,64,512]{2,1,0:T(8,128)(2,1)S(1)} all-to-all(f16[16,64,512]{2,1,0:T(8,128)(2,1)S(1)} %convert_element_type.6), channel_id=1, replica_groups=mesh['x'=4,'y'=4,'c'=2,'z'=8] {'x','y'}, dimensions={0} | all-to-all | bytes 2097152 | tf_op jit(solution)/shard_map/all_to_all | solution.py:164
  59.5 0.1 convert_reduce_fusion.logits_ref
  59.6 0.0 copy-done
  59.6 0.2 stats.1
  59.9 19.8 %all_to_all.48 = f32[256,1,128]{2,1,0:T(1,128)S(1)} all-to-all(f32[256,1,128]{2,1,0:T(1,128)S(1)} %bitcast.18), channel_id=1, replica_groups=mesh['x'=4,'y'=4,'c'=2,'z'=8] {'x','y','c','z'}, dimensions={0} | all-to-all | bytes 262144 | tf_op jit(solution)/shard_map/all_to_all | solution.py:164
  79.6 0.7 join.1
  (1 shorter events, 0.0 us)
Async XLA Ops:
  2.5 18.8 %collective-permute-start = (bf16[16032,128]{1,0:T(8,128)(2,1)}, bf16[16032,128]{1,0:T(8,128)(2,1)S(1)}, u32[]{:S(2)}, u32[]{:S(2)}) collective-permute-start(bf16[16032,128]{1,0:T(8,128)(2,1)} %bitcast.24), channel_id=1, source_target_pairs={{0,0},{8,8},{1,1},{9,9},{2,2},{10,10},{3,3},{11,11},{4,4},{12,12},... | collective-permute-start | bytes 12312584 | tf_op jit(solution)/shard_map/ppermute | solution.py:226
  4.7 16.6 %collective-permute-start.1 = (bf16[16032,128]{1,0:T(8,128)(2,1)}, bf16[16032,128]{1,0:T(8,128)(2,1)S(1)}, u32[]{:S(2)}, u32[]{:S(2)}) collective-permute-start(bf16[16032,128]{1,0:T(8,128)(2,1)} %bitcast.25), channel_id=1, source_target_pairs={{0,8},{8,0},{1,9},{9,1},{2,10},{10,2},{3,11},{11,3},{4,12},{12,4},... | collective-permute-start | bytes 12312584 | tf_op jit(solution)/shard_map/ppermute | solution.py:205
  40.6 19.1 %copy-start = (s32[64]{0:T(128)S(1)}, s32[64]{0:T(128)}, u32[]{:S(2)}) copy-start(s32[64]{0:T(128)} %param.9) | copy-start | bytes 772

commit v7 on v6

--- a/solution.py
+++ b/solution.py
@@ -174,6 +174,7 @@
         in_specs=[VMEM] + [SMEM] * len(first) + [VMEM],
         out_specs=(VMEM, SMEM),
         compiler_params=limit(4),
+        cost_estimate=pl.CostEstimate(flops=10**10, bytes_accessed=1 << 25, transcendentals=0),
         name="pick",
     )(lengths, *first, hidden)
 
@@ -188,6 +189,7 @@
         in_specs=[VMEM, VMEM],
         out_specs=VMEM,
         compiler_params=limit(4),
+        cost_estimate=pl.CostEstimate(flops=10**10, bytes_accessed=1 << 25, transcendentals=0),
         name="norm",
     )(rows, gain)
     return exchange(normed.reshape(chips * cores * SLOTS, width), CP), after
@@ -202,7 +204,6 @@
     half = chips * BLOCK
     start = jnp.zeros((1, 1), jnp.int32)
     rows, most = picked(lengths, (), hidden)
-    other = lax.ppermute(weight, "c", [(0, 1), (1, 0)])
 
     def again(state):
         first, more = state
@@ -223,8 +224,9 @@
         (start + SLOTS, jnp.zeros((n, gain.shape[1] // chips), jnp.bfloat16)),
     )
     rows, more, weight = lax.optimization_barrier((rows, more, weight))
-    own = lax.ppermute(weight, "c", [(0, 0), (1, 1)])
-    found, (own, other) = spread(rows, gain, (own, other))
+    found, weight = spread(rows, gain, weight)
+    other = lax.ppermute(weight, "c", [(0, 1), (1, 0)])
+    own = weight
     parts = pl.pallas_call(
         head_kernel,
         out_shape=shape((chips, n, BLOCK), jnp.float32),

time: 80.7 us -> 77.5 us (0.960)
  starting transfers between devices: 5.37 us -> 2.1 us
  Pallas kernels: 5.95 us -> 4.65 us
  blocking collectives: 67.9 us -> 69.2 us
    ppermute x1 -> x0, starting transfers between devices: 2.17 us -> none  [local(): own = lax.ppermute(weight, 'c', [(0, 0), (1, 1)])]
    all_to_all x4, blocking collectives: 67.9 us -> 69.2 us  [exchange(): return lax.all_to_all(x, axes, split_axis=0, concat_axis=0, tiled=True)]
    ppermute x1, starting transfers between devices: 3.2 us -> 2.1 us  [local(): other = lax.ppermute(weight, 'c', [(0, 1), (1, 0)])]
  transfers between devices with their start and end apart: 2 -> 1, of which waited for: 0 -> 0; matrix products, arithmetic and copies ran while one was open for 0% -> 0% of each run, Pallas kernels for 0% -> 0%
where the time goes in v7:
time: 77.5 us; the launch traced here: 77.2 us
  blocking collectives  69.2 us (89%)
  Pallas kernels  4.65 us (6%)
  starting transfers between devices  2.1 us (3%)
    all_to_all x4, blocking collectives, exchange(): return lax.all_to_all(x, axes, split_axis=0, concat_axis=0, tiled=True)  69.2 us
    ppermute x1, starting transfers between devices, local(): other = lax.ppermute(weight, 'c', [(0, 1), (1, 0)])  2.1 us
    pallas_call x1, Pallas kernels, picked(): pl.pallas_call(pick_kernel, out_shape=(shape((lax.axis_size('z'), SLOTS,...  1.94 us
    pallas_call x1, Pallas kernels, local(): pl.pallas_call(head_kernel, out_shape=shape((chips, n, BLOCK), jnp.float3...  1.65 us
  transfers between devices with their start and end apart: 1, of which 0 were waited for; matrix products, arithmetic and copies ran while one was open for 0% of the time, Pallas kernels for 0%

profile of v7, /device:TPU:1, one launch (start us, length us, event | category | flops | bytes accessed | tf_op | source)
XLA Modules:
  0.0 77.2 jit_solution(3435622523946753545)
XLA Ops:
  0.0 0.0 copy-start.2
  0.0 0.0 copy-start.3
  0.0 0.0 copy-start.4
  0.0 1.9 %pick.3 = (bf16[8,8,512]{2,1,0:T(8,128)(2,1)S(1)}, s32[1,1]{1,0:T(1,128)}) custom-call(s32[1,64]{1,0:T(1,128)} %bitcast.23, bf16[512,512]{1,0:T(8,128)(2,1)} %refs_0_.1), custom_call_target="tpu_custom_call" | custom-call | flops 10000000000 | bytes 33554432 | tf_op jit(solution)/shard_map/pick/pallas_call | solution.py:168
  2.0 0.0 copy-done.2
  2.0 0.0 copy-done.3
  2.0 0.0 copy-done.4
  2.0 0.0 copy-start
  2.0 0.7 while.9
  2.7 16.2 %all_to_all.45.rows_ref = bf16[8,8,512]{2,1,0:T(8,128)(2,1)S(1)} all-to-all(bf16[8,8,512]{2,1,0:T(8,128)(2,1)S(1)} %get-tuple-element.51), channel_id=1, replica_groups=mesh['x'=4,'y'=4,'c'=2,'z'=8] {'z'}, dimensions={0} | all-to-all | bytes 131072 | tf_op jit(solution)/shard_map/all_to_all | solution.py:164
  18.9 0.0 copy-done
  18.9 2.1 %collective-permute-start = (bf16[16032,128]{1,0:T(8,128)(2,1)S(1)}, bf16[16032,128]{1,0:T(8,128)(2,1)S(1)}, u32[]{:S(2)}, u32[]{:S(2)}) collective-permute-start(bf16[16032,128]{1,0:T(8,128)(2,1)S(1)} %bitcast.15), channel_id=1, source_target_pairs={{0,8},{8,0},{1,9},{9,1},{2,10},{10,2},{3,11},{11,3},{4,12},{12,4},... | collective-permute-start | bytes 12312584 | tf_op jit(solution)/shard_map/ppermute | solution.py:228
  21.0 0.1 norm.3
  21.1 14.7 %all_to_all.46 = bf16[32,8,256]{2,1,0:T(8,128)(2,1)S(1)} all-to-all(bf16[32,8,256]{2,1,0:T(8,128)(2,1)S(1)} %bitcast.21), channel_id=1, replica_groups=mesh['x'=4,'y'=4,'c'=2,'z'=8] {'x','y','c'}, dimensions={0} | all-to-all | bytes 262144 | tf_op jit(solution)/shard_map/all_to_all | solution.py:164
  35.8 0.0 collective-permute-done.other_ref
  35.8 1.7 %head.1 = f32[16,64,512]{2,1,0:T(8,128)S(1)} custom-call(s32[1,64]{1,0:T(1,128)S(1)} %get-tuple-element.94, bf16[256,256]{1,0:T(8,128)(2,1)S(1)} %bitcast.18, bf16[64,256]{1,0:T(8,128)(2,1)S(1)} %get-tuple-element.54.more_ref, bf16[16032,128]{1,0:T(8,128)(2,1)S(1)} %bitcast.16, bf16[16032,128]{1,0:T(8,128)(2,1)S(1)} %collective-permute-done.other_ref), custom_call_target="tpu_custom_call" | custom-call | tf_op jit(solution)/shard_map/head/pallas_call | solution.py:230
  37.5 0.0 copy-start.1
  37.5 0.3 convert_element_type.6
  37.7 18.6 %all_to_all.47 = f16[16,64,512]{2,1,0:T(8,128)(2,1)S(1)} all-to-all(f16[16,64,512]{2,1,0:T(8,128)(2,1)S(1)} %convert_element_type.6), channel_id=1, replica_groups=mesh['x'=4,'y'=4,'c'=2,'z'=8] {'x','y'}, dimensions={0} | all-to-all | bytes 2097152 | tf_op jit(solution)/shard_map/all_to_all | solution.py:164
  56.4 0.1 convert_reduce_fusion.logits_ref
  56.5 0.0 copy-done.1
  56.5 0.2 stats.1
  56.8 19.8 %all_to_all.48 = f32[256,1,128]{2,1,0:T(1,128)S(1)} all-to-all(f32[256,1,128]{2,1,0:T(1,128)S(1)} %bitcast.19), channel_id=1, replica_groups=mesh['x'=4,'y'=4,'c'=2,'z'=8] {'x','y','c','z'}, dimensions={0} | all-to-all | bytes 262144 | tf_op jit(solution)/shard_map/all_to_all | solution.py:164
  76.5 0.7 join.1
  (1 shorter events, 0.0 us)
Async XLA Ops:
  0.0 2.0 %copy-start.2 = (s32[64]{0:T(128)S(1)}, s32[64]{0:T(128)}, u32[]{:S(2)}) copy-start(s32[64]{0:T(128)} %param.8) | copy-start | bytes 772
  0.0 2.0 %copy-start.3 = (bf16[512,512]{1,0:T(8,128)(2,1)S(1)}, bf16[512,512]{1,0:T(8,128)(2,1)}, u32[]{:S(2)}) copy-start(bf16[512,512]{1,0:T(8,128)(2,1)} %refs_0_.1) | copy-start | bytes 1572868
  0.0 2.0 %copy-start.4 = (f32[4096]{0:T(1024)S(1)}, f32[4096]{0:T(1024)}, u32[]{:S(2)}) copy-start(f32[4096]{0:T(1024)} %param.10) | copy-start | bytes 49156
  2.0 16.9 %copy-start = (bf16[128,16032]{0,1:T(8,128)(2,1)S(1)}, bf16[128,16032]{0,1:T(8,128)(2,1)}, u32[]{:S(2)}) copy-start(bf16[128,16032]{0,1:T(8,128)(2,1)} %param.11) | copy-start | bytes 12312580
  18.9 16.9 %collective-permute-start = (bf16[16032,128]{1,0:T(8,128)(2,1)S(1)}, bf16[16032,128]{1,0:T(8,128)(2,1)S(1)}, u32[]{:S(2)}, u32[]{:S(2)}) collective-permute-start(bf16[16032,128]{1,0:T(8,128)(2,1)S(1)} %bitcast.15), channel_id=1, source_target_pairs={{0,8},{8,0},{1,9},{9,1},{2,10},{10,2},{3,11},{11,3},{4,12},{12,4},... | collective-permute-start | bytes 12312584 | tf_op jit(solution)/shard_map/ppermute | solution.py:228
  37.5 19.1 %copy-start.1 = (s32[64]{0:T(128)S(1)}, s32[64]{0:T(128)}, u32[]{:S(2)}) copy-start(s32[64]{0:T(128)} %param.9) | copy-start | bytes 772

commit v8 on v7

--- a/solution.py
+++ b/solution.py
@@ -16,6 +16,7 @@
 NEG = -1e30
 
 VMEM = pl.BlockSpec(memory_space=pltpu.VMEM)
+HBM = pl.BlockSpec(memory_space=pltpu.HBM)
 SMEM = pl.BlockSpec(memory_space=pltpu.SMEM)
 MIB = 1 << 20
 
@@ -52,24 +53,33 @@
 
 
 def pick_kernel(lengths_ref, *refs):
-    *first_ref, hidden_ref, out_ref, most_ref = refs
-    n, rows_here = lengths_ref.shape[1], hidden_ref.shape[0]
-    ends, _ = ends_of(lengths_ref)
+    *first_ref, hidden_ref, out_ref, more_ref, lengths, hidden, flag, sems = refs
+    small = pltpu.make_async_copy(lengths_ref, lengths, sems.at[0])
+    large = pltpu.make_async_copy(hidden_ref, hidden, sems.at[1])
+    small.start()
+    large.start()
+    first = first_ref[0][0, 0] if first_ref else jnp.int32(0)
+    small.wait()
+    n, rows_here = lengths.shape[1], hidden.shape[0]
+    ends, _ = ends_of(lengths)
+    counts = total(jnp.where(jnp.floor(ends / rows_here) == iota((32, n), 0), 1.0, 0.0), 1)
+    most = jnp.max(counts).astype(jnp.int32)
+    flag[0, 0] = (most > first + SLOTS).astype(jnp.int32)
+    tell = pltpu.make_async_copy(flag, more_ref, sems.at[2])
+    tell.start()
     base = (place() * rows_here).astype(jnp.float32)
     owned = (ends >= base) & (ends < base + rows_here)
     before = total(jnp.where(ends < base, 1.0, 0.0), 1)
-    slot = iota((1, n), 1) - before
-    if first_ref:
-        slot = slot - first_ref[0][0, 0].astype(jnp.float32)
+    slot = iota((1, n), 1) - before - first.astype(jnp.float32)
     wanted = owned & (slot == iota((SLOTS, n), 0))
     at = total(jnp.where(wanted, ends - base + 1.0, 0.0), 1) - 1.0
     selector = (at == iota((SLOTS, rows_here), 1)).astype(jnp.bfloat16)
-    counts = total(jnp.where(jnp.floor(ends / rows_here) == iota((32, n), 0), 1.0, 0.0), 1)
-    most_ref[0, 0] = jnp.max(counts).astype(jnp.int32)
-    picked = jnp.dot(selector, hidden_ref[...], preferred_element_type=jnp.float32)
+    large.wait()
+    picked = jnp.dot(selector, hidden[...], preferred_element_type=jnp.float32)
     picked = picked.astype(jnp.bfloat16)
     for peer in range(out_ref.shape[0]):
         out_ref[peer] = picked
+    tell.wait()
 
 
 def norm_kernel(rows_ref, gain_ref, out_ref):
@@ -160,6 +170,10 @@
     return jax.ShapeDtypeStruct(dims, dtype)
 
 
+def in_hbm(x):
+    return pltpu.with_memory_space_constraint(x, pltpu.HBM)
+
+
 def exchange(x, axes):
     return lax.all_to_all(x, axes, split_axis=0, concat_axis=0, tiled=True)
 
@@ -171,12 +185,18 @@
             shape((lax.axis_size("z"), SLOTS, hidden.shape[1]), hidden.dtype),
             shape((1, 1), jnp.int32),
         ),
-        in_specs=[VMEM] + [SMEM] * len(first) + [VMEM],
-        out_specs=(VMEM, SMEM),
+        in_specs=[HBM] + [SMEM] * len(first) + [HBM],
+        out_specs=(VMEM, HBM),
+        scratch_shapes=[
+            pltpu.VMEM(lengths.shape, lengths.dtype),
+            pltpu.VMEM(hidden.shape, hidden.dtype),
+            pltpu.SMEM((1, 1), jnp.int32),
+            pltpu.SemaphoreType.DMA((3,)),
+        ],
         compiler_params=limit(4),
         cost_estimate=pl.CostEstimate(flops=10**10, bytes_accessed=1 << 25, transcendentals=0),
         name="pick",
-    )(lengths, *first, hidden)
+    )(in_hbm(lengths), *first, in_hbm(hidden))
 
 
 def spread(rows, gain, after=()):
@@ -203,12 +223,13 @@
     chips = lax.axis_size(CHIPS)
     half = chips * BLOCK
     start = jnp.zeros((1, 1), jnp.int32)
-    rows, most = picked(lengths, (), hidden)
+    rows, some = picked(lengths, (), hidden)
 
     def again(state):
-        first, more = state
-        found = spread(picked(lengths, (first,), hidden)[0], gain)[0]
-        return pl.pallas_call(
+        _, first, more = state
+        rows, some = picked(lengths, (first,), hidden)
+        found = spread(rows, gain)[0]
+        first, more = pl.pallas_call(
             order_kernel,
             out_shape=(shape(first.shape, first.dtype), shape(more.shape, more.dtype)),
             in_specs=[VMEM, SMEM, VMEM, VMEM],
@@ -217,11 +238,12 @@
             compiler_params=limit(4),
             name="order",
         )(lengths, first, found, more)
-
-    _, more = lax.while_loop(
-        lambda state: state[0][0, 0] < most[0, 0],
+        return some, first, more
+
+    _, _, more = lax.while_loop(
+        lambda state: state[0][0, 0] != 0,
         again,
-        (start + SLOTS, jnp.zeros((n, gain.shape[1] // chips), jnp.bfloat16)),
+        (some, start + SLOTS, jnp.zeros((n, gain.shape[1] // chips), jnp.bfloat16)),
     )
     rows, more, weight = lax.optimization_barrier((rows, more, weight))
     found, weight = spread(rows, gain, weight)

time: 77.5 us -> 77.1 us (level)
  no operation moved by 1% of the time
where the time goes in v8:
time: 77.1 us; the launch traced here: 76.9 us
  blocking collectives  69.2 us (90%)
  Pallas kernels  4.19 us (5%)
  starting transfers between devices  2.1 us (3%)
  loops' own time  0.8 us (1%)
    all_to_all x4, blocking collectives, exchange(): return lax.all_to_all(x, axes, split_axis=0, concat_axis=0, tiled=True)  69.2 us
    ppermute x1, starting transfers between devices, local(): other = lax.ppermute(weight, 'c', [(0, 1), (1, 0)])  2.1 us
    pallas_call x1, Pallas kernels, local(): pl.pallas_call(head_kernel, out_shape=shape((chips, n, BLOCK), jnp.float3...  1.64 us
  transfers between devices with their start and end apart: 1, of which 0 were waited for; matrix products, arithmetic and copies ran while one was open for 0% of the time, Pallas kernels for 0%

profile of v8, /device:TPU:1, one launch (start us, length us, event | category | flops | bytes accessed | tf_op | source)
XLA Modules:
  0.0 76.9 jit_solution(6139967626160733268)
XLA Ops:
  0.0 0.0 copy-start.2
  0.0 0.0 copy-start.4
  0.0 1.5 %pick.3 = (bf16[8,8,512]{2,1,0:T(8,128)(2,1)S(1)}, s32[1,1]{1,0:T(1,128)}) custom-call(s32[1,64]{1,0:T(1,128)} %bitcast.23, bf16[512,512]{1,0:T(8,128)(2,1)} %refs_0_.1), custom_call_target="tpu_custom_call" | custom-call | flops 10000000000 | bytes 33554432 | tf_op jit(solution)/shard_map/pick/pallas_call | solution.py:182
  1.5 0.0 copy-done.2
  1.5 0.0 copy-done.4
  1.5 0.0 copy-start
  1.5 0.8 %while.11 = (s32[1,1]{1,0:T(1,128)}, s32[1,1]{1,0:T(1,128)}, bf16[64,256]{1,0:T(8,128)(2,1)S(1)}, s32[1,64]{1,0:T(1,128)S(1)}, bf16[512,512]{1,0:T(8,128)(2,1)}, /*index=5*/f32[1,4096]{1,0:T(1,128)S(1)}, s32[64]{0:T(128)}) while((s32[1,1]{1,0:T(1,128)}, s32[1,1]{1,0:T(1,128)}, bf16[64,256]{1,0:T(8,128)(2,1)S(1)}, s32[1,64]{1,0:T(1,128)S(1)}, ...), condition=%region_1.0_spmd, body=%region_0.0_spmd | while | flops 20000000000 | bytes 67503200 | solution.py:243
  2.4 16.2 %all_to_all.45.rows_ref = bf16[8,8,512]{2,1,0:T(8,128)(2,1)S(1)} all-to-all(bf16[8,8,512]{2,1,0:T(8,128)(2,1)S(1)} %get-tuple-element.50), channel_id=1, replica_groups=mesh['x'=4,'y'=4,'c'=2,'z'=8] {'z'}, dimensions={0} | all-to-all | bytes 131072 | tf_op jit(solution)/shard_map/all_to_all | solution.py:178
  18.5 0.0 copy-done
  18.5 2.1 %collective-permute-start = (bf16[16032,128]{1,0:T(8,128)(2,1)S(1)}, bf16[16032,128]{1,0:T(8,128)(2,1)S(1)}, u32[]{:S(2)}, u32[]{:S(2)}) collective-permute-start(bf16[16032,128]{1,0:T(8,128)(2,1)S(1)} %bitcast.15), channel_id=1, source_target_pairs={{0,8},{8,0},{1,9},{9,1},{2,10},{10,2},{3,11},{11,3},{4,12},{12,4},... | collective-permute-start | bytes 12312584 | tf_op jit(solution)/shard_map/ppermute | solution.py:250
  20.6 0.1 norm.3
  20.8 14.7 %all_to_all.46 = bf16[32,8,256]{2,1,0:T(8,128)(2,1)S(1)} all-to-all(bf16[32,8,256]{2,1,0:T(8,128)(2,1)S(1)} %bitcast.21), channel_id=1, replica_groups=mesh['x'=4,'y'=4,'c'=2,'z'=8] {'x','y','c'}, dimensions={0} | all-to-all | bytes 262144 | tf_op jit(solution)/shard_map/all_to_all | solution.py:178
  35.4 0.0 collective-permute-done.other_ref
  35.4 1.6 %head.1 = f32[16,64,512]{2,1,0:T(8,128)S(1)} custom-call(s32[1,64]{1,0:T(1,128)S(1)} %get-tuple-element.96, bf16[256,256]{1,0:T(8,128)(2,1)S(1)} %bitcast.18, bf16[64,256]{1,0:T(8,128)(2,1)S(1)} %get-tuple-element.95, bf16[16032,128]{1,0:T(8,128)(2,1)S(1)} %bitcast.16, bf16[16032,128]{1,0:T(8,128)(2,1)S(1)} %collective-permute-done.other_ref), custom_call_target="tpu_custom_call" | custom-call | tf_op jit(solution)/shard_map/head/pallas_call | solution.py:252
  37.1 0.0 copy-start.1
  37.1 0.3 convert_element_type.6
  37.4 18.6 %all_to_all.47 = f16[16,64,512]{2,1,0:T(8,128)(2,1)S(1)} all-to-all(f16[16,64,512]{2,1,0:T(8,128)(2,1)S(1)} %convert_element_type.6), channel_id=1, replica_groups=mesh['x'=4,'y'=4,'c'=2,'z'=8] {'x','y'}, dimensions={0} | all-to-all | bytes 2097152 | tf_op jit(solution)/shard_map/all_to_all | solution.py:178
  56.0 0.1 convert_reduce_fusion.logits_ref
  56.2 0.0 copy-done.1
  56.2 0.2 stats.1
  56.4 19.8 %all_to_all.48 = f32[256,1,128]{2,1,0:T(1,128)S(1)} all-to-all(f32[256,1,128]{2,1,0:T(1,128)S(1)} %bitcast.19), channel_id=1, replica_groups=mesh['x'=4,'y'=4,'c'=2,'z'=8] {'x','y','c','z'}, dimensions={0} | all-to-all | bytes 262144 | tf_op jit(solution)/shard_map/all_to_all | solution.py:178
  76.1 0.7 join.1
  (1 shorter events, 0.0 us)
Async XLA Ops:
  0.0 1.5 %copy-start.2 = (s32[64]{0:T(128)S(1)}, s32[64]{0:T(128)}, u32[]{:S(2)}) copy-start(s32[64]{0:T(128)} %param.8) | copy-start | bytes 772
  0.0 1.5 %copy-start.4 = (f32[4096]{0:T(1024)S(1)}, f32[4096]{0:T(1024)}, u32[]{:S(2)}) copy-start(f32[4096]{0:T(1024)} %param.10) | copy-start | bytes 49156
  1.5 17.0 %copy-start = (bf16[128,16032]{0,1:T(8,128)(2,1)S(1)}, bf16[128,16032]{0,1:T(8,128)(2,1)}, u32[]{:S(2)}) copy-start(bf16[128,16032]{0,1:T(8,128)(2,1)} %param.11) | copy-start | bytes 12312580
  18.5 16.9 %collective-permute-start = (bf16[16032,128]{1,0:T(8,128)(2,1)S(1)}, bf16[16032,128]{1,0:T(8,128)(2,1)S(1)}, u32[]{:S(2)}, u32[]{:S(2)}) collective-permute-start(bf16[16032,128]{1,0:T(8,128)(2,1)S(1)} %bitcast.15), channel_id=1, source_target_pairs={{0,8},{8,0},{1,9},{9,1},{2,10},{10,2},{3,11},{11,3},{4,12},{12,4},... | collective-permute-start | bytes 12312584 | tf_op jit(solution)/shard_map/ppermute | solution.py:250
  37.1 19.1 %copy-start.1 = (s32[64]{0:T(128)S(1)}, s32[64]{0:T(128)}, u32[]{:S(2)}) copy-start(s32[64]{0:T(128)} %param.9) | copy-start | bytes 772

commit v9 on v8

--- a/solution.py
+++ b/solution.py
@@ -53,7 +53,7 @@
 
 
 def pick_kernel(lengths_ref, *refs):
-    *first_ref, hidden_ref, out_ref, more_ref, lengths, hidden, flag, sems = refs
+    *first_ref, hidden_ref, out_ref, more_ref, lengths, hidden, sems = refs
     small = pltpu.make_async_copy(lengths_ref, lengths, sems.at[0])
     large = pltpu.make_async_copy(hidden_ref, hidden, sems.at[1])
     small.start()
@@ -64,9 +64,7 @@
     ends, _ = ends_of(lengths)
     counts = total(jnp.where(jnp.floor(ends / rows_here) == iota((32, n), 0), 1.0, 0.0), 1)
     most = jnp.max(counts).astype(jnp.int32)
-    flag[0, 0] = (most > first + SLOTS).astype(jnp.int32)
-    tell = pltpu.make_async_copy(flag, more_ref, sems.at[2])
-    tell.start()
+    more_ref[0, 0] = (most > first + SLOTS).astype(jnp.int32)
     base = (place() * rows_here).astype(jnp.float32)
     owned = (ends >= base) & (ends < base + rows_here)
     before = total(jnp.where(ends < base, 1.0, 0.0), 1)
@@ -79,7 +77,6 @@
     picked = picked.astype(jnp.bfloat16)
     for peer in range(out_ref.shape[0]):
         out_ref[peer] = picked
-    tell.wait()
 
 
 def norm_kernel(rows_ref, gain_ref, out_ref):
@@ -183,15 +180,14 @@
         pick_kernel,
         out_shape=(
             shape((lax.axis_size("z"), SLOTS, hidden.shape[1]), hidden.dtype),
-            shape((1, 1), jnp.int32),
+            pltpu.SMEM((1, 1), jnp.int32),
         ),
         in_specs=[HBM] + [SMEM] * len(first) + [HBM],
-        out_specs=(VMEM, HBM),
+        out_specs=(VMEM, SMEM),
         scratch_shapes=[
             pltpu.VMEM(lengths.shape, lengths.dtype),
             pltpu.VMEM(hidden.shape, hidden.dtype),
-            pltpu.SMEM((1, 1), jnp.int32),
-            pltpu.SemaphoreType.DMA((3,)),
+            pltpu.SemaphoreType.DMA((2,)),
         ],
         compiler_params=limit(4),
         cost_estimate=pl.CostEstimate(flops=10**10, bytes_accessed=1 << 25, transcendentals=0),
@@ -238,12 +234,12 @@
             compiler_params=limit(4),
             name="order",
         )(lengths, first, found, more)
-        return some, first, more
+        return some[0, 0], first, more
 
     _, _, more = lax.while_loop(
-        lambda state: state[0][0, 0] != 0,
+        lambda state: state[0] != 0,
         again,
-        (some, start + SLOTS, jnp.zeros((n, gain.shape[1] // chips), jnp.bfloat16)),
+        (some[0, 0], start + SLOTS, jnp.zeros((n, gain.shape[1] // chips), jnp.bfloat16)),
     )
     rows, more, weight = lax.optimization_barrier((rows, more, weight))
     found, weight = spread(rows, gain, weight)

time: 77.1 us -> 76.1 us (0.987)
  loops' own time: 0.8 us -> 0.01 us
    another operation x1, loops' own time: 0.8 us -> 0.01 us  [local(): lax.while_loop(lambda state: state[0] != 0, again, (some[0, 0], start + S...]
where the time goes in v9:
time: 76.1 us; the launch traced here: 75.9 us
  blocking collectives  69.3 us (91%)
  Pallas kernels  3.99 us (5%)
  starting transfers between devices  2.1 us (3%)
    all_to_all x4, blocking collectives, exchange(): return lax.all_to_all(x, axes, split_axis=0, concat_axis=0, tiled=True)  69.3 us
    ppermute x1, starting transfers between devices, local(): other = lax.ppermute(weight, 'c', [(0, 1), (1, 0)])  2.1 us
    pallas_call x1, Pallas kernels, local(): pl.pallas_call(head_kernel, out_shape=shape((chips, n, BLOCK), jnp.float3...  1.65 us
  transfers between devices with their start and end apart: 1, of which 0 were waited for; matrix products, arithmetic and copies ran while one was open for 0% of the time, Pallas kernels for 0%

profile of v9, /device:TPU:1, one launch (start us, length us, event | category | flops | bytes accessed | tf_op | source)
XLA Modules:
  0.0 75.9 jit_solution(2378755090322923530)
XLA Ops:
  0.0 0.0 copy-start.2
  0.0 0.0 copy-start.4
  0.0 1.3 %pick.3 = (bf16[8,8,512]{2,1,0:T(8,128)(2,1)S(1)}, s32[1,1]{1,0:T(1,128)S(4)}) custom-call(s32[1,64]{1,0:T(1,128)} %bitcast.24, bf16[512,512]{1,0:T(8,128)(2,1)} %refs_0_.1), custom_call_target="tpu_custom_call" | custom-call | flops 10000000000 | bytes 33554432 | tf_op jit(solution)/shard_map/pick/pallas_call | solution.py:179
  1.3 0.0 copy-done.2
  1.3 0.0 copy-done.4
  1.3 16.0 %all_to_all.45.rows_ref = bf16[8,8,512]{2,1,0:T(8,128)(2,1)S(1)} all-to-all(bf16[8,8,512]{2,1,0:T(8,128)(2,1)S(1)} %get-tuple-element.50), channel_id=1, replica_groups=mesh['x'=4,'y'=4,'c'=2,'z'=8] {'z'}, dimensions={0} | all-to-all | bytes 131072 | tf_op jit(solution)/shard_map/all_to_all | solution.py:175
  17.4 0.0 copy-start
  17.4 2.1 %collective-permute-start = (bf16[16032,128]{1,0:T(8,128)(2,1)}, bf16[16032,128]{1,0:T(8,128)(2,1)S(1)}, u32[]{:S(2)}, u32[]{:S(2)}) collective-permute-start(bf16[16032,128]{1,0:T(8,128)(2,1)} %bitcast.16), channel_id=1, source_target_pairs={{0,8},{8,0},{1,9},{9,1},{2,10},{10,2},{3,11},{11,3},{4,12},{12,4},... | collective-permute-start | bytes 12312584 | tf_op jit(solution)/shard_map/ppermute | solution.py:246
  19.5 0.1 norm.3
  19.6 14.8 %all_to_all.46 = bf16[32,8,256]{2,1,0:T(8,128)(2,1)S(1)} all-to-all(bf16[32,8,256]{2,1,0:T(8,128)(2,1)S(1)} %bitcast.22), channel_id=1, replica_groups=mesh['x'=4,'y'=4,'c'=2,'z'=8] {'x','y','c'}, dimensions={0} | all-to-all | bytes 262144 | tf_op jit(solution)/shard_map/all_to_all | solution.py:175
  34.4 0.0 collective-permute-done.other_ref
  34.4 0.0 copy-done
  34.4 1.7 %head.1 = f32[16,64,512]{2,1,0:T(8,128)S(1)} custom-call(s32[1,64]{1,0:T(1,128)S(1)} %get-tuple-element.96, bf16[256,256]{1,0:T(8,128)(2,1)S(1)} %bitcast.19, bf16[64,256]{1,0:T(8,128)(2,1)S(1)} %get-tuple-element.95, bf16[16032,128]{1,0:T(8,128)(2,1)S(1)} %bitcast.17, bf16[16032,128]{1,0:T(8,128)(2,1)S(1)} %collective-permute-done.other_ref), custom_call_target="tpu_custom_call" | custom-call | tf_op jit(solution)/shard_map/head/pallas_call | solution.py:248
  36.1 0.0 copy-start.1
  36.1 0.3 convert_element_type.6
  36.4 18.6 %all_to_all.47 = f16[16,64,512]{2,1,0:T(8,128)(2,1)S(1)} all-to-all(f16[16,64,512]{2,1,0:T(8,128)(2,1)S(1)} %convert_element_type.6), channel_id=1, replica_groups=mesh['x'=4,'y'=4,'c'=2,'z'=8] {'x','y'}, dimensions={0} | all-to-all | bytes 2097152 | tf_op jit(solution)/shard_map/all_to_all | solution.py:175
  55.0 0.1 convert_reduce_fusion.logits_ref
  55.2 0.0 copy-done.1
  55.2 0.2 stats.1
  55.4 19.8 %all_to_all.48 = f32[256,1,128]{2,1,0:T(1,128)S(1)} all-to-all(f32[256,1,128]{2,1,0:T(1,128)S(1)} %bitcast.20), channel_id=1, replica_groups=mesh['x'=4,'y'=4,'c'=2,'z'=8] {'x','y','c','z'}, dimensions={0} | all-to-all | bytes 262144 | tf_op jit(solution)/shard_map/all_to_all | solution.py:175
  75.2 0.7 join.1
  (2 shorter events, 0.0 us)
Async XLA Ops:
  0.0 1.3 %copy-start.2 = (s32[64]{0:T(128)S(1)}, s32[64]{0:T(128)}, u32[]{:S(2)}) copy-start(s32[64]{0:T(128)} %param.8) | copy-start | bytes 772
  0.0 1.3 %copy-start.4 = (f32[4096]{0:T(1024)S(1)}, f32[4096]{0:T(1024)}, u32[]{:S(2)}) copy-start(f32[4096]{0:T(1024)} %param.10) | copy-start | bytes 49156
  17.4 17.1 %copy-start = (bf16[128,16032]{0,1:T(8,128)(2,1)S(1)}, bf16[128,16032]{0,1:T(8,128)(2,1)}, u32[]{:S(2)}) copy-start(bf16[128,16032]{0,1:T(8,128)(2,1)} %param.11) | copy-start | bytes 12312580
  17.4 17.1 %collective-permute-start = (bf16[16032,128]{1,0:T(8,128)(2,1)}, bf16[16032,128]{1,0:T(8,128)(2,1)S(1)}, u32[]{:S(2)}, u32[]{:S(2)}) collective-permute-start(bf16[16032,128]{1,0:T(8,128)(2,1)} %bitcast.16), channel_id=1, source_target_pairs={{0,8},{8,0},{1,9},{9,1},{2,10},{10,2},{3,11},{11,3},{4,12},{12,4},... | collective-permute-start | bytes 12312584 | tf_op jit(solution)/shard_map/ppermute | solution.py:246
  36.1 19.1 %copy-start.1 = (s32[64]{0:T(128)S(1)}, s32[64]{0:T(128)}, u32[]{:S(2)}) copy-start(s32[64]{0:T(128)} %param.9) | copy-start | bytes 772

commit v10 on v9

--- a/solution.py
+++ b/solution.py
@@ -9,6 +9,7 @@
 from jax.sharding import PartitionSpec as P
 
 CHIPS = ("x", "y")
+LINE = ("c", "z")
 CP = ("x", "y", "c")
 ALL = ("x", "y", "c", "z")
 SLOTS = 8
@@ -80,20 +81,20 @@
 
 
 def norm_kernel(rows_ref, gain_ref, out_ref):
-    parts, _, width = rows_ref.shape
-    squares = jnp.zeros((SLOTS, 1), jnp.float32)
-    for part in range(parts):
-        values = rows_ref[part].astype(jnp.float32)
-        squares = squares + total(values * values, 1)
-    scale = jnp.sqrt(squares / (parts * width) + 1e-05)
-    chips, cores, _, block = out_ref.shape
-    for chip in range(chips):
-        part, at = divmod(chip * block, width)
-        values = rows_ref[part, :, at : at + block].astype(jnp.float32)
-        gain = gain_ref[:, chip * block : (chip + 1) * block]
-        normed = (values * gain / scale).astype(jnp.bfloat16)
-        for core in range(cores):
-            out_ref[chip, core] = normed
+    cores, parts, _, width = rows_ref.shape
+    chips, _, block = out_ref.shape
+    for core in range(cores):
+        squares = jnp.zeros((SLOTS, 1), jnp.float32)
+        for part in range(parts):
+            values = rows_ref[core, part].astype(jnp.float32)
+            squares = squares + total(values * values, 1)
+        scale = jnp.sqrt(squares / (parts * width) + 1e-05)
+        for chip in range(chips):
+            part, at = divmod(chip * block, width)
+            values = rows_ref[core, part, :, at : at + block].astype(jnp.float32)
+            gain = gain_ref[:, chip * block : (chip + 1) * block]
+            normed = (values * gain / scale).astype(jnp.bfloat16)
+            out_ref[chip, core * SLOTS : (core + 1) * SLOTS] = normed
 
 
 def rows_in_order(lengths_ref, found_ref, first=0.0):
@@ -179,7 +180,7 @@
     return pl.pallas_call(
         pick_kernel,
         out_shape=(
-            shape((lax.axis_size("z"), SLOTS, hidden.shape[1]), hidden.dtype),
+            shape((lax.axis_size(LINE), SLOTS, hidden.shape[1]), hidden.dtype),
             pltpu.SMEM((1, 1), jnp.int32),
         ),
         in_specs=[HBM] + [SMEM] * len(first) + [HBM],
@@ -198,17 +199,18 @@
 def spread(rows, gain, after=()):
     chips, cores = lax.axis_size(CHIPS), lax.axis_size("c")
     width = gain.shape[1] // chips
-    rows, after = lax.optimization_barrier((exchange(rows, "z"), after))
+    rows, after = lax.optimization_barrier((exchange(rows, LINE), after))
+    rows = rows.reshape(cores, -1, *rows.shape[1:])
     normed = pl.pallas_call(
         norm_kernel,
-        out_shape=shape((chips, cores, SLOTS, width), jnp.bfloat16),
+        out_shape=shape((chips, cores * SLOTS, width), jnp.bfloat16),
         in_specs=[VMEM, VMEM],
         out_specs=VMEM,
         compiler_params=limit(4),
         cost_estimate=pl.CostEstimate(flops=10**10, bytes_accessed=1 << 25, transcendentals=0),
         name="norm",
     )(rows, gain)
-    return exchange(normed.reshape(chips * cores * SLOTS, width), CP), after
+    return exchange(normed.reshape(chips * cores * SLOTS, width), CHIPS), after
 
 
 def local(hidden, lengths, targets, norm_gain, lm_weight):

time: 76.1 us -> 76.2 us (level)
  blocking collectives: 69.3 us -> 70.2 us
  starting transfers between devices: 2.1 us -> 1.26 us
    all_to_all x4, blocking collectives: 69.3 us -> 70.2 us  [exchange(): return lax.all_to_all(x, axes, split_axis=0, concat_axis=0, tiled=True)]
    ppermute x1, starting transfers between devices: 2.1 us -> 1.26 us  [local(): other = lax.ppermute(weight, 'c', [(0, 1), (1, 0)])]
where the time goes in v10:
time: 76.2 us; the launch traced here: 76 us
  blocking collectives  70.2 us (92%)
  Pallas kernels  4.03 us (5%)
  starting transfers between devices  1.26 us (2%)
    all_to_all x4, blocking collectives, exchange(): return lax.all_to_all(x, axes, split_axis=0, concat_axis=0, tiled=True)  70.2 us
    pallas_call x1, Pallas kernels, local(): pl.pallas_call(head_kernel, out_shape=shape((chips, n, BLOCK), jnp.float3...  1.65 us
  transfers between devices with their start and end apart: 1, of which 0 were waited for; matrix products, arithmetic and copies ran while one was open for 0% of the time, Pallas kernels for 0%

profile of v10, /device:TPU:1, one launch (start us, length us, event | category | flops | bytes accessed | tf_op | source)
XLA Modules:
  0.0 76.0 jit_solution(10136123249630094921)
XLA Ops:
  0.0 0.0 copy-start.2
  0.0 0.0 copy-start.4
  0.0 1.3 %pick.3 = (bf16[16,8,512]{2,1,0:T(8,128)(2,1)S(1)}, s32[1,1]{1,0:T(1,128)S(4)}) custom-call(s32[1,64]{1,0:T(1,128)} %bitcast.24, bf16[512,512]{1,0:T(8,128)(2,1)} %refs_0_.1), custom_call_target="tpu_custom_call" | custom-call | flops 10000000000 | bytes 33554432 | tf_op jit(solution)/shard_map/pick/pallas_call | solution.py:180
  1.3 0.0 copy-done.2
  1.3 0.0 copy-done.4
  1.4 17.1 %all_to_all.40 = bf16[16,8,512]{2,1,0:T(8,128)(2,1)S(1)} all-to-all(bf16[16,8,512]{2,1,0:T(8,128)(2,1)S(1)} %get-tuple-element.50), channel_id=1, replica_groups=mesh['x'=4,'y'=4,'c'=2,'z'=8] {'c','z'}, dimensions={0} | all-to-all | bytes 262144 | tf_op jit(solution)/shard_map/all_to_all | solution.py:176
  18.5 1.3 %collective-permute-start = (bf16[16032,128]{1,0:T(8,128)(2,1)}, bf16[16032,128]{1,0:T(8,128)(2,1)S(1)}, u32[]{:S(2)}, u32[]{:S(2)}) collective-permute-start(bf16[16032,128]{1,0:T(8,128)(2,1)} %bitcast.16), channel_id=1, source_target_pairs={{0,8},{8,0},{1,9},{9,1},{2,10},{10,2},{3,11},{11,3},{4,12},{12,4},... | collective-permute-start | bytes 12312584 | tf_op jit(solution)/shard_map/ppermute | solution.py:248
  19.8 0.0 copy-start
  19.8 0.1 norm.3
  19.9 13.5 %all_to_all.41 = bf16[16,16,256]{2,1,0:T(8,128)(2,1)S(1)} all-to-all(bf16[16,16,256]{2,1,0:T(8,128)(2,1)S(1)} %norm.3), channel_id=1, replica_groups=mesh['x'=4,'y'=4,'c'=2,'z'=8] {'x','y'}, dimensions={0} | all-to-all | bytes 262144 | tf_op jit(solution)/shard_map/all_to_all | solution.py:176
  33.5 0.0 collective-permute-done.other_ref
  33.5 0.0 copy-done
  33.5 1.7 %head.1 = f32[16,64,512]{2,1,0:T(8,128)S(1)} custom-call(s32[1,64]{1,0:T(1,128)S(1)} %get-tuple-element.96, bf16[256,256]{1,0:T(8,128)(2,1)S(1)} %bitcast.19, bf16[64,256]{1,0:T(8,128)(2,1)S(1)} %get-tuple-element.95, bf16[16032,128]{1,0:T(8,128)(2,1)S(1)} %bitcast.17, bf16[16032,128]{1,0:T(8,128)(2,1)S(1)} %collective-permute-done.other_ref), custom_call_target="tpu_custom_call" | custom-call | tf_op jit(solution)/shard_map/head/pallas_call | solution.py:250
  35.1 0.0 copy-start.1
  35.1 0.3 convert_element_type.6
  35.4 18.0 %all_to_all.42 = f16[16,64,512]{2,1,0:T(8,128)(2,1)S(1)} all-to-all(f16[16,64,512]{2,1,0:T(8,128)(2,1)S(1)} %convert_element_type.6), channel_id=1, replica_groups=mesh['x'=4,'y'=4,'c'=2,'z'=8] {'x','y'}, dimensions={0} | all-to-all | bytes 2097152 | tf_op jit(solution)/shard_map/all_to_all | solution.py:176
  53.4 0.1 convert_reduce_fusion.logits_ref
  53.6 0.0 copy-done.1
  53.6 0.2 stats.1
  53.8 21.5 %all_to_all.43 = f32[256,1,128]{2,1,0:T(1,128)S(1)} all-to-all(f32[256,1,128]{2,1,0:T(1,128)S(1)} %bitcast.20), channel_id=1, replica_groups=mesh['x'=4,'y'=4,'c'=2,'z'=8] {'x','y','c','z'}, dimensions={0} | all-to-all | bytes 262144 | tf_op jit(solution)/shard_map/all_to_all | solution.py:176
  75.3 0.7 join.1
  (2 shorter events, 0.0 us)
Async XLA Ops:
  0.0 1.3 %copy-start.2 = (s32[64]{0:T(128)S(1)}, s32[64]{0:T(128)}, u32[]{:S(2)}) copy-start(s32[64]{0:T(128)} %param.8) | copy-start | bytes 772
  0.0 1.3 %copy-start.4 = (f32[4096]{0:T(1024)S(1)}, f32[4096]{0:T(1024)}, u32[]{:S(2)}) copy-start(f32[4096]{0:T(1024)} %param.10) | copy-start | bytes 49156
  18.5 15.0 %collective-permute-start = (bf16[16032,128]{1,0:T(8,128)(2,1)}, bf16[16032,128]{1,0:T(8,128)(2,1)S(1)}, u32[]{:S(2)}, u32[]{:S(2)}) collective-permute-start(bf16[16032,128]{1,0:T(8,128)(2,1)} %bitcast.16), channel_id=1, source_target_pairs={{0,8},{8,0},{1,9},{9,1},{2,10},{10,2},{3,11},{11,3},{4,12},{12,4},... | collective-permute-start | bytes 12312584 | tf_op jit(solution)/shard_map/ppermute | solution.py:248
  19.8 13.7 %copy-start = (bf16[128,16032]{0,1:T(8,128)(2,1)S(1)}, bf16[128,16032]{0,1:T(8,128)(2,1)}, u32[]{:S(2)}) copy-start(bf16[128,16032]{0,1:T(8,128)(2,1)} %param.11) | copy-start | bytes 12312580
  35.1 18.4 %copy-start.1 = (s32[64]{0:T(128)S(1)}, s32[64]{0:T(128)}, u32[]{:S(2)}) copy-start(s32[64]{0:T(128)} %param.9) | copy-start | bytes 772

commit v11 on v9

--- a/solution.py
+++ b/solution.py
@@ -12,6 +12,7 @@
 CP = ("x", "y", "c")
 ALL = ("x", "y", "c", "z")
 SLOTS = 8
+ORDER = [5, 6, 7, 0, 1, 2, 3, 4]
 BLOCK = 512
 NEG = -1e30
 
@@ -89,6 +90,7 @@
     chips, cores, _, block = out_ref.shape
     for chip in range(chips):
         part, at = divmod(chip * block, width)
+        part = ORDER.index(part)
         values = rows_ref[part, :, at : at + block].astype(jnp.float32)
         gain = gain_ref[:, chip * block : (chip + 1) * block]
         normed = (values * gain / scale).astype(jnp.bfloat16)
@@ -171,8 +173,10 @@
     return pltpu.with_memory_space_constraint(x, pltpu.HBM)
 
 
-def exchange(x, axes):
-    return lax.all_to_all(x, axes, split_axis=0, concat_axis=0, tiled=True)
+def exchange(x, axes, groups=None):
+    return lax.all_to_all(
+        x, axes, split_axis=0, concat_axis=0, tiled=True, axis_index_groups=groups
+    )
 
 
 def picked(lengths, first, hidden):
@@ -198,7 +202,7 @@
 def spread(rows, gain, after=()):
     chips, cores = lax.axis_size(CHIPS), lax.axis_size("c")
     width = gain.shape[1] // chips
-    rows, after = lax.optimization_barrier((exchange(rows, "z"), after))
+    rows, after = lax.optimization_barrier((exchange(rows, "z", [ORDER]), after))
     normed = pl.pallas_call(
         norm_kernel,
         out_shape=shape((chips, cores, SLOTS, width), jnp.bfloat16),

time: 76.1 us -> 75.9 us (level)
  no operation moved by 1% of the time
where the time goes in v11:
time: 75.9 us; the launch traced here: 75.7 us
  blocking collectives  69.5 us (92%)
  Pallas kernels  3.99 us (5%)
  starting transfers between devices  1.62 us (2%)
    all_to_all x4, blocking collectives, exchange(): lax.all_to_all(x, axes, split_axis=0, concat_axis=0, tiled=True, axis_ind...  69.5 us
    pallas_call x1, Pallas kernels, local(): pl.pallas_call(head_kernel, out_shape=shape((chips, n, BLOCK), jnp.float3...  1.65 us
    ppermute x1, starting transfers between devices, local(): other = lax.ppermute(weight, 'c', [(0, 1), (1, 0)])  1.62 us
  transfers between devices with their start and end apart: 1, of which 0 were waited for; matrix products, arithmetic and copies ran while one was open for 0% of the time, Pallas kernels for 0%

profile of v11, /device:TPU:1, one launch (start us, length us, event | category | flops | bytes accessed | tf_op | source)
XLA Modules:
  0.0 75.7 jit_solution(4483565301015933480)
XLA Ops:
  0.0 0.0 copy-start.2
  0.0 0.0 copy-start.4
  0.0 1.3 %pick.3 = (bf16[8,8,512]{2,1,0:T(8,128)(2,1)S(1)}, s32[1,1]{1,0:T(1,128)S(4)}) custom-call(s32[1,64]{1,0:T(1,128)} %bitcast.24, bf16[512,512]{1,0:T(8,128)(2,1)} %refs_0_.1), custom_call_target="tpu_custom_call" | custom-call | flops 10000000000 | bytes 33554432 | tf_op jit(solution)/shard_map/pick/pallas_call | solution.py:183
  1.3 0.0 copy-done.2
  1.3 0.0 copy-done.4
  1.3 12.8 %all_to_all.45.rows_ref = bf16[8,8,512]{2,1,0:T(8,128)(2,1)S(1)} all-to-all(bf16[8,8,512]{2,1,0:T(8,128)(2,1)S(1)} %get-tuple-element.50), channel_id=1, replica_groups={{5,6,7,0,1,2,3,4},{13,14,15,8,9,10,11,12},{21,22,23,16,17,18,19,20},{29..., dimensions={0} | all-to-all | bytes 131072 | tf_op jit(solution)/shard_map/all_to_all | solution.py:177
  14.2 0.0 copy-start
  14.2 1.6 %collective-permute-start = (bf16[16032,128]{1,0:T(8,128)(2,1)}, bf16[16032,128]{1,0:T(8,128)(2,1)S(1)}, u32[]{:S(2)}, u32[]{:S(2)}) collective-permute-start(bf16[16032,128]{1,0:T(8,128)(2,1)} %bitcast.16), channel_id=1, source_target_pairs={{0,8},{8,0},{1,9},{9,1},{2,10},{10,2},{3,11},{11,3},{4,12},{12,4},... | collective-permute-start | bytes 12312584 | tf_op jit(solution)/shard_map/ppermute | solution.py:250
  15.8 0.1 norm.3
  15.9 14.8 %all_to_all.46 = bf16[32,8,256]{2,1,0:T(8,128)(2,1)S(1)} all-to-all(bf16[32,8,256]{2,1,0:T(8,128)(2,1)S(1)} %bitcast.22), channel_id=1, replica_groups=mesh['x'=4,'y'=4,'c'=2,'z'=8] {'x','y','c'}, dimensions={0} | all-to-all | bytes 262144 | tf_op jit(solution)/shard_map/all_to_all | solution.py:177
  30.7 0.0 collective-permute-done.other_ref
  30.7 0.0 copy-done
  30.7 1.6 %head.1 = f32[16,64,512]{2,1,0:T(8,128)S(1)} custom-call(s32[1,64]{1,0:T(1,128)S(1)} %get-tuple-element.96, bf16[256,256]{1,0:T(8,128)(2,1)S(1)} %bitcast.19, bf16[64,256]{1,0:T(8,128)(2,1)S(1)} %get-tuple-element.95, bf16[16032,128]{1,0:T(8,128)(2,1)S(1)} %bitcast.17, bf16[16032,128]{1,0:T(8,128)(2,1)S(1)} %collective-permute-done.other_ref), custom_call_target="tpu_custom_call" | custom-call | tf_op jit(solution)/shard_map/head/pallas_call | solution.py:252
  32.4 0.0 copy-start.1
  32.4 0.3 convert_element_type.6
  32.7 18.6 %all_to_all.47 = f16[16,64,512]{2,1,0:T(8,128)(2,1)S(1)} all-to-all(f16[16,64,512]{2,1,0:T(8,128)(2,1)S(1)} %convert_element_type.6), channel_id=1, replica_groups=mesh['x'=4,'y'=4,'c'=2,'z'=8] {'x','y'}, dimensions={0} | all-to-all | bytes 2097152 | tf_op jit(solution)/shard_map/all_to_all | solution.py:177
  51.3 0.1 convert_reduce_fusion.logits_ref
  51.5 0.0 copy-done.1
  51.5 0.2 stats.1
  51.7 23.2 %all_to_all.48 = f32[256,1,128]{2,1,0:T(1,128)S(1)} all-to-all(f32[256,1,128]{2,1,0:T(1,128)S(1)} %bitcast.20), channel_id=1, replica_groups=mesh['x'=4,'y'=4,'c'=2,'z'=8] {'x','y','c','z'}, dimensions={0} | all-to-all | bytes 262144 | tf_op jit(solution)/shard_map/all_to_all | solution.py:177
  74.9 0.7 join.1
  (2 shorter events, 0.0 us)
Async XLA Ops:
  0.0 1.3 %copy-start.2 = (s32[64]{0:T(128)S(1)}, s32[64]{0:T(128)}, u32[]{:S(2)}) copy-start(s32[64]{0:T(128)} %param.8) | copy-start | bytes 772
  0.0 1.3 %copy-start.4 = (f32[4096]{0:T(1024)S(1)}, f32[4096]{0:T(1024)}, u32[]{:S(2)}) copy-start(f32[4096]{0:T(1024)} %param.10) | copy-start | bytes 49156
  14.2 16.6 %copy-start = (bf16[128,16032]{0,1:T(8,128)(2,1)S(1)}, bf16[128,16032]{0,1:T(8,128)(2,1)}, u32[]{:S(2)}) copy-start(bf16[128,16032]{0,1:T(8,128)(2,1)} %param.11) | copy-start | bytes 12312580
  14.2 16.6 %collective-permute-start = (bf16[16032,128]{1,0:T(8,128)(2,1)}, bf16[16032,128]{1,0:T(8,128)(2,1)S(1)}, u32[]{:S(2)}, u32[]{:S(2)}) collective-permute-start(bf16[16032,128]{1,0:T(8,128)(2,1)} %bitcast.16), channel_id=1, source_target_pairs={{0,8},{8,0},{1,9},{9,1},{2,10},{10,2},{3,11},{11,3},{4,12},{12,4},... | collective-permute-start | bytes 12312584 | tf_op jit(solution)/shard_map/ppermute | solution.py:250
  32.4 19.1 %copy-start.1 = (s32[64]{0:T(128)S(1)}, s32[64]{0:T(128)}, u32[]{:S(2)}) copy-start(s32[64]{0:T(128)} %param.9) | copy-start | bytes 772

commit v12 on v11

--- a/solution.py
+++ b/solution.py
@@ -8,11 +8,11 @@
 from jax.sharding import Mesh
 from jax.sharding import PartitionSpec as P
 
-CHIPS = ("x", "y")
-CP = ("x", "y", "c")
-ALL = ("x", "y", "c", "z")
 SLOTS = 8
-ORDER = [5, 6, 7, 0, 1, 2, 3, 4]
+SIDE = 4
+CHIPS = SIDE * SIDE
+CORES = 2
+DEEP = 8
 BLOCK = 512
 NEG = -1e30
 
@@ -34,10 +34,36 @@
     return jnp.sum(x, axis=axis, keepdims=True)
 
 
-def place():
-    return (lax.axis_index("x") * lax.axis_size("y") + lax.axis_index("y")) * lax.axis_size(
-        "c"
-    ) + lax.axis_index("c")
+def chip_rank(chip):
+    x, y = chip // SIDE, chip % SIDE
+    return (x + SIDE // 2) % SIDE * SIDE + (y + SIDE // 2) % SIDE
+
+
+PLANE = sorted(range(CHIPS), key=chip_rank)
+COLUMN = [(k + DEEP // 2) % DEEP for k in range(DEEP)]
+BOTH = [chip * CORES + core for chip in PLANE for core in (1, 0)]
+EACH = [[chip * CORES + core for chip in PLANE] for core in (0, 1)]
+WHOLE = [place * DEEP + z for place in BOTH for z in COLUMN]
+PAIRS = [(place, place ^ 1) for place in range(CHIPS * CORES)]
+
+
+def core_index():
+    return lax.axis_index("q") & 1
+
+
+def chip_index():
+    return lax.axis_index("q") >> 1
+
+
+def modulo(x, n):
+    return x - n * jnp.floor(x / n)
+
+
+def place_rank(place):
+    chip = jnp.floor(place / CORES)
+    x, y = jnp.floor(chip / SIDE), modulo(chip, SIDE)
+    x, y = modulo(x + SIDE // 2, SIDE), modulo(y + SIDE // 2, SIDE)
+    return (x * SIDE + y) * CORES + (1.0 - modulo(place, CORES))
 
 
 def as_column(row):
@@ -66,7 +92,7 @@
     counts = total(jnp.where(jnp.floor(ends / rows_here) == iota((32, n), 0), 1.0, 0.0), 1)
     most = jnp.max(counts).astype(jnp.int32)
     more_ref[0, 0] = (most > first + SLOTS).astype(jnp.int32)
-    base = (place() * rows_here).astype(jnp.float32)
+    base = (lax.axis_index("q") * rows_here).astype(jnp.float32)
     owned = (ends >= base) & (ends < base + rows_here)
     before = total(jnp.where(ends < base, 1.0, 0.0), 1)
     slot = iota((1, n), 1) - before - first.astype(jnp.float32)
@@ -88,14 +114,14 @@
         squares = squares + total(values * values, 1)
     scale = jnp.sqrt(squares / (parts * width) + 1e-05)
     chips, cores, _, block = out_ref.shape
-    for chip in range(chips):
+    for rank, chip in enumerate(PLANE):
         part, at = divmod(chip * block, width)
-        part = ORDER.index(part)
+        part = COLUMN.index(part)
         values = rows_ref[part, :, at : at + block].astype(jnp.float32)
         gain = gain_ref[:, chip * block : (chip + 1) * block]
         normed = (values * gain / scale).astype(jnp.bfloat16)
         for core in range(cores):
-            out_ref[chip, core] = normed
+            out_ref[rank, core] = normed
 
 
 def rows_in_order(lengths_ref, found_ref, first=0.0):
@@ -107,7 +133,7 @@
     before = total(jnp.where(ends_row < owner * rows, 1.0, 0.0), 1)
     slot = iota((n, 1), 0) - before - first
     inside = (slot >= 0.0) & (slot < SLOTS)
-    at = jnp.where(inside, owner * SLOTS + slot, -1.0)
+    at = jnp.where(inside, place_rank(owner) * SLOTS + slot, -1.0)
     selector = (at == iota((n, places), 1)).astype(jnp.bfloat16)
     return jnp.dot(selector, found_ref[...], preferred_element_type=jnp.float32)
 
@@ -122,8 +148,8 @@
 def head_kernel(lengths_ref, found_ref, more_ref, weight_ref, other_ref, out_ref):
     width = weight_ref.shape[1]
     blocks = out_ref.shape[0]
-    start = lax.axis_index("c") * (weight_ref.shape[0] - blocks * BLOCK)
-    first = lax.axis_index("c") == 0
+    start = core_index() * (weight_ref.shape[0] - blocks * BLOCK)
+    first = core_index() == 0
     rows = rows_in_order(lengths_ref, found_ref).astype(jnp.bfloat16) + more_ref[...]
     low, high = rows[:, :width], rows[:, width:]
     left = jnp.concatenate([jnp.where(first, low, high), jnp.where(first, high, low)], axis=1)
@@ -139,9 +165,11 @@
 def stats_kernel(spare, vocab, logits_ref, targets_ref, out_ref):
     logits = logits_ref[...]
     n, block = logits.shape
-    core = lax.axis_index("c")
-    chip = lax.axis_index("x") * lax.axis_size("y") + lax.axis_index("y")
-    start = (core * spare + chip * block).astype(jnp.float32)
+    core = core_index()
+    chip = chip_index()
+    x, y = chip >> 2, chip & (SIDE - 1)
+    rank = ((x + SIDE // 2) & (SIDE - 1)) * SIDE + ((y + SIDE // 2) & (SIDE - 1))
+    start = (core * spare + rank * block).astype(jnp.float32)
     column = iota((1, block), 1) + start
     half = vocab - spare
     valid = column >= (core * half).astype(jnp.float32)
@@ -173,9 +201,9 @@
     return pltpu.with_memory_space_constraint(x, pltpu.HBM)
 
 
-def exchange(x, axes, groups=None):
+def exchange(x, axis, groups):
     return lax.all_to_all(
-        x, axes, split_axis=0, concat_axis=0, tiled=True, axis_index_groups=groups
+        x, axis, split_axis=0, concat_axis=0, tiled=True, axis_index_groups=groups
     )
 
 
@@ -183,7 +211,7 @@
     return pl.pallas_call(
         pick_kernel,
         out_shape=(
-            shape((lax.axis_size("z"), SLOTS, hidden.shape[1]), hidden.dtype),
+            shape((DEEP, SLOTS, hidden.shape[1]), hidden.dtype),
             pltpu.SMEM((1, 1), jnp.int32),
         ),
         in_specs=[HBM] + [SMEM] * len(first) + [HBM],
@@ -200,9 +228,9 @@
 
 
 def spread(rows, gain, after=()):
-    chips, cores = lax.axis_size(CHIPS), lax.axis_size("c")
+    chips, cores = CHIPS, CORES
     width = gain.shape[1] // chips
-    rows, after = lax.optimization_barrier((exchange(rows, "z", [ORDER]), after))
+    rows, after = lax.optimization_barrier((exchange(rows, "z", [COLUMN]), after))
     normed = pl.pallas_call(
         norm_kernel,
         out_shape=shape((chips, cores, SLOTS, width), jnp.bfloat16),
@@ -212,7 +240,7 @@
         cost_estimate=pl.CostEstimate(flops=10**10, bytes_accessed=1 << 25, transcendentals=0),
         name="norm",
     )(rows, gain)
-    return exchange(normed.reshape(chips * cores * SLOTS, width), CP), after
+    return exchange(normed.reshape(chips * cores * SLOTS, width), "q", [BOTH]), after
 
 
 def local(hidden, lengths, targets, norm_gain, lm_weight):
@@ -220,7 +248,7 @@
     lengths, targets, gain = lengths[None], targets[None], norm_gain[None]
     weight = lm_weight.T
     vocab, depth = weight.shape
-    chips = lax.axis_size(CHIPS)
+    chips = CHIPS
     half = chips * BLOCK
     start = jnp.zeros((1, 1), jnp.int32)
     rows, some = picked(lengths, (), hidden)
@@ -247,7 +275,7 @@
     )
     rows, more, weight = lax.optimization_barrier((rows, more, weight))
     found, weight = spread(rows, gain, weight)
-    other = lax.ppermute(weight, "c", [(0, 1), (1, 0)])
+    other = lax.ppermute(weight, "q", PAIRS)
     own = weight
     parts = pl.pallas_call(
         head_kernel,
@@ -257,16 +285,19 @@
         compiler_params=limit(16),
         name="head",
     )(lengths, found, more, own, other)
-    logits = jnp.sum(exchange(parts.astype(jnp.float16), CHIPS).astype(jnp.float32), axis=0)
-    line = pl.pallas_call(
+    logits = jnp.sum(exchange(parts.astype(jnp.float16), "q", EACH).astype(jnp.float32), axis=0)
+    return pl.pallas_call(
         functools.partial(stats_kernel, vocab - half, vocab),
-        out_shape=shape((lax.axis_size(ALL), 2 * n), jnp.float32),
+        out_shape=shape((len(WHOLE), 2 * n), jnp.float32),
         in_specs=[VMEM, VMEM],
         out_specs=VMEM,
         compiler_params=limit(4),
         name="stats",
     )(logits, targets)
-    lines = exchange(line, ALL)
+
+
+def joined(line):
+    n = line.shape[1] // 2
     out = pl.pallas_call(
         join_kernel,
         out_shape=shape((1, n), jnp.float32),
@@ -274,16 +305,24 @@
         out_specs=VMEM,
         compiler_params=limit(4),
         name="join",
-    )(lines)
+    )(exchange(line, "d", [WHOLE]))
     return out[0]
 
 
 def solution(mesh):
-    split = Mesh(mesh.devices.reshape(4, 4, 2, mesh.shape["tp"]), ALL)
-    return jax.shard_map(
+    devices = mesh.devices.reshape(CHIPS * CORES, DEEP)
+    first = jax.shard_map(
         local,
-        mesh=split,
-        in_specs=(P(CP, "z"), P(), P(), P(), P(CP, "z")),
+        mesh=Mesh(devices, ("q", "z")),
+        in_specs=(P("q", "z"), P(), P(), P(), P("q", "z")),
+        out_specs=P(("q", "z")),
+        check_vma=False,
+    )
+    last = jax.shard_map(
+        joined,
+        mesh=Mesh(devices.reshape(-1), ("d",)),
+        in_specs=P("d"),
         out_specs=P(),
         check_vma=False,
     )
+    return lambda *args: last(first(*args))

time: 75.9 us -> 75.1 us (0.989)
  blocking collectives: 69.5 us -> 68.6 us
    all_to_all x4, blocking collectives: 69.5 us -> 68.6 us  [exchange(): lax.all_to_all(x, axis, split_axis=0, concat_axis=0, tiled=True, axis_ind...]
where the time goes in v12:
time: 75.1 us; the launch traced here: 74.9 us
  blocking collectives  68.6 us (91%)
  Pallas kernels  3.99 us (5%)
  starting transfers between devices  1.74 us (2%)
    all_to_all x4, blocking collectives, exchange(): lax.all_to_all(x, axis, split_axis=0, concat_axis=0, tiled=True, axis_ind...  68.6 us
    ppermute x1, starting transfers between devices, local(): other = lax.ppermute(weight, 'q', PAIRS)  1.74 us
    pallas_call x1, Pallas kernels, local(): pl.pallas_call(head_kernel, out_shape=shape((chips, n, BLOCK), jnp.float3...  1.65 us
  transfers between devices with their start and end apart: 1, of which 0 were waited for; matrix products, arithmetic and copies ran while one was open for 0% of the time, Pallas kernels for 0%

profile of v12, /device:TPU:1, one launch (start us, length us, event | category | flops | bytes accessed | tf_op | source)
XLA Modules:
  0.0 74.9 jit_solution(16837547825575267193)
XLA Ops:
  0.0 0.0 copy-start.2
  0.0 0.0 copy-start.4
  0.0 1.3 %pick.3 = (bf16[8,8,512]{2,1,0:T(8,128)(2,1)S(1)}, s32[1,1]{1,0:T(1,128)S(4)}) custom-call(s32[1,64]{1,0:T(1,128)} %bitcast.24, bf16[512,512]{1,0:T(8,128)(2,1)} %refs_0_.1), custom_call_target="tpu_custom_call" | custom-call | flops 10000000000 | bytes 33554432 | tf_op jit(solution)/shard_map/pick/pallas_call | solution.py:211
  1.3 0.0 copy-done.2
  1.3 0.0 copy-done.4
  1.3 12.9 %all_to_all.45.rows_ref = bf16[8,8,512]{2,1,0:T(8,128)(2,1)S(1)} all-to-all(bf16[8,8,512]{2,1,0:T(8,128)(2,1)S(1)} %get-tuple-element.51), channel_id=1, replica_groups={{4,5,6,7,0,1,2,3},{12,13,14,15,8,9,10,11},{20,21,22,23,16,17,18,19},{28..., dimensions={0} | all-to-all | bytes 131072 | tf_op jit(solution)/shard_map/all_to_all | solution.py:205
  14.2 0.0 copy-start
  14.2 1.7 %collective-permute-start = (bf16[16032,128]{1,0:T(8,128)(2,1)}, bf16[16032,128]{1,0:T(8,128)(2,1)S(1)}, u32[]{:S(2)}, u32[]{:S(2)}) collective-permute-start(bf16[16032,128]{1,0:T(8,128)(2,1)} %bitcast.16), channel_id=1, source_target_pairs={{0,8},{8,0},{16,24},{24,16},{32,40},{40,32},{48,56},{56,48},{64,72... | collective-permute-start | bytes 12312584 | tf_op jit(solution)/shard_map/ppermute | solution.py:278
  16.0 0.1 norm.3
  16.1 11.2 %all_to_all.46 = bf16[32,8,256]{2,1,0:T(8,128)(2,1)S(1)} all-to-all(bf16[32,8,256]{2,1,0:T(8,128)(2,1)S(1)} %bitcast.22), channel_id=1, replica_groups={{168,160,184,176,136,128,152,144,232,224,248,240,200,192,216,208,40,32,..., dimensions={0} | all-to-all | bytes 262144 | tf_op jit(solution)/shard_map/all_to_all | solution.py:205
  27.3 0.0 collective-permute-done.other_ref
  27.3 0.0 copy-done
  27.3 1.7 %head.1 = f32[16,64,512]{2,1,0:T(8,128)S(1)} custom-call(s32[1,64]{1,0:T(1,128)S(1)} %get-tuple-element.97, bf16[256,256]{1,0:T(8,128)(2,1)S(1)} %bitcast.19, bf16[64,256]{1,0:T(8,128)(2,1)S(1)} %get-tuple-element.96, bf16[16032,128]{1,0:T(8,128)(2,1)S(1)} %bitcast.17, bf16[16032,128]{1,0:T(8,128)(2,1)S(1)} %collective-permute-done.other_ref), custom_call_target="tpu_custom_call" | custom-call | tf_op jit(solution)/shard_map/head/pallas_call | solution.py:280
  29.0 0.0 copy-start.1
  29.0 0.3 convert_element_type.6
  29.2 18.9 %all_to_all.47 = f16[16,64,512]{2,1,0:T(8,128)(2,1)S(1)} all-to-all(f16[16,64,512]{2,1,0:T(8,128)(2,1)S(1)} %convert_element_type.6), channel_id=1, replica_groups={{160,176,128,144,224,240,192,208,32,48,0,16,96,112,64,80},{168,184,136,..., dimensions={0} | all-to-all | bytes 2097152 | tf_op jit(solution)/shard_map/all_to_all | solution.py:205
  48.2 0.1 convert_reduce_fusion.logits_ref
  48.3 0.0 copy-done.1
  48.3 0.2 stats.1
  48.5 25.6 %all_to_all.48 = f32[256,1,128]{2,1,0:T(1,128)S(1)} all-to-all(f32[256,1,128]{2,1,0:T(1,128)S(1)} %bitcast.20), channel_id=1, replica_groups={{172,173,174,175,168,169,170,171,164,165,166,167,160,161,162,163,188,18..., dimensions={0} | all-to-all | bytes 262144 | tf_op jit(solution)/shard_map/all_to_all | solution.py:205
  74.2 0.7 join.1
  (2 shorter events, 0.0 us)
Async XLA Ops:
  0.0 1.3 %copy-start.2 = (s32[64]{0:T(128)S(1)}, s32[64]{0:T(128)}, u32[]{:S(2)}) copy-start(s32[64]{0:T(128)} %param.9) | copy-start | bytes 772
  0.0 1.3 %copy-start.4 = (f32[4096]{0:T(1024)S(1)}, f32[4096]{0:T(1024)}, u32[]{:S(2)}) copy-start(f32[4096]{0:T(1024)} %param.11) | copy-start | bytes 49156
  14.2 13.1 %copy-start = (bf16[128,16032]{0,1:T(8,128)(2,1)S(1)}, bf16[128,16032]{0,1:T(8,128)(2,1)}, u32[]{:S(2)}) copy-start(bf16[128,16032]{0,1:T(8,128)(2,1)} %param.12) | copy-start | bytes 12312580
  14.2 13.1 %collective-permute-start = (bf16[16032,128]{1,0:T(8,128)(2,1)}, bf16[16032,128]{1,0:T(8,128)(2,1)S(1)}, u32[]{:S(2)}, u32[]{:S(2)}) collective-permute-start(bf16[16032,128]{1,0:T(8,128)(2,1)} %bitcast.16), channel_id=1, source_target_pairs={{0,8},{8,0},{16,24},{24,16},{32,40},{40,32},{48,56},{56,48},{64,72... | collective-permute-start | bytes 12312584 | tf_op jit(solution)/shard_map/ppermute | solution.py:278
  29.0 19.3 %copy-start.1 = (s32[64]{0:T(128)S(1)}, s32[64]{0:T(128)}, u32[]{:S(2)}) copy-start(s32[64]{0:T(128)} %param.10) | copy-start | bytes 772

commit v13 on v12

--- a/solution.py
+++ b/solution.py
@@ -43,7 +43,7 @@
 COLUMN = [(k + DEEP // 2) % DEEP for k in range(DEEP)]
 BOTH = [chip * CORES + core for chip in PLANE for core in (1, 0)]
 EACH = [[chip * CORES + core for chip in PLANE] for core in (0, 1)]
-WHOLE = [place * DEEP + z for place in BOTH for z in COLUMN]
+HALVES = [[place * DEEP + z for place in group for z in COLUMN] for group in EACH]
 PAIRS = [(place, place ^ 1) for place in range(CHIPS * CORES)]
 
 
@@ -181,7 +181,15 @@
     both = top + jnp.log(total(jnp.exp(logits - top), 1))
     down, across = iota((n, 2 * n), 0), iota((n, 2 * n), 1)
     line = jnp.where(across == down, both, 0.0) + jnp.where(across == down + n, found, 0.0)
-    out_ref[...] = jnp.broadcast_to(total(line, 0), out_ref.shape)
+    out_ref[...] = total(line, 0)
+
+
+def pair_kernel(mine_ref, theirs_ref, out_ref):
+    mine, theirs = mine_ref[...], theirs_ref[...]
+    top = jnp.maximum(mine, theirs)
+    both = top + jnp.log(jnp.exp(mine - top) + jnp.exp(theirs - top))
+    half = iota(mine.shape, 1) < mine.shape[1] // 2
+    out_ref[...] = jnp.broadcast_to(jnp.where(half, both, mine + theirs), out_ref.shape)
 
 
 def join_kernel(found_ref, out_ref):
@@ -286,14 +294,22 @@
         name="head",
     )(lengths, found, more, own, other)
     logits = jnp.sum(exchange(parts.astype(jnp.float16), "q", EACH).astype(jnp.float32), axis=0)
-    return pl.pallas_call(
+    line = pl.pallas_call(
         functools.partial(stats_kernel, vocab - half, vocab),
-        out_shape=shape((len(WHOLE), 2 * n), jnp.float32),
+        out_shape=shape((1, 2 * n), jnp.float32),
         in_specs=[VMEM, VMEM],
         out_specs=VMEM,
         compiler_params=limit(4),
         name="stats",
     )(logits, targets)
+    return pl.pallas_call(
+        pair_kernel,
+        out_shape=shape((len(HALVES[0]), 2 * n), jnp.float32),
+        in_specs=[VMEM, VMEM],
+        out_specs=VMEM,
+        compiler_params=limit(4),
+        name="pair",
+    )(line, lax.ppermute(line, "q", PAIRS))
 
 
 def joined(line):
@@ -305,7 +321,7 @@
         out_specs=VMEM,
         compiler_params=limit(4),
         name="join",
-    )(exchange(line, "d", [WHOLE]))
+    )(exchange(line, "d", HALVES))
     return out[0]
 
 

time: 75.1 us -> 67.4 us (0.90)
  blocking collectives: 68.6 us -> 57.6 us
  starting transfers between devices: 1.74 us -> 4.01 us
  waiting for transfers between devices: 0.01 us -> 0.82 us
    all_to_all x4, blocking collectives: 68.6 us -> 57.6 us  [exchange(): lax.all_to_all(x, axis, split_axis=0, concat_axis=0, tiled=True, axis_ind...]
    ppermute x0 -> x1, starting transfers between devices: none -> 2.27 us  [local(): lax.ppermute(line, 'q', PAIRS)]
    ppermute x0 -> x1, waiting for transfers between devices: none -> 0.82 us  [local(): lax.ppermute(line, 'q', PAIRS)]
  transfers between devices with their start and end apart: 1 -> 2, of which waited for: 0 -> 1; matrix products, arithmetic and copies ran while one was open for 0% -> 0% of each run, Pallas kernels for 0% -> 0%
where the time goes in v13:
time: 67.4 us; the launch traced here: 66.9 us
  blocking collectives  57.6 us (85%)
  starting transfers between devices  4.01 us (6%)
  Pallas kernels  3.98 us (6%)
  waiting for transfers between devices  0.82 us (1%)
    all_to_all x4, blocking collectives, exchange(): lax.all_to_all(x, axis, split_axis=0, concat_axis=0, tiled=True, axis_ind...  57.6 us
    ppermute x1, starting transfers between devices, local(): lax.ppermute(line, 'q', PAIRS)  2.27 us
    ppermute x1, starting transfers between devices, local(): other = lax.ppermute(weight, 'q', PAIRS)  1.74 us
    pallas_call x1, Pallas kernels, local(): pl.pallas_call(head_kernel, out_shape=shape((chips, n, BLOCK), jnp.float3...  1.65 us
  transfers between devices with their start and end apart: 2, of which 1 were waited for; matrix products, arithmetic and copies ran while one was open for 0% of the time, Pallas kernels for 0%

profile of v13, /device:TPU:1, one launch (start us, length us, event | category | flops | bytes accessed | tf_op | source)
XLA Modules:
  0.0 66.9 jit_solution(2892370225467536083)
XLA Ops:
  0.0 0.0 copy-start.2
  0.0 0.0 copy-start.4
  0.0 1.3 %pick.3 = (bf16[8,8,512]{2,1,0:T(8,128)(2,1)S(1)}, s32[1,1]{1,0:T(1,128)S(4)}) custom-call(s32[1,64]{1,0:T(1,128)} %bitcast.24, bf16[512,512]{1,0:T(8,128)(2,1)} %refs_0_.1), custom_call_target="tpu_custom_call" | custom-call | flops 10000000000 | bytes 33554432 | tf_op jit(solution)/shard_map/pick/pallas_call | solution.py:219
  1.3 0.0 copy-done.2
  1.3 0.0 copy-done.4
  1.3 12.9 %all_to_all.45.rows_ref = bf16[8,8,512]{2,1,0:T(8,128)(2,1)S(1)} all-to-all(bf16[8,8,512]{2,1,0:T(8,128)(2,1)S(1)} %get-tuple-element.51), channel_id=1, replica_groups={{4,5,6,7,0,1,2,3},{12,13,14,15,8,9,10,11},{20,21,22,23,16,17,18,19},{28..., dimensions={0} | all-to-all | bytes 131072 | tf_op jit(solution)/shard_map/all_to_all | solution.py:213
  14.2 0.0 copy-start
  14.2 1.7 %collective-permute-start = (bf16[16032,128]{1,0:T(8,128)(2,1)}, bf16[16032,128]{1,0:T(8,128)(2,1)S(1)}, u32[]{:S(2)}, u32[]{:S(2)}) collective-permute-start(bf16[16032,128]{1,0:T(8,128)(2,1)} %bitcast.16), channel_id=1, source_target_pairs={{0,8},{8,0},{16,24},{24,16},{32,40},{40,32},{48,56},{56,48},{64,72... | collective-permute-start | bytes 12312584 | tf_op jit(solution)/shard_map/ppermute | solution.py:286
  16.0 0.1 norm.3
  16.1 11.2 %all_to_all.46 = bf16[32,8,256]{2,1,0:T(8,128)(2,1)S(1)} all-to-all(bf16[32,8,256]{2,1,0:T(8,128)(2,1)S(1)} %bitcast.22), channel_id=1, replica_groups={{168,160,184,176,136,128,152,144,232,224,248,240,200,192,216,208,40,32,..., dimensions={0} | all-to-all | bytes 262144 | tf_op jit(solution)/shard_map/all_to_all | solution.py:213
  27.3 0.0 collective-permute-done.other_ref
  27.3 0.0 copy-done
  27.3 1.7 %head.1 = f32[16,64,512]{2,1,0:T(8,128)S(1)} custom-call(s32[1,64]{1,0:T(1,128)S(1)} %get-tuple-element.99, bf16[256,256]{1,0:T(8,128)(2,1)S(1)} %bitcast.19, bf16[64,256]{1,0:T(8,128)(2,1)S(1)} %get-tuple-element.98, bf16[16032,128]{1,0:T(8,128)(2,1)S(1)} %bitcast.17, bf16[16032,128]{1,0:T(8,128)(2,1)S(1)} %collective-permute-done.other_ref), custom_call_target="tpu_custom_call" | custom-call | tf_op jit(solution)/shard_map/head/pallas_call | solution.py:288
  29.0 0.0 copy-start.1
  29.0 0.3 convert_element_type.6
  29.2 18.9 %all_to_all.47 = f16[16,64,512]{2,1,0:T(8,128)(2,1)S(1)} all-to-all(f16[16,64,512]{2,1,0:T(8,128)(2,1)S(1)} %convert_element_type.6), channel_id=1, replica_groups={{160,176,128,144,224,240,192,208,32,48,0,16,96,112,64,80},{168,184,136,..., dimensions={0} | all-to-all | bytes 2097152 | tf_op jit(solution)/shard_map/all_to_all | solution.py:213
  48.2 0.1 convert_reduce_fusion.logits_ref
  48.3 0.0 copy-done.1
  48.3 0.2 stats.1.mine_ref
  48.5 2.3 %collective-permute-start.1 = (f32[1,128]{1,0:T(1,128)S(1)}, f32[1,128]{1,0:T(1,128)S(1)}, u32[]{:S(2)}, u32[]{:S(2)}) collective-permute-start(f32[1,128]{1,0:T(1,128)S(1)} %stats.1.mine_ref), channel_id=1, source_target_pairs={{0,8},{8,0},{16,24},{24,16},{32,40},{40,32},{48,56},{56,48},{64,72... | collective-permute-start | bytes 1544 | tf_op jit(solution)/shard_map/ppermute | solution.py:312
  50.8 0.8 %collective-permute-done.1.theirs_ref = f32[1,128]{1,0:T(1,128)S(1)} collective-permute-done((f32[1,128]{1,0:T(1,128)S(1)}, f32[1,128]{1,0:T(1,128)S(1)}, u32[]{:S(2)}, u32[]{:S(2)}) %collective-permute-start.1) | collective-permute-done | bytes 544 | tf_op jit(solution)/shard_map/ppermute | solution.py:312
  51.6 14.6 %all_to_all.48 = f32[128,1,128]{2,1,0:T(1,128)S(1)} all-to-all(f32[128,1,128]{2,1,0:T(1,128)S(1)} %bitcast.20), channel_id=1, replica_groups={{164,165,166,167,160,161,162,163,180,181,182,183,176,177,178,179,132,13..., dimensions={0} | all-to-all | bytes 131072 | tf_op jit(solution)/shard_map/all_to_all | solution.py:213
  66.2 0.7 %join.1 = f32[1,64]{1,0:T(1,128)} custom-call(f32[128,128]{1,0:T(8,128)S(1)} %bitcast.21), custom_call_target="tpu_custom_call" | custom-call | tf_op jit(solution)/shard_map/join/pallas_call | solution.py:317
  (3 shorter events, 0.0 us)
Async XLA Ops:
  0.0 1.3 %copy-start.2 = (s32[64]{0:T(128)S(1)}, s32[64]{0:T(128)}, u32[]{:S(2)}) copy-start(s32[64]{0:T(128)} %param.9) | copy-start | bytes 772
  0.0 1.3 %copy-start.4 = (f32[4096]{0:T(1024)S(1)}, f32[4096]{0:T(1024)}, u32[]{:S(2)}) copy-start(f32[4096]{0:T(1024)} %param.11) | copy-start | bytes 49156
  14.2 13.1 %copy-start = (bf16[128,16032]{0,1:T(8,128)(2,1)S(1)}, bf16[128,16032]{0,1:T(8,128)(2,1)}, u32[]{:S(2)}) copy-start(bf16[128,16032]{0,1:T(8,128)(2,1)} %param.12) | copy-start | bytes 12312580
  14.2 13.1 %collective-permute-start = (bf16[16032,128]{1,0:T(8,128)(2,1)}, bf16[16032,128]{1,0:T(8,128)(2,1)S(1)}, u32[]{:S(2)}, u32[]{:S(2)}) collective-permute-start(bf16[16032,128]{1,0:T(8,128)(2,1)} %bitcast.16), channel_id=1, source_target_pairs={{0,8},{8,0},{16,24},{24,16},{32,40},{40,32},{48,56},{56,48},{64,72... | collective-permute-start | bytes 12312584 | tf_op jit(solution)/shard_map/ppermute | solution.py:286
  29.0 19.3 %copy-start.1 = (s32[64]{0:T(128)S(1)}, s32[64]{0:T(128)}, u32[]{:S(2)}) copy-start(s32[64]{0:T(128)} %param.10) | copy-start | bytes 772
  48.5 3.1 %collective-permute-start.1 = (f32[1,128]{1,0:T(1,128)S(1)}, f32[1,128]{1,0:T(1,128)S(1)}, u32[]{:S(2)}, u32[]{:S(2)}) collective-permute-start(f32[1,128]{1,0:T(1,128)S(1)} %stats.1.mine_ref), channel_id=1, source_target_pairs={{0,8},{8,0},{16,24},{24,16},{32,40},{40,32},{48,56},{56,48},{64,72... | collective-permute-start | bytes 1544 | tf_op jit(solution)/shard_map/ppermute | solution.py:312

commit v14 on v13

--- a/solution.py
+++ b/solution.py
@@ -13,6 +13,7 @@
 CHIPS = SIDE * SIDE
 CORES = 2
 DEEP = 8
+FAR_X, FAR_Y, FAR_Z, FAR_CORE = 2, 2, 4, 1
 BLOCK = 512
 NEG = -1e30
 
@@ -36,12 +37,12 @@
 
 def chip_rank(chip):
     x, y = chip // SIDE, chip % SIDE
-    return (x + SIDE // 2) % SIDE * SIDE + (y + SIDE // 2) % SIDE
+    return (x - FAR_X) % SIDE * SIDE + (y - FAR_Y) % SIDE
 
 
 PLANE = sorted(range(CHIPS), key=chip_rank)
-COLUMN = [(k + DEEP // 2) % DEEP for k in range(DEEP)]
-BOTH = [chip * CORES + core for chip in PLANE for core in (1, 0)]
+COLUMN = [(k + FAR_Z) % DEEP for k in range(DEEP)]
+BOTH = [chip * CORES + core for chip in PLANE for core in (FAR_CORE, 1 - FAR_CORE)]
 EACH = [[chip * CORES + core for chip in PLANE] for core in (0, 1)]
 HALVES = [[place * DEEP + z for place in group for z in COLUMN] for group in EACH]
 PAIRS = [(place, place ^ 1) for place in range(CHIPS * CORES)]
@@ -62,8 +63,9 @@
 def place_rank(place):
     chip = jnp.floor(place / CORES)
     x, y = jnp.floor(chip / SIDE), modulo(chip, SIDE)
-    x, y = modulo(x + SIDE // 2, SIDE), modulo(y + SIDE // 2, SIDE)
-    return (x * SIDE + y) * CORES + (1.0 - modulo(place, CORES))
+    x, y = modulo(x - FAR_X, SIDE), modulo(y - FAR_Y, SIDE)
+    core = modulo(place, CORES)
+    return (x * SIDE + y) * CORES + (core if FAR_CORE == 0 else 1.0 - core)
 
 
 def as_column(row):
@@ -79,8 +81,18 @@
     return total(jnp.where(down <= across, as_column(row), 0.0), 0) - 1.0, column
 
 
+def order_of(ends, column, rows, first, places):
+    n = column.shape[0]
+    owner = jnp.floor(column / rows)
+    before = total(jnp.where(ends < owner * rows, 1.0, 0.0), 1)
+    slot = iota((n, 1), 0) - before - first
+    inside = (slot >= 0.0) & (slot < SLOTS)
+    at = jnp.where(inside, place_rank(owner) * SLOTS + slot, -1.0)
+    return (at == iota((n, places), 1)).astype(jnp.bfloat16)
+
+
 def pick_kernel(lengths_ref, *refs):
-    *first_ref, hidden_ref, out_ref, more_ref, lengths, hidden, sems = refs
+    *first_ref, hidden_ref, out_ref, more_ref, order_ref, lengths, hidden, sems = refs
     small = pltpu.make_async_copy(lengths_ref, lengths, sems.at[0])
     large = pltpu.make_async_copy(hidden_ref, hidden, sems.at[1])
     small.start()
@@ -88,7 +100,7 @@
     first = first_ref[0][0, 0] if first_ref else jnp.int32(0)
     small.wait()
     n, rows_here = lengths.shape[1], hidden.shape[0]
-    ends, _ = ends_of(lengths)
+    ends, column = ends_of(lengths)
     counts = total(jnp.where(jnp.floor(ends / rows_here) == iota((32, n), 0), 1.0, 0.0), 1)
     most = jnp.max(counts).astype(jnp.int32)
     more_ref[0, 0] = (most > first + SLOTS).astype(jnp.int32)
@@ -99,6 +111,7 @@
     wanted = owned & (slot == iota((SLOTS, n), 0))
     at = total(jnp.where(wanted, ends - base + 1.0, 0.0), 1) - 1.0
     selector = (at == iota((SLOTS, rows_here), 1)).astype(jnp.bfloat16)
+    order_ref[...] = order_of(ends, column, rows_here, first.astype(jnp.float32), order_ref.shape[1])
     large.wait()
     picked = jnp.dot(selector, hidden[...], preferred_element_type=jnp.float32)
     picked = picked.astype(jnp.bfloat16)
@@ -124,33 +137,19 @@
             out_ref[rank, core] = normed
 
 
-def rows_in_order(lengths_ref, found_ref, first=0.0):
-    n = lengths_ref.shape[1]
-    places = found_ref.shape[0]
-    rows = 512
-    ends_row, ends = ends_of(lengths_ref)
-    owner = jnp.floor(ends / rows)
-    before = total(jnp.where(ends_row < owner * rows, 1.0, 0.0), 1)
-    slot = iota((n, 1), 0) - before - first
-    inside = (slot >= 0.0) & (slot < SLOTS)
-    at = jnp.where(inside, place_rank(owner) * SLOTS + slot, -1.0)
-    selector = (at == iota((n, places), 1)).astype(jnp.bfloat16)
-    return jnp.dot(selector, found_ref[...], preferred_element_type=jnp.float32)
-
-
-def order_kernel(lengths_ref, first_ref, found_ref, more_ref, next_ref, out_ref):
+def order_kernel(order_ref, first_ref, found_ref, more_ref, next_ref, out_ref):
     next_ref[0, 0] = first_ref[0, 0] + SLOTS
-    first = first_ref[0, 0].astype(jnp.float32)
-    rows = rows_in_order(lengths_ref, found_ref, first)
+    rows = jnp.dot(order_ref[...], found_ref[...], preferred_element_type=jnp.float32)
     out_ref[...] = more_ref[...] + rows.astype(jnp.bfloat16)
 
 
-def head_kernel(lengths_ref, found_ref, more_ref, weight_ref, other_ref, out_ref):
+def head_kernel(order_ref, found_ref, more_ref, weight_ref, other_ref, out_ref):
     width = weight_ref.shape[1]
     blocks = out_ref.shape[0]
     start = core_index() * (weight_ref.shape[0] - blocks * BLOCK)
     first = core_index() == 0
-    rows = rows_in_order(lengths_ref, found_ref).astype(jnp.bfloat16) + more_ref[...]
+    rows = jnp.dot(order_ref[...], found_ref[...], preferred_element_type=jnp.float32)
+    rows = rows.astype(jnp.bfloat16) + more_ref[...]
     low, high = rows[:, :width], rows[:, width:]
     left = jnp.concatenate([jnp.where(first, low, high), jnp.where(first, high, low)], axis=1)
     for block in range(blocks):
@@ -168,7 +167,7 @@
     core = core_index()
     chip = chip_index()
     x, y = chip >> 2, chip & (SIDE - 1)
-    rank = ((x + SIDE // 2) & (SIDE - 1)) * SIDE + ((y + SIDE // 2) & (SIDE - 1))
+    rank = ((x - FAR_X) & (SIDE - 1)) * SIDE + ((y - FAR_Y) & (SIDE - 1))
     start = (core * spare + rank * block).astype(jnp.float32)
     column = iota((1, block), 1) + start
     half = vocab - spare
@@ -221,9 +220,10 @@
         out_shape=(
             shape((DEEP, SLOTS, hidden.shape[1]), hidden.dtype),
             pltpu.SMEM((1, 1), jnp.int32),
+            shape((lengths.shape[1], CHIPS * CORES * SLOTS), jnp.bfloat16),
         ),
         in_specs=[HBM] + [SMEM] * len(first) + [HBM],
-        out_specs=(VMEM, SMEM),
+        out_specs=(VMEM, SMEM, VMEM),
         scratch_shapes=[
             pltpu.VMEM(lengths.shape, lengths.dtype),
             pltpu.VMEM(hidden.shape, hidden.dtype),
@@ -259,11 +259,11 @@
     chips = CHIPS
     half = chips * BLOCK
     start = jnp.zeros((1, 1), jnp.int32)
-    rows, some = picked(lengths, (), hidden)
+    rows, some, order = picked(lengths, (), hidden)
 
     def again(state):
         _, first, more = state
-        rows, some = picked(lengths, (first,), hidden)
+        rows, some, order = picked(lengths, (first,), hidden)
         found = spread(rows, gain)[0]
         first, more = pl.pallas_call(
             order_kernel,
@@ -273,7 +273,7 @@
             input_output_aliases={1: 0, 3: 1},
             compiler_params=limit(4),
             name="order",
-        )(lengths, first, found, more)
+        )(order, first, found, more)
         return some[0, 0], first, more
 
     _, _, more = lax.while_loop(
@@ -292,7 +292,7 @@
         out_specs=VMEM,
         compiler_params=limit(16),
         name="head",
-    )(lengths, found, more, own, other)
+    )(order, found, more, own, other)
     logits = jnp.sum(exchange(parts.astype(jnp.float16), "q", EACH).astype(jnp.float32), axis=0)
     line = pl.pallas_call(
         functools.partial(stats_kernel, vocab - half, vocab),

time: 67.4 us -> 67.2 us (level)
  no operation moved by 1% of the time
where the time goes in v14:
time: 67.2 us; the launch traced here: 66.7 us
  blocking collectives  57.6 us (86%)
  starting transfers between devices  4.01 us (6%)
  Pallas kernels  3.8 us (6%)
  waiting for transfers between devices  0.82 us (1%)
    all_to_all x4, blocking collectives, exchange(): lax.all_to_all(x, axis, split_axis=0, concat_axis=0, tiled=True, axis_ind...  57.6 us
    ppermute x1, starting transfers between devices, local(): lax.ppermute(line, 'q', PAIRS)  2.27 us
    ppermute x1, starting transfers between devices, local(): other = lax.ppermute(weight, 'q', PAIRS)  1.74 us
    pallas_call x1, Pallas kernels, local(): pl.pallas_call(head_kernel, out_shape=shape((chips, n, BLOCK), jnp.float3...  1.49 us
  transfers between devices with their start and end apart: 2, of which 1 were waited for; matrix products, arithmetic and copies ran while one was open for 0% of the time, Pallas kernels for 0%

profile of v14, /device:TPU:1, one launch (start us, length us, event | category | flops | bytes accessed | tf_op | source)
XLA Modules:
  0.0 66.7 jit_solution(12879755300593974718)
XLA Ops:
  0.0 0.0 copy-start.2
  0.0 1.3 %pick.3 = (bf16[8,8,512]{2,1,0:T(8,128)(2,1)S(1)}, s32[1,1]{1,0:T(1,128)S(4)}, bf16[64,256]{1,0:T(8,128)(2,1)S(1)}) custom-call(s32[1,64]{1,0:T(1,128)} %bitcast.25, bf16[512,512]{1,0:T(8,128)(2,1)} %refs_0_.1), custom_call_target="tpu_custom_call" | custom-call | flops 10000000000 | bytes 33554432 | tf_op jit(solution)/shard_map/pick/pallas_call | solution.py:218
  1.3 0.0 copy-done.2
  1.3 12.9 %all_to_all.45.rows_ref = bf16[8,8,512]{2,1,0:T(8,128)(2,1)S(1)} all-to-all(bf16[8,8,512]{2,1,0:T(8,128)(2,1)S(1)} %get-tuple-element.54), channel_id=1, replica_groups={{4,5,6,7,0,1,2,3},{12,13,14,15,8,9,10,11},{20,21,22,23,16,17,18,19},{28..., dimensions={0} | all-to-all | bytes 131072 | tf_op jit(solution)/shard_map/all_to_all | solution.py:212
  14.2 0.0 copy-start
  14.2 1.7 %collective-permute-start = (bf16[16032,128]{1,0:T(8,128)(2,1)}, bf16[16032,128]{1,0:T(8,128)(2,1)S(1)}, u32[]{:S(2)}, u32[]{:S(2)}) collective-permute-start(bf16[16032,128]{1,0:T(8,128)(2,1)} %bitcast.16), channel_id=1, source_target_pairs={{0,8},{8,0},{16,24},{24,16},{32,40},{40,32},{48,56},{56,48},{64,72... | collective-permute-start | bytes 12312584 | tf_op jit(solution)/shard_map/ppermute | solution.py:286
  15.9 0.1 norm.3
  16.1 11.2 %all_to_all.46 = bf16[32,8,256]{2,1,0:T(8,128)(2,1)S(1)} all-to-all(bf16[32,8,256]{2,1,0:T(8,128)(2,1)S(1)} %bitcast.22), channel_id=1, replica_groups={{168,160,184,176,136,128,152,144,232,224,248,240,200,192,216,208,40,32,..., dimensions={0} | all-to-all | bytes 262144 | tf_op jit(solution)/shard_map/all_to_all | solution.py:212
  27.3 0.0 collective-permute-done.other_ref
  27.3 0.0 copy-done
  27.3 1.5 %head.1 = f32[16,64,512]{2,1,0:T(8,128)S(1)} custom-call(bf16[64,256]{1,0:T(8,128)(2,1)S(1)} %get-tuple-element.50.order_ref, bf16[256,256]{1,0:T(8,128)(2,1)S(1)} %bitcast.19, bf16[64,256]{1,0:T(8,128)(2,1)S(1)} %get-tuple-element.57.more_ref, bf16[16032,128]{1,0:T(8,128)(2,1)S(1)} %bitcast.17, bf16[16032,128]{1,0:T(8,128)(2,1)S(1)} %collective-permute-done.other_ref), custom_call_target="tpu_custom_call" | custom-call | tf_op jit(solution)/shard_map/head/pallas_call | solution.py:288
  28.8 0.0 copy-start.1
  28.8 0.3 convert_element_type.6
  29.1 18.9 %all_to_all.47 = f16[16,64,512]{2,1,0:T(8,128)(2,1)S(1)} all-to-all(f16[16,64,512]{2,1,0:T(8,128)(2,1)S(1)} %convert_element_type.6), channel_id=1, replica_groups={{160,176,128,144,224,240,192,208,32,48,0,16,96,112,64,80},{168,184,136,..., dimensions={0} | all-to-all | bytes 2097152 | tf_op jit(solution)/shard_map/all_to_all | solution.py:212
  48.0 0.1 convert_reduce_fusion.logits_ref
  48.1 0.0 copy-done.1
  48.1 0.2 stats.1.mine_ref
  48.3 2.3 %collective-permute-start.1 = (f32[1,128]{1,0:T(1,128)S(1)}, f32[1,128]{1,0:T(1,128)S(1)}, u32[]{:S(2)}, u32[]{:S(2)}) collective-permute-start(f32[1,128]{1,0:T(1,128)S(1)} %stats.1.mine_ref), channel_id=1, source_target_pairs={{0,8},{8,0},{16,24},{24,16},{32,40},{40,32},{48,56},{56,48},{64,72... | collective-permute-start | bytes 1544 | tf_op jit(solution)/shard_map/ppermute | solution.py:312
  50.6 0.8 %collective-permute-done.1.theirs_ref = f32[1,128]{1,0:T(1,128)S(1)} collective-permute-done((f32[1,128]{1,0:T(1,128)S(1)}, f32[1,128]{1,0:T(1,128)S(1)}, u32[]{:S(2)}, u32[]{:S(2)}) %collective-permute-start.1) | collective-permute-done | bytes 544 | tf_op jit(solution)/shard_map/ppermute | solution.py:312
  51.4 14.6 %all_to_all.48 = f32[128,1,128]{2,1,0:T(1,128)S(1)} all-to-all(f32[128,1,128]{2,1,0:T(1,128)S(1)} %bitcast.20), channel_id=1, replica_groups={{164,165,166,167,160,161,162,163,180,181,182,183,176,177,178,179,132,13..., dimensions={0} | all-to-all | bytes 131072 | tf_op jit(solution)/shard_map/all_to_all | solution.py:212
  66.0 0.7 %join.1 = f32[1,64]{1,0:T(1,128)} custom-call(f32[128,128]{1,0:T(8,128)S(1)} %bitcast.21), custom_call_target="tpu_custom_call" | custom-call | tf_op jit(solution)/shard_map/join/pallas_call | solution.py:317
  (3 shorter events, 0.0 us)
Async XLA Ops:
  0.0 1.3 %copy-start.2 = (f32[4096]{0:T(1024)S(1)}, f32[4096]{0:T(1024)}, u32[]{:S(2)}) copy-start(f32[4096]{0:T(1024)} %param.11) | copy-start | bytes 49156
  14.2 13.1 %copy-start = (bf16[128,16032]{0,1:T(8,128)(2,1)S(1)}, bf16[128,16032]{0,1:T(8,128)(2,1)}, u32[]{:S(2)}) copy-start(bf16[128,16032]{0,1:T(8,128)(2,1)} %param.12) | copy-start | bytes 12312580
  14.2 13.1 %collective-permute-start = (bf16[16032,128]{1,0:T(8,128)(2,1)}, bf16[16032,128]{1,0:T(8,128)(2,1)S(1)}, u32[]{:S(2)}, u32[]{:S(2)}) collective-permute-start(bf16[16032,128]{1,0:T(8,128)(2,1)} %bitcast.16), channel_id=1, source_target_pairs={{0,8},{8,0},{16,24},{24,16},{32,40},{40,32},{48,56},{56,48},{64,72... | collective-permute-start | bytes 12312584 | tf_op jit(solution)/shard_map/ppermute | solution.py:286
  28.8 19.4 %copy-start.1 = (s32[64]{0:T(128)S(1)}, s32[64]{0:T(128)}, u32[]{:S(2)}) copy-start(s32[64]{0:T(128)} %param.10) | copy-start | bytes 772
  48.3 3.1 %collective-permute-start.1 = (f32[1,128]{1,0:T(1,128)S(1)}, f32[1,128]{1,0:T(1,128)S(1)}, u32[]{:S(2)}, u32[]{:S(2)}) collective-permute-start(f32[1,128]{1,0:T(1,128)S(1)} %stats.1.mine_ref), channel_id=1, source_target_pairs={{0,8},{8,0},{16,24},{24,16},{32,40},{40,32},{48,56},{56,48},{64,72... | collective-permute-start | bytes 1544 | tf_op jit(solution)/shard_map/ppermute | solution.py:312

commit v15 on v14

--- a/solution.py
+++ b/solution.py
@@ -156,9 +156,9 @@
         span = pl.ds(pl.multiple_of(start + block * BLOCK, 16), BLOCK)
         weight = jnp.concatenate([weight_ref[span, :], other_ref[span, :]], axis=1)
         part = lax.dot_general(
-            left, weight, (((1,), (1,)), ((), ())), preferred_element_type=jnp.float32
+            weight, left, (((1,), (1,)), ((), ())), preferred_element_type=jnp.float32
         )
-        out_ref[block] = part.astype(out_ref.dtype)
+        out_ref[block] = part.T.astype(out_ref.dtype)
 
 
 def stats_kernel(spare, vocab, logits_ref, targets_ref, out_ref):

time: 67.2 us -> 67.2 us (level)
  no operation moved by 1% of the time
where the time goes in v15:
time: 67.2 us; the launch traced here: 66.7 us
  blocking collectives  57.6 us (86%)
  starting transfers between devices  4.01 us (6%)
  Pallas kernels  3.8 us (6%)
  waiting for transfers between devices  0.82 us (1%)
    all_to_all x4, blocking collectives, exchange(): lax.all_to_all(x, axis, split_axis=0, concat_axis=0, tiled=True, axis_ind...  57.6 us
    ppermute x1, starting transfers between devices, local(): lax.ppermute(line, 'q', PAIRS)  2.27 us
    ppermute x1, starting transfers between devices, local(): other = lax.ppermute(weight, 'q', PAIRS)  1.74 us
    pallas_call x1, Pallas kernels, local(): pl.pallas_call(head_kernel, out_shape=shape((chips, n, BLOCK), jnp.float3...  1.49 us
  transfers between devices with their start and end apart: 2, of which 1 were waited for; matrix products, arithmetic and copies ran while one was open for 0% of the time, Pallas kernels for 0%

profile of v15, /device:TPU:1, one launch (start us, length us, event | category | flops | bytes accessed | tf_op | source)
XLA Modules:
  0.0 66.7 jit_solution(10554452210537576003)
XLA Ops:
  0.0 0.0 copy-start.2
  0.0 1.3 %pick.3 = (bf16[8,8,512]{2,1,0:T(8,128)(2,1)S(1)}, s32[1,1]{1,0:T(1,128)S(4)}, bf16[64,256]{1,0:T(8,128)(2,1)S(1)}) custom-call(s32[1,64]{1,0:T(1,128)} %bitcast.25, bf16[512,512]{1,0:T(8,128)(2,1)} %refs_0_.1), custom_call_target="tpu_custom_call" | custom-call | flops 10000000000 | bytes 33554432 | tf_op jit(solution)/shard_map/pick/pallas_call | solution.py:218
  1.3 0.0 copy-done.2
  1.3 12.9 %all_to_all.45.rows_ref = bf16[8,8,512]{2,1,0:T(8,128)(2,1)S(1)} all-to-all(bf16[8,8,512]{2,1,0:T(8,128)(2,1)S(1)} %get-tuple-element.54), channel_id=1, replica_groups={{4,5,6,7,0,1,2,3},{12,13,14,15,8,9,10,11},{20,21,22,23,16,17,18,19},{28..., dimensions={0} | all-to-all | bytes 131072 | tf_op jit(solution)/shard_map/all_to_all | solution.py:212
  14.2 0.0 copy-start
  14.2 1.7 %collective-permute-start = (bf16[16032,128]{1,0:T(8,128)(2,1)}, bf16[16032,128]{1,0:T(8,128)(2,1)S(1)}, u32[]{:S(2)}, u32[]{:S(2)}) collective-permute-start(bf16[16032,128]{1,0:T(8,128)(2,1)} %bitcast.16), channel_id=1, source_target_pairs={{0,8},{8,0},{16,24},{24,16},{32,40},{40,32},{48,56},{56,48},{64,72... | collective-permute-start | bytes 12312584 | tf_op jit(solution)/shard_map/ppermute | solution.py:286
  15.9 0.1 norm.3
  16.1 11.2 %all_to_all.46 = bf16[32,8,256]{2,1,0:T(8,128)(2,1)S(1)} all-to-all(bf16[32,8,256]{2,1,0:T(8,128)(2,1)S(1)} %bitcast.22), channel_id=1, replica_groups={{168,160,184,176,136,128,152,144,232,224,248,240,200,192,216,208,40,32,..., dimensions={0} | all-to-all | bytes 262144 | tf_op jit(solution)/shard_map/all_to_all | solution.py:212
  27.3 0.0 collective-permute-done.other_ref
  27.3 0.0 copy-done
  27.3 1.5 %head.1 = f32[16,64,512]{2,1,0:T(8,128)S(1)} custom-call(bf16[64,256]{1,0:T(8,128)(2,1)S(1)} %get-tuple-element.50.order_ref, bf16[256,256]{1,0:T(8,128)(2,1)S(1)} %bitcast.19, bf16[64,256]{1,0:T(8,128)(2,1)S(1)} %get-tuple-element.57.more_ref, bf16[16032,128]{1,0:T(8,128)(2,1)S(1)} %bitcast.17, bf16[16032,128]{1,0:T(8,128)(2,1)S(1)} %collective-permute-done.other_ref), custom_call_target="tpu_custom_call" | custom-call | tf_op jit(solution)/shard_map/head/pallas_call | solution.py:288
  28.8 0.0 copy-start.1
  28.8 0.3 convert_element_type.6
  29.1 18.9 %all_to_all.47 = f16[16,64,512]{2,1,0:T(8,128)(2,1)S(1)} all-to-all(f16[16,64,512]{2,1,0:T(8,128)(2,1)S(1)} %convert_element_type.6), channel_id=1, replica_groups={{160,176,128,144,224,240,192,208,32,48,0,16,96,112,64,80},{168,184,136,..., dimensions={0} | all-to-all | bytes 2097152 | tf_op jit(solution)/shard_map/all_to_all | solution.py:212
  48.0 0.1 convert_reduce_fusion.logits_ref
  48.1 0.0 copy-done.1
  48.1 0.2 stats.1.mine_ref
  48.3 2.3 %collective-permute-start.1 = (f32[1,128]{1,0:T(1,128)S(1)}, f32[1,128]{1,0:T(1,128)S(1)}, u32[]{:S(2)}, u32[]{:S(2)}) collective-permute-start(f32[1,128]{1,0:T(1,128)S(1)} %stats.1.mine_ref), channel_id=1, source_target_pairs={{0,8},{8,0},{16,24},{24,16},{32,40},{40,32},{48,56},{56,48},{64,72... | collective-permute-start | bytes 1544 | tf_op jit(solution)/shard_map/ppermute | solution.py:312
  50.6 0.8 %collective-permute-done.1.theirs_ref = f32[1,128]{1,0:T(1,128)S(1)} collective-permute-done((f32[1,128]{1,0:T(1,128)S(1)}, f32[1,128]{1,0:T(1,128)S(1)}, u32[]{:S(2)}, u32[]{:S(2)}) %collective-permute-start.1) | collective-permute-done | bytes 544 | tf_op jit(solution)/shard_map/ppermute | solution.py:312
  51.4 14.6 %all_to_all.48 = f32[128,1,128]{2,1,0:T(1,128)S(1)} all-to-all(f32[128,1,128]{2,1,0:T(1,128)S(1)} %bitcast.20), channel_id=1, replica_groups={{164,165,166,167,160,161,162,163,180,181,182,183,176,177,178,179,132,13..., dimensions={0} | all-to-all | bytes 131072 | tf_op jit(solution)/shard_map/all_to_all | solution.py:212
  66.0 0.7 %join.1 = f32[1,64]{1,0:T(1,128)} custom-call(f32[128,128]{1,0:T(8,128)S(1)} %bitcast.21), custom_call_target="tpu_custom_call" | custom-call | tf_op jit(solution)/shard_map/join/pallas_call | solution.py:317
  (3 shorter events, 0.0 us)
Async XLA Ops:
  0.0 1.3 %copy-start.2 = (f32[4096]{0:T(1024)S(1)}, f32[4096]{0:T(1024)}, u32[]{:S(2)}) copy-start(f32[4096]{0:T(1024)} %param.11) | copy-start | bytes 49156
  14.2 13.1 %copy-start = (bf16[128,16032]{0,1:T(8,128)(2,1)S(1)}, bf16[128,16032]{0,1:T(8,128)(2,1)}, u32[]{:S(2)}) copy-start(bf16[128,16032]{0,1:T(8,128)(2,1)} %param.12) | copy-start | bytes 12312580
  14.2 13.1 %collective-permute-start = (bf16[16032,128]{1,0:T(8,128)(2,1)}, bf16[16032,128]{1,0:T(8,128)(2,1)S(1)}, u32[]{:S(2)}, u32[]{:S(2)}) collective-permute-start(bf16[16032,128]{1,0:T(8,128)(2,1)} %bitcast.16), channel_id=1, source_target_pairs={{0,8},{8,0},{16,24},{24,16},{32,40},{40,32},{48,56},{56,48},{64,72... | collective-permute-start | bytes 12312584 | tf_op jit(solution)/shard_map/ppermute | solution.py:286
  28.8 19.3 %copy-start.1 = (s32[64]{0:T(128)S(1)}, s32[64]{0:T(128)}, u32[]{:S(2)}) copy-start(s32[64]{0:T(128)} %param.10) | copy-start | bytes 772
  48.3 3.1 %collective-permute-start.1 = (f32[1,128]{1,0:T(1,128)S(1)}, f32[1,128]{1,0:T(1,128)S(1)}, u32[]{:S(2)}, u32[]{:S(2)}) collective-permute-start(f32[1,128]{1,0:T(1,128)S(1)} %stats.1.mine_ref), channel_id=1, source_target_pairs={{0,8},{8,0},{16,24},{24,16},{32,40},{40,32},{48,56},{56,48},{64,72... | collective-permute-start | bytes 1544 | tf_op jit(solution)/shard_map/ppermute | solution.py:312

commit v16 on v15

--- a/solution.py
+++ b/solution.py
@@ -41,10 +41,11 @@
 
 
 PLANE = sorted(range(CHIPS), key=chip_rank)
-COLUMN = [(k + FAR_Z) % DEEP for k in range(DEEP)]
+COLUMN = [(k + FAR_Z + 1) % DEEP for k in range(DEEP)]
 BOTH = [chip * CORES + core for chip in PLANE for core in (FAR_CORE, 1 - FAR_CORE)]
 EACH = [[chip * CORES + core for chip in PLANE] for core in (0, 1)]
-HALVES = [[place * DEEP + z for place in group for z in COLUMN] for group in EACH]
+LAST = [(k + FAR_Z) % DEEP for k in range(DEEP)]
+HALVES = [[place * DEEP + z for place in group for z in LAST] for group in EACH]
 PAIRS = [(place, place ^ 1) for place in range(CHIPS * CORES)]
 
 

time: 67.2 us -> 67.2 us (level)
  no operation moved by 1% of the time
where the time goes in v16:
time: 67.2 us; the launch traced here: 66.7 us
  blocking collectives  57.7 us (86%)
  starting transfers between devices  3.89 us (6%)
  Pallas kernels  3.8 us (6%)
  waiting for transfers between devices  0.82 us (1%)
    all_to_all x4, blocking collectives, exchange(): lax.all_to_all(x, axis, split_axis=0, concat_axis=0, tiled=True, axis_ind...  57.7 us
    ppermute x1, starting transfers between devices, local(): lax.ppermute(line, 'q', PAIRS)  2.26 us
    ppermute x1, starting transfers between devices, local(): other = lax.ppermute(weight, 'q', PAIRS)  1.62 us
    pallas_call x1, Pallas kernels, local(): pl.pallas_call(head_kernel, out_shape=shape((chips, n, BLOCK), jnp.float3...  1.48 us
  transfers between devices with their start and end apart: 2, of which 1 were waited for; matrix products, arithmetic and copies ran while one was open for 0% of the time, Pallas kernels for 0%

profile of v16, /device:TPU:1, one launch (start us, length us, event | category | flops | bytes accessed | tf_op | source)
XLA Modules:
  0.0 66.7 jit_solution(10175323019315692107)
XLA Ops:
  0.0 0.0 copy-start.2
  0.0 1.3 %pick.3 = (bf16[8,8,512]{2,1,0:T(8,128)(2,1)S(1)}, s32[1,1]{1,0:T(1,128)S(4)}, bf16[64,256]{1,0:T(8,128)(2,1)S(1)}) custom-call(s32[1,64]{1,0:T(1,128)} %bitcast.25, bf16[512,512]{1,0:T(8,128)(2,1)} %refs_0_.1), custom_call_target="tpu_custom_call" | custom-call | flops 10000000000 | bytes 33554432 | tf_op jit(solution)/shard_map/pick/pallas_call | solution.py:219
  1.3 0.0 copy-done.2
  1.3 12.8 %all_to_all.45.rows_ref = bf16[8,8,512]{2,1,0:T(8,128)(2,1)S(1)} all-to-all(bf16[8,8,512]{2,1,0:T(8,128)(2,1)S(1)} %get-tuple-element.54), channel_id=1, replica_groups={{5,6,7,0,1,2,3,4},{13,14,15,8,9,10,11,12},{21,22,23,16,17,18,19,20},{29..., dimensions={0} | all-to-all | bytes 131072 | tf_op jit(solution)/shard_map/all_to_all | solution.py:213
  14.1 0.0 copy-start
  14.1 1.6 %collective-permute-start = (bf16[16032,128]{1,0:T(8,128)(2,1)}, bf16[16032,128]{1,0:T(8,128)(2,1)S(1)}, u32[]{:S(2)}, u32[]{:S(2)}) collective-permute-start(bf16[16032,128]{1,0:T(8,128)(2,1)} %bitcast.16), channel_id=1, source_target_pairs={{0,8},{8,0},{16,24},{24,16},{32,40},{40,32},{48,56},{56,48},{64,72... | collective-permute-start | bytes 12312584 | tf_op jit(solution)/shard_map/ppermute | solution.py:287
  15.8 0.1 norm.3
  15.9 11.2 %all_to_all.46 = bf16[32,8,256]{2,1,0:T(8,128)(2,1)S(1)} all-to-all(bf16[32,8,256]{2,1,0:T(8,128)(2,1)S(1)} %bitcast.22), channel_id=1, replica_groups={{168,160,184,176,136,128,152,144,232,224,248,240,200,192,216,208,40,32,..., dimensions={0} | all-to-all | bytes 262144 | tf_op jit(solution)/shard_map/all_to_all | solution.py:213
  27.1 0.0 collective-permute-done.other_ref
  27.1 0.0 copy-done
  27.1 1.5 %head.1 = f32[16,64,512]{2,1,0:T(8,128)S(1)} custom-call(bf16[64,256]{1,0:T(8,128)(2,1)S(1)} %get-tuple-element.50.order_ref, bf16[256,256]{1,0:T(8,128)(2,1)S(1)} %bitcast.19, bf16[64,256]{1,0:T(8,128)(2,1)S(1)} %get-tuple-element.57.more_ref, bf16[16032,128]{1,0:T(8,128)(2,1)S(1)} %bitcast.17, bf16[16032,128]{1,0:T(8,128)(2,1)S(1)} %collective-permute-done.other_ref), custom_call_target="tpu_custom_call" | custom-call | tf_op jit(solution)/shard_map/head/pallas_call | solution.py:289
  28.6 0.0 copy-start.1
  28.6 0.3 convert_element_type.6
  28.9 18.9 %all_to_all.47 = f16[16,64,512]{2,1,0:T(8,128)(2,1)S(1)} all-to-all(f16[16,64,512]{2,1,0:T(8,128)(2,1)S(1)} %convert_element_type.6), channel_id=1, replica_groups={{160,176,128,144,224,240,192,208,32,48,0,16,96,112,64,80},{168,184,136,..., dimensions={0} | all-to-all | bytes 2097152 | tf_op jit(solution)/shard_map/all_to_all | solution.py:213
  47.8 0.1 convert_reduce_fusion.logits_ref
  48.0 0.0 copy-done.1
  48.0 0.2 stats.1.mine_ref
  48.2 2.3 %collective-permute-start.1 = (f32[1,128]{1,0:T(1,128)S(1)}, f32[1,128]{1,0:T(1,128)S(1)}, u32[]{:S(2)}, u32[]{:S(2)}) collective-permute-start(f32[1,128]{1,0:T(1,128)S(1)} %stats.1.mine_ref), channel_id=1, source_target_pairs={{0,8},{8,0},{16,24},{24,16},{32,40},{40,32},{48,56},{56,48},{64,72... | collective-permute-start | bytes 1544 | tf_op jit(solution)/shard_map/ppermute | solution.py:313
  50.4 0.8 %collective-permute-done.1.theirs_ref = f32[1,128]{1,0:T(1,128)S(1)} collective-permute-done((f32[1,128]{1,0:T(1,128)S(1)}, f32[1,128]{1,0:T(1,128)S(1)}, u32[]{:S(2)}, u32[]{:S(2)}) %collective-permute-start.1) | collective-permute-done | bytes 544 | tf_op jit(solution)/shard_map/ppermute | solution.py:313
  51.3 14.7 %all_to_all.48 = f32[128,1,128]{2,1,0:T(1,128)S(1)} all-to-all(f32[128,1,128]{2,1,0:T(1,128)S(1)} %bitcast.20), channel_id=1, replica_groups={{164,165,166,167,160,161,162,163,180,181,182,183,176,177,178,179,132,13..., dimensions={0} | all-to-all | bytes 131072 | tf_op jit(solution)/shard_map/all_to_all | solution.py:213
  66.0 0.7 %join.1 = f32[1,64]{1,0:T(1,128)} custom-call(f32[128,128]{1,0:T(8,128)S(1)} %bitcast.21), custom_call_target="tpu_custom_call" | custom-call | tf_op jit(solution)/shard_map/join/pallas_call | solution.py:318
  (3 shorter events, 0.0 us)
Async XLA Ops:
  0.0 1.3 %copy-start.2 = (f32[4096]{0:T(1024)S(1)}, f32[4096]{0:T(1024)}, u32[]{:S(2)}) copy-start(f32[4096]{0:T(1024)} %param.11) | copy-start | bytes 49156
  14.1 13.0 %copy-start = (bf16[128,16032]{0,1:T(8,128)(2,1)S(1)}, bf16[128,16032]{0,1:T(8,128)(2,1)}, u32[]{:S(2)}) copy-start(bf16[128,16032]{0,1:T(8,128)(2,1)} %param.12) | copy-start | bytes 12312580
  14.1 13.0 %collective-permute-start = (bf16[16032,128]{1,0:T(8,128)(2,1)}, bf16[16032,128]{1,0:T(8,128)(2,1)S(1)}, u32[]{:S(2)}, u32[]{:S(2)}) collective-permute-start(bf16[16032,128]{1,0:T(8,128)(2,1)} %bitcast.16), channel_id=1, source_target_pairs={{0,8},{8,0},{16,24},{24,16},{32,40},{40,32},{48,56},{56,48},{64,72... | collective-permute-start | bytes 12312584 | tf_op jit(solution)/shard_map/ppermute | solution.py:287
  28.6 19.4 %copy-start.1 = (s32[64]{0:T(128)S(1)}, s32[64]{0:T(128)}, u32[]{:S(2)}) copy-start(s32[64]{0:T(128)} %param.10) | copy-start | bytes 772
  48.2 3.1 %collective-permute-start.1 = (f32[1,128]{1,0:T(1,128)S(1)}, f32[1,128]{1,0:T(1,128)S(1)}, u32[]{:S(2)}, u32[]{:S(2)}) collective-permute-start(f32[1,128]{1,0:T(1,128)S(1)} %stats.1.mine_ref), channel_id=1, source_target_pairs={{0,8},{8,0},{16,24},{24,16},{32,40},{40,32},{48,56},{56,48},{64,72... | collective-permute-start | bytes 1544 | tf_op jit(solution)/shard_map/ppermute | solution.py:313
